TPU v7x, 32 devices: a whole 2x2x4 slice. The times are simulated.
32 devices in a mesh: cfg: 4 (over z), tm: 8 (over y, x, core).
Axes of the slice: x: 2, y: 2, z: 4, core: 2. Of those that a mesh axis runs over, the one named last changes fastest.
Arguments:
- linv: bfloat16 [16384, 1024], P(('cfg', 'tm')), parts along dimension 0, as said below
- sub: bfloat16 [16384, 1024], P(('cfg', 'tm')), parts along dimension 0, may hold values from -0.046875 to 0.046875
- owner: int32 [16], P('cfg'), parts along dimension 0, may hold values from 0 to 7, as said below
Outputs:
- diag_cov: bfloat16 [16384, 1024], P(('cfg', 'tm')), parts along dimension 0
- off_cov: bfloat16 [16384, 1024], P(('cfg', 'tm')), parts along dimension 0
- owned_var: float32 [64, 1024], P(('cfg', 'tm')), parts along dimension 0
There are 4 independent parts, one for each index of `cfg`. A program takes and returns all parts, laid end to end along the dimension named above; each array names one. Nothing has to cross between parts.
Inputs may be any that keep to these rules, and one draw needn't show every extreme that they name: Each block of 1024 rows of linv is lower triangular with a positive diagonal. Exactly two time blocks, adjacent in time, share an owner; all other time blocks have distinct owners, so no owner receives more than 2 blocks and one receives exactly 2.
All inputs are finite; a program needn't handle non-finite values.
Results may differ from a plain program's by a relative error of at most 0.0075.
Values may be sent and summed in bfloat16 or wider, within the bound.
No kernel may reach another device: no remote copies, remote signals or barrier semaphores. Data moves between devices by JAX's collectives and lax.ppermute only.
A program may use at most 64 MiB of HBM per device.

v0:
```python
import jax
import jax.numpy as jnp
from jax import lax
from jax.sharding import PartitionSpec as P

TB = 4
SLOTS = 2


CONTRACT_FIRST = (((0,), (0,)), ((), ()))


def partner_2(block, axis, stride):
    count = lax.axis_size(axis)
    route = []
    for low in range(count):
        high = low | 1 << stride
        if high != low and high < count:
            route += [(low, high), (high, low)]
    return lax.ppermute(block, axis, route)


def from_behind(array, axis, by):
    count = lax.axis_size(axis)
    pairs = [(i, i + by) for i in range(count) if 0 <= i + by < count]
    return lax.ppermute(array, axis, pairs)


def assemble(own_piece, swapper, bit_count, dev_index):
    bit_order = list(range(bit_count))
    gathered = own_piece
    for bit_index in bit_order:
        partner = swapper(gathered, bit_index)
        upper_half = dev_index >> bit_index & 1 == 1
        lower_part = jnp.where(upper_half, partner, gathered)
        upper_part = jnp.where(upper_half, gathered, partner)
        gathered = jnp.concatenate([lower_part, upper_part], 0)
    return gathered


def shards(linv, sub, owner):
    group_size = lax.axis_size("tm") // TB
    row_count = linv.shape[0]
    col_count = linv.shape[1]
    bit_count = group_size.bit_length() - 1
    dev_index = lax.axis_index("tm")
    member = dev_index % group_size
    my_block = dev_index // group_size
    row_start = member * row_count
    row_iota = lax.broadcasted_iota(jnp.int32, (row_count, col_count), 0)
    col_iota = lax.broadcasted_iota(jnp.int32, (row_count, col_count), 1)
    on_diagonal = row_iota + row_start == col_iota
    ident_rows = on_diagonal.astype(jnp.bfloat16)

    def swap_pairs(values, bit_index):
        return partner_2(values, "tm", bit_index)

    def swap_offdiag(values, bit_index):
        return partner_2(values, "tm", bit_index)

    joined = jnp.concatenate([linv, sub], 1)
    both_full = assemble(joined, swap_pairs, bit_count, dev_index)
    linv_full = both_full[:, :col_count]
    sub_full = both_full[:, col_count:]
    coupling_full = jnp.dot(sub_full, linv_full, preferred_element_type=jnp.float32).astype(
        jnp.bfloat16
    )
    factor_cols = lax.dynamic_slice_in_dim(linv_full, row_start, row_count, 1)
    gram_rows = lax.dot_general(
        factor_cols, linv_full, CONTRACT_FIRST, preferred_element_type=jnp.float32
    )
    coupling_cols = lax.dynamic_slice_in_dim(coupling_full, row_start, row_count, 1)
    at_end = my_block == TB - 1
    carried = ident_rows
    cov_rows = ident_rows
    off_rows = ident_rows
    for turn_index in range(TB):
        if turn_index > 0:
            arrived = from_behind(cov_rows, "tm", -group_size)
            carried = jnp.where(at_end, ident_rows, arrived)
        off_rows = (-jnp.dot(carried, coupling_full, preferred_element_type=jnp.float32)).astype(
            jnp.bfloat16
        )
        off_full = assemble(off_rows, swap_offdiag, bit_count, dev_index)
        cov_rows = (
            gram_rows
            - lax.dot_general(
                coupling_cols, off_full, CONTRACT_FIRST, preferred_element_type=jnp.float32
            )
        ).astype(jnp.bfloat16)
    var_rows = jnp.sum(jnp.where(on_diagonal, cov_rows.astype(jnp.float32), 0.0), axis=1)
    all_var = lax.all_gather(var_rows[None, :], "tm", axis=0, tiled=True).reshape(TB, col_count)
    positions = lax.broadcasted_iota(jnp.int32, (TB, TB), 1)
    current = lax.broadcasted_iota(jnp.int32, (TB, TB), 0)
    same_owner = owner[:, None] == owner[None, :]
    slot_rank = jnp.sum(jnp.where(same_owner & (positions < current), 1, 0), axis=1)
    slot_iota = lax.broadcasted_iota(jnp.int32, (SLOTS, TB), 0)
    selector = ((owner[None, :] == dev_index) & (slot_rank[None, :] == slot_iota)).astype(
        jnp.float32
    )
    owned_var = jnp.dot(selector, all_var, precision=lax.Precision.HIGHEST)
    return (cov_rows, off_rows, owned_var)


def solution(mesh):
    return jax.shard_map(
        shards,
        mesh=mesh,
        in_specs=(P(("cfg", "tm"), None), P(("cfg", "tm"), None), P("cfg")),
        out_specs=(P(("cfg", "tm"), None), P(("cfg", "tm"), None), P(("cfg", "tm"), None)),
        check_vma=False,
    )
```

profile of v0, /device:TPU:0, one launch (start us, length us, event | category | flops | bytes accessed | tf_op | source)
XLA Modules:
  0.0 134.2 jit_solution(11692226478106050238)
XLA Ops:
  0.6 0.0 copy-start.5
  0.6 1.4 %constant_dynamic-update-slice_fusion.1 = bf16[512,2048]{1,0:T(8,128)(2,1)S(1)} fusion(bf16[512,1024]{1,0:T(8,128)(2,1)} %param.3), kind=kLoop, calls=%fused_computation.62 | loop fusion | bytes 2097152
  2.0 0.1 copy-done.5
  2.2 0.1 constant_dynamic-update-slice_fusion
  2.3 0.6 collective-permute-start
  2.8 3.9 %collective-permute-done = bf16[512,2048]{1,0:T(8,128)(2,1)} collective-permute-done((bf16[512,2048]{1,0:T(8,128)(2,1)S(1)}, bf16[512,2048]{1,0:T(8,128)(2,1)}, u32[]{:S(2)}, u32[]{:S(2)}) %collective-permute-start) | collective-permute-done | bytes 2097184 | tf_op jit(solution)/shard_map/ppermute | solution.py:20
  6.7 1.9 %broadcast_select_fusion = (bf16[512,2048]{1,0:T(8,128)(2,1)S(1)}, bf16[512,2048]{1,0:T(8,128)(2,1)S(1)}) fusion(bf16[512,2048]{1,0:T(8,128)(2,1)S(1)} %constant_dynamic-update-slice_fusion, bf16[512,2048]{1,0:T(8,128)(2,1)} %collective-permute-done, pred[]{:T(512)S(6)} %eq.43), kind=kLoop, calls=%fused_computation.34 | loop fusion | flops 2097152 | bytes 8388609 | tf_op jit(solution)/shard_map/jit(_where)/select_n | solution.py:36
  8.6 0.2 fusion
  8.8 0.0 copy-start
  8.8 2.3 %fusion.21 = bf16[1024,1024]{1,0:T(8,128)(2,1)S(1)} fusion(bf16[1024,1024]{1,0:T(8,128)(2,1)S(1)} %fusion, bf16[512,2048]{1,0:T(8,128)(2,1)S(1)} %get-tuple-element.3, bf16[512,2048]{1,0:T(8,128)(2,1)S(1)} %get-tuple-element.4), kind=kOutput, calls=%fused_computation.36 | convolution fusion | flops 2152726528 | bytes 8388608 | tf_op jit(solution)/shard_map/dot_general | solution.py:65
  11.2 0.0 copy-done
  11.2 0.0 copy-start.1
  11.2 1.3 negate_convert_fusion.3
  12.5 0.0 copy-done.1
  12.5 0.4 collective-permute-start.1
  12.9 3.2 %fusion.40 = f32[512,1024]{1,0:T(8,128)S(1)} fusion(bf16[1024,1024]{1,0:T(8,128)(2,1)} %copy-done, s32[]{:T(128)S(6)} %select_n.89), kind=kOutput, calls=%fused_computation.44 | convolution fusion | flops 1073741824 | bytes 5242884 | tf_op jit(solution)/shard_map/dot_general | solution.py:69
  16.1 0.0 copy-start.2
  16.1 0.0 collective-permute-done.1
  16.1 1.5 %broadcast_select_fusion.9 = (bf16[512,1024]{1,0:T(8,128)(2,1)S(1)}, bf16[512,1024]{1,0:T(8,128)(2,1)S(1)}) fusion(bf16[512,1024]{1,0:T(8,128)(2,1)} %collective-permute-done.1, bf16[512,1024]{1,0:T(8,128)(2,1)S(1)} %negate_convert_fusion.3, pred[]{:T(512)S(6)} %eq.43), kind=kLoop, calls=%fused_computation.56 | loop fusion | flops 1048576 | bytes 4194305 | tf_op jit(solution)/shard_map/jit(_where)/select_n | solution.py:35
  17.7 0.4 copy-done.2
  18.0 1.3 subtract_convert_fusion.3
  19.3 1.3 collective-permute-start.2
  20.6 27.0 %collective-permute-done.2 = bf16[512,1024]{1,0:T(8,128)(2,1)} collective-permute-done((bf16[512,1024]{1,0:T(8,128)(2,1)S(1)}, bf16[512,1024]{1,0:T(8,128)(2,1)}, u32[]{:S(2)}, u32[]{:S(2)}) %collective-permute-start.2) | collective-permute-done | bytes 1048608 | tf_op jit(solution)/shard_map/ppermute | solution.py:26
  47.6 3.2 %negate_convert_fusion.2 = bf16[512,1024]{1,0:T(8,128)(2,1)S(1)} fusion(bf16[1024,1024]{1,0:T(8,128)(2,1)} %copy-done.1, bf16[512,1024]{1,0:T(8,128)(2,1)} %collective-permute-done.2, s32[512]{0:T(512)S(1)} %iota_add_fusion, pred[]{:T(512)S(6)} %eq.44), kind=kOutput, calls=%fused_computation.28 | convolution fusion | flops 1076363264 | bytes 4196353 | tf_op jit(solution)/shard_map/dot_general | solution.py:81
  50.9 0.0 copy-start.3
  50.9 0.1 collective-permute-start.3
  51.0 2.6 %collective-permute-done.3 = bf16[512,1024]{1,0:T(8,128)(2,1)S(1)} collective-permute-done((bf16[512,1024]{1,0:T(8,128)(2,1)S(1)}, bf16[512,1024]{1,0:T(8,128)(2,1)S(1)}, u32[]{:S(2)}, u32[]{:S(2)}) %collective-permute-start.3) | collective-permute-done | bytes 1048608 | tf_op jit(solution)/shard_map/ppermute | solution.py:20
  53.6 0.3 broadcast_select_fusion.7
  53.9 0.0 copy-done.3
  53.9 1.3 subtract_convert_fusion.2
  55.2 1.3 collective-permute-start.4
  56.5 26.7 %collective-permute-done.4 = bf16[512,1024]{1,0:T(8,128)(2,1)S(1)} collective-permute-done((bf16[512,1024]{1,0:T(8,128)(2,1)S(1)}, bf16[512,1024]{1,0:T(8,128)(2,1)S(1)}, u32[]{:S(2)}, u32[]{:S(2)}) %collective-permute-start.4) | collective-permute-done | bytes 1048608 | tf_op jit(solution)/shard_map/ppermute | solution.py:26
  83.2 1.3 negate_convert_fusion.1
  84.5 0.1 collective-permute-start.5
  84.6 2.6 %collective-permute-done.5 = bf16[512,1024]{1,0:T(8,128)(2,1)S(1)} collective-permute-done((bf16[512,1024]{1,0:T(8,128)(2,1)S(1)}, bf16[512,1024]{1,0:T(8,128)(2,1)S(1)}, u32[]{:S(2)}, u32[]{:S(2)}) %collective-permute-start.5) | collective-permute-done | bytes 1048608 | tf_op jit(solution)/shard_map/ppermute | solution.py:20
  87.2 0.3 broadcast_select_fusion.5
  87.5 1.3 subtract_convert_fusion.1
  88.8 0.0 copy-start.6
  88.8 1.5 %collective-permute-start.6 = (bf16[512,1024]{1,0:T(8,128)(2,1)S(1)}, bf16[512,1024]{1,0:T(8,128)(2,1)S(1)}, u32[]{:S(2)}, u32[]{:S(2)}) collective-permute-start(bf16[512,1024]{1,0:T(8,128)(2,1)S(1)} %subtract_convert_fusion.1), channel_id=1, source_target_pairs={{2,0},{3,1},{4,2},{5,3},{6,4},{7,5},{10,8},{11,9},{12,10},{13,11},... | collective-permute-start | bytes 3145736 | tf_op jit(solution)/shard_map/ppermute | solution.py:26
  90.3 26.5 %collective-permute-done.6 = bf16[512,1024]{1,0:T(8,128)(2,1)S(1)} collective-permute-done((bf16[512,1024]{1,0:T(8,128)(2,1)S(1)}, bf16[512,1024]{1,0:T(8,128)(2,1)S(1)}, u32[]{:S(2)}, u32[]{:S(2)}) %collective-permute-start.6) | collective-permute-done | bytes 1048608 | tf_op jit(solution)/shard_map/ppermute | solution.py:26
  116.8 1.3 negate_convert_fusion
  118.1 0.0 copy-start.4
  118.2 0.1 collective-permute-start.7
  118.2 0.0 copy-done.6
  118.2 0.2 select_reduce_fusion.1
  118.4 2.4 %collective-permute-done.7 = bf16[512,1024]{1,0:T(8,128)(2,1)S(1)} collective-permute-done((bf16[512,1024]{1,0:T(8,128)(2,1)S(1)}, bf16[512,1024]{1,0:T(8,128)(2,1)S(1)}, u32[]{:S(2)}, u32[]{:S(2)}) %collective-permute-start.7) | collective-permute-done | bytes 1048608 | tf_op jit(solution)/shard_map/ppermute | solution.py:20
  120.9 0.1 broadcast_select_fusion.3
  121.0 0.0 copy-done.4
  121.0 2.3 %select_reduce_fusion = (f32[512]{0:T(512)S(1)}, bf16[512,1024]{1,0:T(8,128)(2,1)}) fusion(s32[512]{0:T(512)S(1)} %iota_add_fusion, f32[512,1024]{1,0:T(8,128)S(1)} %fusion.40, bf16[512,1024]{1,0:T(8,128)(2,1)S(1)} %get-tuple-element.6, bf16[512,1024]{1,0:T(8,128)(2,1)S(1)} %get-tuple-element.5, bf16[1024,1024]{1,0:T(8,128)(2,1)S(1)} %copy-done.3, ...), kind=kOutput, calls=%fused_computation.22 | convolution fusion | flops 1081081344 | bytes 6295556 | tf_op jit(solution)/shard_map/dot_general | solution.py:87
  123.4 10.0 %all-gather.1 = f32[8,1,512]{2,1,0:T(1,128)S(1)} all-gather(f32[1,1,512]{2,1,0:T(1,128)S(1)} %bitcast.8), channel_id=2, replica_groups=mesh['cfg'=4,'tm'=8] {'tm'}, dimensions={0}, use_global_device_ids=true | all-gather | bytes 18432 | tf_op jit(solution)/shard_map/all_gather | solution.py:92
  133.5 0.7 fusion.50
  (4 shorter events, 0.1 us)
Async XLA Ops:
  0.6 1.5 %copy-start.5 = (bf16[512,1024]{1,0:T(8,128)(2,1)S(1)}, bf16[512,1024]{1,0:T(8,128)(2,1)}, u32[]{:S(2)}) copy-start(bf16[512,1024]{1,0:T(8,128)(2,1)} %param.4) | copy-start | bytes 3145732
  2.3 4.5 %collective-permute-start = (bf16[512,2048]{1,0:T(8,128)(2,1)S(1)}, bf16[512,2048]{1,0:T(8,128)(2,1)}, u32[]{:S(2)}, u32[]{:S(2)}) collective-permute-start(bf16[512,2048]{1,0:T(8,128)(2,1)S(1)} %constant_dynamic-update-slice_fusion), channel_id=1, source_target_pairs={{0,1},{1,0},{2,3},{3,2},{4,5},{5,4},{6,7},{7,6},{8,9},{9,8},{10,11... | collective-permute-start | bytes 6291464 | tf_op jit(solution)/shard_map/ppermute | solution.py:20
  8.8 2.4 %copy-start = (bf16[1024,1024]{1,0:T(8,128)(2,1)}, bf16[1024,1024]{1,0:T(8,128)(2,1)S(1)}, u32[]{:S(2)}) copy-start(bf16[1024,1024]{1,0:T(8,128)(2,1)S(1)} %fusion) | copy-start | bytes 6291460
  11.2 1.3 copy-start.1
  12.5 3.6 %collective-permute-start.1 = (bf16[512,1024]{1,0:T(8,128)(2,1)S(1)}, bf16[512,1024]{1,0:T(8,128)(2,1)}, u32[]{:S(2)}, u32[]{:S(2)}) collective-permute-start(bf16[512,1024]{1,0:T(8,128)(2,1)S(1)} %negate_convert_fusion.3), channel_id=1, source_target_pairs={{0,1},{1,0},{2,3},{3,2},{4,5},{5,4},{6,7},{7,6},{8,9},{9,8},{10,11... | collective-permute-start | bytes 3145736 | tf_op jit(solution)/shard_map/ppermute | solution.py:20
  16.1 1.9 %copy-start.2 = (bf16[1024,1024]{1,0:T(8,128)(2,1)S(1)}, bf16[1024,1024]{1,0:T(8,128)(2,1)}, u32[]{:S(2)}) copy-start(bf16[1024,1024]{1,0:T(8,128)(2,1)} %copy-done.1) | copy-start | bytes 6291460
  19.3 28.3 %collective-permute-start.2 = (bf16[512,1024]{1,0:T(8,128)(2,1)S(1)}, bf16[512,1024]{1,0:T(8,128)(2,1)}, u32[]{:S(2)}, u32[]{:S(2)}) collective-permute-start(bf16[512,1024]{1,0:T(8,128)(2,1)S(1)} %subtract_convert_fusion.3), channel_id=1, source_target_pairs={{2,0},{3,1},{4,2},{5,3},{6,4},{7,5},{10,8},{11,9},{12,10},{13,11},... | collective-permute-start | bytes 3145736 | tf_op jit(solution)/shard_map/ppermute | solution.py:26
  50.9 3.0 %copy-start.3 = (bf16[1024,1024]{1,0:T(8,128)(2,1)S(1)}, bf16[1024,1024]{1,0:T(8,128)(2,1)}, u32[]{:S(2)}) copy-start(bf16[1024,1024]{1,0:T(8,128)(2,1)} %copy-done.1) | copy-start | bytes 6291460
  50.9 2.7 %collective-permute-start.3 = (bf16[512,1024]{1,0:T(8,128)(2,1)S(1)}, bf16[512,1024]{1,0:T(8,128)(2,1)S(1)}, u32[]{:S(2)}, u32[]{:S(2)}) collective-permute-start(bf16[512,1024]{1,0:T(8,128)(2,1)S(1)} %negate_convert_fusion.2), channel_id=1, source_target_pairs={{0,1},{1,0},{2,3},{3,2},{4,5},{5,4},{6,7},{7,6},{8,9},{9,8},{10,11... | collective-permute-start | bytes 3145736 | tf_op jit(solution)/shard_map/ppermute | solution.py:20
  55.2 28.0 %collective-permute-start.4 = (bf16[512,1024]{1,0:T(8,128)(2,1)S(1)}, bf16[512,1024]{1,0:T(8,128)(2,1)S(1)}, u32[]{:S(2)}, u32[]{:S(2)}) collective-permute-start(bf16[512,1024]{1,0:T(8,128)(2,1)S(1)} %subtract_convert_fusion.2), channel_id=1, source_target_pairs={{2,0},{3,1},{4,2},{5,3},{6,4},{7,5},{10,8},{11,9},{12,10},{13,11},... | collective-permute-start | bytes 3145736 | tf_op jit(solution)/shard_map/ppermute | solution.py:26
  84.5 2.7 %collective-permute-start.5 = (bf16[512,1024]{1,0:T(8,128)(2,1)S(1)}, bf16[512,1024]{1,0:T(8,128)(2,1)S(1)}, u32[]{:S(2)}, u32[]{:S(2)}) collective-permute-start(bf16[512,1024]{1,0:T(8,128)(2,1)S(1)} %negate_convert_fusion.1), channel_id=1, source_target_pairs={{0,1},{1,0},{2,3},{3,2},{4,5},{5,4},{6,7},{7,6},{8,9},{9,8},{10,11... | collective-permute-start | bytes 3145736 | tf_op jit(solution)/shard_map/ppermute | solution.py:20
  88.8 29.4 %copy-start.6 = (s32[4]{0:T(128)S(1)}, s32[4]{0:T(128)}, u32[]{:S(2)}) copy-start(s32[4]{0:T(128)} %param.5) | copy-start | bytes 52
  88.8 28.0 %collective-permute-start.6 = (bf16[512,1024]{1,0:T(8,128)(2,1)S(1)}, bf16[512,1024]{1,0:T(8,128)(2,1)S(1)}, u32[]{:S(2)}, u32[]{:S(2)}) collective-permute-start(bf16[512,1024]{1,0:T(8,128)(2,1)S(1)} %subtract_convert_fusion.1), channel_id=1, source_target_pairs={{2,0},{3,1},{4,2},{5,3},{6,4},{7,5},{10,8},{11,9},{12,10},{13,11},... | collective-permute-start | bytes 3145736 | tf_op jit(solution)/shard_map/ppermute | solution.py:26
  118.1 2.9 %copy-start.4 = (bf16[512,1024]{1,0:T(8,128)(2,1)}, bf16[512,1024]{1,0:T(8,128)(2,1)S(1)}, u32[]{:S(2)}) copy-start(bf16[512,1024]{1,0:T(8,128)(2,1)S(1)} %negate_convert_fusion) | copy-start | bytes 3145732
  118.2 2.7 %collective-permute-start.7 = (bf16[512,1024]{1,0:T(8,128)(2,1)S(1)}, bf16[512,1024]{1,0:T(8,128)(2,1)S(1)}, u32[]{:S(2)}, u32[]{:S(2)}) collective-permute-start(bf16[512,1024]{1,0:T(8,128)(2,1)S(1)} %negate_convert_fusion), channel_id=1, source_target_pairs={{0,1},{1,0},{2,3},{3,2},{4,5},{5,4},{6,7},{7,6},{8,9},{9,8},{10,11... | collective-permute-start | bytes 3145736 | tf_op jit(solution)/shard_map/ppermute | solution.py:20
where the time goes:
time: 135 us; the launch traced here: 134 us
  waiting for transfers between devices  91.9 us (68%)
  matrix products  19.6 us (15%)
  blocking collectives  10 us (7%)
  starting transfers between devices  5.27 us (4%)
  other arithmetic  4.45 us (3%)
  local copies, waits for them, and re-layouts  2.03 us (2%)
    ppermute x3, waiting for transfers between devices, from_behind(): return lax.ppermute(array, axis, pairs)  80.2 us
    ppermute x5, waiting for transfers between devices, partner_2(): return lax.ppermute(block, axis, route)  11.7 us
    all_gather x1, blocking collectives, shards(): lax.all_gather(var_rows[None, :], 'tm', axis=0, tiled=True)  10 us
    dot_general x4, matrix products, shards(): jnp.dot(carried, coupling_full, preferred_element_type=jnp.float32)  7.15 us
    dot_general x4, matrix products, shards(): lax.dot_general(coupling_cols, off_full, CONTRACT_FIRST, preferred_elemen...  6.22 us
    ppermute x3, starting transfers between devices, from_behind(): return lax.ppermute(array, axis, pairs)  4.06 us
    dot_general x1, matrix products, shards(): lax.dot_general(factor_cols, linv_full, CONTRACT_FIRST, preferred_element...  3.18 us
  transfers between devices with their start and end apart: 8, of which 7 were waited for; matrix products, arithmetic and copies ran while one was open for 3% of the time, Pallas kernels for 0%

commit v1 on v0

v1 whole, which is shorter than its diff:
```python
import jax
import jax.numpy as jnp
from jax import lax
from jax.sharding import PartitionSpec as P

TB = 4
SLOTS = 2
SPARE = 8

CONTRACT_FIRST = (((0,), (0,)), ((), ()))
BF16 = jnp.bfloat16
F32 = jnp.float32


def mm(a, b):
    return jnp.dot(a, b, preferred_element_type=F32)


def mm_t(a, b):
    return lax.dot_general(a, b, CONTRACT_FIRST, preferred_element_type=F32)


def shards(linv, sub, owner):
    group = lax.axis_size("tm") // TB
    rows, n = linv.shape
    half = n // 2
    paired = group == 2
    dev = lax.axis_index("tm")
    member = dev % group
    block = dev // group
    start = member * rows

    def block_to_block(values, source, target, members=range(group)):
        pairs = [(source * group + i, target * group + i) for i in members]
        return lax.ppermute(values, "tm", pairs)

    def gather(piece):
        step = 1
        while step < group:
            route = [(i, i ^ step) for i in range(TB * group)]
            other = lax.ppermute(piece, "tm", route)
            upper = (member // step) % 2 == 1
            piece = jnp.concatenate(
                [jnp.where(upper, other, piece), jnp.where(upper, piece, other)], 0
            )
            step *= 2
        return piece

    def gather_stacked(piece):
        return gather(piece[None])

    def own_cols(full):
        return lax.dynamic_slice_in_dim(full, start, rows, 1)

    def diagonal(square):
        size = square.shape[0]
        r = lax.broadcasted_iota(jnp.int32, (size, size), 0)
        c = lax.broadcasted_iota(jnp.int32, (size, size), 1)
        return jnp.sum(jnp.where(r == c, square.astype(F32), 0.0), axis=0)

    if paired:
        r_iota = lax.broadcasted_iota(jnp.int32, (rows, rows), 0)
        c_iota = lax.broadcasted_iota(jnp.int32, (rows, rows), 1)

    def pack(own_rows, passenger):
        if not paired:
            spare = jnp.zeros((SPARE, n), BF16).at[0].set(passenger.astype(BF16))
            return jnp.concatenate([own_rows, spare], 0)
        mine = lax.dynamic_slice_in_dim(own_rows, start, rows, 1)
        cross = lax.dynamic_slice_in_dim(own_rows, rows - start, rows, 1)
        body = jnp.where(c_iota >= r_iota, mine, cross)
        spare = jnp.concatenate(
            [
                diagonal(cross)[None],
                passenger.reshape(2, rows),
                jnp.zeros((SPARE - 3, rows), F32),
            ],
            0,
        ).astype(BF16)
        return jnp.concatenate([body, spare], 0)

    def unpack(packet):
        if not paired:
            full = gather(packet[:rows])
            return full, diagonal(full), packet[rows].astype(F32)
        both = gather_stacked(packet)
        p0 = both[0, :rows]
        p1 = both[1, :rows]
        p0t = p0.T
        p1t = p1.T
        on_cross = both[0, rows][None, :]
        s00 = jnp.where(c_iota >= r_iota, p0, p0t)
        s11 = jnp.where(c_iota >= r_iota, p1, p1t)
        s01 = jnp.where(c_iota < r_iota, p0, jnp.where(c_iota > r_iota, p1t, on_cross))
        s10 = jnp.where(c_iota > r_iota, p0t, jnp.where(c_iota < r_iota, p1, on_cross))
        full = jnp.concatenate(
            [jnp.concatenate([s00, s01], 1), jnp.concatenate([s10, s11], 1)], 0
        )
        diag = jnp.concatenate([diagonal(p0), diagonal(p1)])
        passenger = both[0, rows + 1 : rows + 3].astype(F32).reshape(n)
        return full, diag, passenger

    sub_1 = block_to_block(sub, 1, 0)
    left_1 = block_to_block(linv[:, :half], 1, 0)
    right_1 = block_to_block(linv[:, half:], 1, 0, range(group // 2, group))

    factor = gather(linv)
    lower = gather(sub)
    coupling = mm(lower, factor).astype(BF16)
    gram_rows = mm_t(own_cols(factor), factor)
    gram_diag = jnp.sum(jnp.square(factor.astype(F32)), axis=0)
    coupling_cols = own_cols(coupling)
    off_3 = -lax.dynamic_slice_in_dim(coupling, start, rows, 0)
    cov_3 = (gram_rows + mm_t(coupling_cols, coupling)).astype(BF16)

    packet = block_to_block(pack(cov_3, jnp.zeros((n,), F32)), 3, 2)
    carried, var_3, _ = unpack(packet)
    off_2_full = (-mm(carried, coupling)).astype(BF16)
    off_2 = lax.dynamic_slice_in_dim(off_2_full, start, rows, 0)
    cov_2 = (gram_rows - mm_t(coupling_cols, off_2_full)).astype(BF16)

    packet = pack(cov_2, var_3)
    packet_0 = block_to_block(packet, 2, 0)
    packet_1 = block_to_block(packet, 2, 1)

    at_first = block == 0
    factor_1 = gather(jnp.where(at_first, jnp.concatenate([left_1, right_1], 1), linv))
    lower_1 = gather(jnp.where(at_first, sub_1, sub))
    coupling_1 = mm(lower_1, factor_1).astype(BF16)
    gram_1 = mm_t(factor_1, factor_1)

    carried, var_2, var_3 = unpack(jnp.where(at_first, packet_0, packet_1))
    off_1_full = (-mm(carried, coupling_1)).astype(BF16)
    cov_1_full = (gram_1 - mm_t(coupling_1, off_1_full)).astype(BF16)
    off_1 = lax.dynamic_slice_in_dim(off_1_full, start, rows, 0)
    cov_1 = lax.dynamic_slice_in_dim(cov_1_full, start, rows, 0)
    var_1 = diagonal(cov_1_full)

    off_0_full = (-mm(cov_1_full, coupling)).astype(BF16)
    off_0 = lax.dynamic_slice_in_dim(off_0_full, start, rows, 0)
    var_0 = gram_diag - jnp.sum(coupling.astype(F32) * off_0_full.astype(F32), axis=0)
    cov_0 = (gram_rows - mm_t(coupling_cols, off_0_full)).astype(BF16)

    variances = jnp.stack([var_0, var_1, var_2, var_3]).astype(BF16)
    heard = [block_to_block(variances, 0, t) for t in range(1, TB)]
    variances = jnp.where(at_first, variances, sum(heard)).astype(F32)

    def choose(at_0, at_1, at_2, at_3):
        late = jnp.where(at_first, at_0, at_1)
        return jnp.where(block < 2, late, jnp.where(block == 2, at_2, at_3))

    cov_rows = choose(cov_0, cov_1, cov_2, cov_3)
    off_rows = choose(off_0, off_1, off_2, off_3)

    positions = lax.broadcasted_iota(jnp.int32, (TB, TB), 1)
    current = lax.broadcasted_iota(jnp.int32, (TB, TB), 0)
    same_owner = owner[:, None] == owner[None, :]
    slot_rank = jnp.sum(jnp.where(same_owner & (positions < current), 1, 0), axis=1)
    slot_iota = lax.broadcasted_iota(jnp.int32, (SLOTS, TB), 0)
    selector = (owner[None, :] == dev) & (slot_rank[None, :] == slot_iota)
    owned_var = sum(
        jnp.where(selector[:, t, None], variances[t][None, :], 0.0) for t in range(TB)
    )
    return (cov_rows, off_rows, owned_var)


def solution(mesh):
    return jax.shard_map(
        shards,
        mesh=mesh,
        in_specs=(P(("cfg", "tm"), None), P(("cfg", "tm"), None), P("cfg")),
        out_specs=(P(("cfg", "tm"), None), P(("cfg", "tm"), None), P(("cfg", "tm"), None)),
        check_vma=False,
    )
```

time: 135 us -> 113 us (0.84)
  waiting for transfers between devices: 91.9 us -> 44 us
  starting transfers between devices: 5.27 us -> 17.9 us
  other arithmetic: 4.45 us -> 16.6 us
  blocking collectives: 10 us -> 0 us
  local copies, waits for them, and re-layouts: 2.03 us -> 8.48 us
  matrix products: 19.6 us -> 24.5 us
    ppermute x8 -> x15, waiting for transfers between devices: 91.9 us -> 44 us  [the longest x9 43.2 us: block_to_block(): return lax.ppermute(values, 'tm', pairs)]
    ppermute x8 -> x15, starting transfers between devices: 5.27 us -> 17.9 us  [the longest x9 11.6 us: block_to_block(): return lax.ppermute(values, 'tm', pairs)]
    all_gather x1 -> x0, blocking collectives: 10 us -> none  [shards(): lax.all_gather(var_rows[None, :], 'tm', axis=0, tiled=True)]
    select_n x5 -> x11, other arithmetic: 4.05 us -> 11 us  [the longest x5 4.62 us: gather(): jnp.where(upper, other, piece)]
    dot_general x11, matrix products: 19.6 us -> 24.5 us  [the longest x5 13.1 us: mm(): return jnp.dot(a, b, preferred_element_type=F32)]
    squeeze x0 -> x6, local copies, waits for them, and re-layouts: none -> 4.35 us  [the longest x4 3.12 us: unpack(): p0 = both[0, :rows]]
    reduce_sum x0 -> x6, other arithmetic: none -> 2.27 us  [the longest x1 1.7 us: shards(): gram_diag = jnp.sum(jnp.square(factor.astype(F32)), axis=0)]
  transfers between devices with their start and end apart: 8 -> 15, of which waited for: 7 -> 4; matrix products, arithmetic and copies ran while one was open for 3% -> 26% of each run, Pallas kernels for 0% -> 0%
where the time goes in v1:
time: 113 us
  waiting for transfers between devices  44 us (39%)
  matrix products  24.5 us (22%)
  starting transfers between devices  17.9 us (16%)
  other arithmetic  16.6 us (15%)
  local copies, waits for them, and re-layouts  8.48 us (8%)
  between operations  1.29 us (1%)
    ppermute x9, waiting for transfers between devices, block_to_block(): return lax.ppermute(values, 'tm', pairs)  43.2 us
    dot_general x5, matrix products, mm(): return jnp.dot(a, b, preferred_element_type=F32)  13.1 us
    ppermute x9, starting transfers between devices, block_to_block(): return lax.ppermute(values, 'tm', pairs)  11.6 us
    dot_general x6, matrix products, mm_t(): return lax.dot_general(a, b, CONTRACT_FIRST, preferred_element_type=F32)  11.4 us
    ppermute x6, starting transfers between devices, gather(): other = lax.ppermute(piece, 'tm', route)  6.34 us
    select_n x5, other arithmetic, gather(): jnp.where(upper, other, piece)  4.62 us
    squeeze x4, local copies, waits for them, and re-layouts, unpack(): p0 = both[0, :rows]  3.12 us
    unnamed x48, local copies, waits for them, and re-layouts  2.59 us
  transfers between devices with their start and end apart: 15, of which 4 were waited for; matrix products, arithmetic and copies ran while one was open for 26% of the time, Pallas kernels for 0%

profile of v1, /device:TPU:0, one launch (start us, length us, event | category | flops | bytes accessed | tf_op | source)
XLA Modules:
  0.0 112.8 jit_solution(7079302913246923817)
XLA Ops:
  0.6 0.6 collective-permute-start
  1.2 1.3 %fusion.66 = (bf16[512,512]{1,0:T(8,128)(2,1)S(1)}, bf16[512,512]{1,0:T(8,128)(2,1)S(1)}) fusion(bf16[512,1024]{1,0:T(8,128)(2,1)} %param.3), kind=kLoop, calls=%fused_computation.120 | loop fusion | bytes 2097152 | tf_op jit(solution)/shard_map/slice | solution.py:104
  2.5 1.3 %collective-permute-start.2 = (bf16[512,512]{1,0:T(8,128)(2,1)S(1)}, bf16[512,512]{1,0:T(8,128)(2,1)}, u32[]{:S(2)}, u32[]{:S(2)}) collective-permute-start(bf16[512,512]{1,0:T(8,128)(2,1)S(1)} %get-tuple-element.16), channel_id=1, source_target_pairs={{2,0},{3,1},{10,8},{11,9},{18,16},{19,17},{26,24},{27,25}} | collective-permute-start | bytes 1572872 | tf_op jit(solution)/shard_map/ppermute | solution.py:35
  3.8 1.5 %collective-permute-start.3 = (bf16[512,512]{1,0:T(8,128)(2,1)S(1)}, bf16[512,512]{1,0:T(8,128)(2,1)}, u32[]{:S(2)}, u32[]{:S(2)}) collective-permute-start(bf16[512,512]{1,0:T(8,128)(2,1)S(1)} %get-tuple-element.17), channel_id=1, source_target_pairs={{3,1},{11,9},{19,17},{27,25}} | collective-permute-start | bytes 1572872 | tf_op jit(solution)/shard_map/ppermute | solution.py:35
  5.3 0.0 collective-permute-start.1
  5.3 1.3 %collective-permute-start.5 = (bf16[512,1024]{1,0:T(8,128)(2,1)S(1)}, bf16[512,1024]{1,0:T(8,128)(2,1)}, u32[]{:S(2)}, u32[]{:S(2)}) collective-permute-start(bf16[512,1024]{1,0:T(8,128)(2,1)S(1)} %copy-done.12), channel_id=1, source_target_pairs={{2,0},{3,1},{10,8},{11,9},{18,16},{19,17},{26,24},{27,25}} | collective-permute-start | bytes 3145736 | tf_op jit(solution)/shard_map/ppermute | solution.py:35
  6.7 0.1 pad.23.clone
  6.7 0.1 pad.22.clone
  6.8 12.5 %collective-permute-done.2 = bf16[512,512]{1,0:T(8,128)(2,1)} collective-permute-done((bf16[512,512]{1,0:T(8,128)(2,1)S(1)}, bf16[512,512]{1,0:T(8,128)(2,1)}, u32[]{:S(2)}, u32[]{:S(2)}) %collective-permute-start.2) | collective-permute-done | bytes 524320 | tf_op jit(solution)/shard_map/ppermute | solution.py:35
  19.3 2.4 %broadcast_select_fusion.6 = (bf16[512,1024]{1,0:T(8,128)(2,1)S(1)}, bf16[512,1024]{1,0:T(8,128)(2,1)S(1)}, bf16[512,1024]{1,0:T(8,128)(2,1)S(1)}) fusion(bf16[512,1024]{1,0:T(8,128)(2,1)S(1)} %copy-done, bf16[512,1024]{1,0:T(8,128)(2,1)} %collective-permute-done, pred[]{:T(512)S(6)} %eq.73, bf16[512,512]{1,0:T(8,128)(2,1)} %collective-permute-done.3, ...), kind=kLoop, calls=%fused_computation.74 | loop fusion | flops 3670016 | bytes 6291458 | tf_op jit(solution)/shard_map/jit(_where)/select_n | solution.py:44
  21.7 1.3 %fusion.29 = f32[512,1024]{1,0:T(8,128)S(1)} fusion(s32[]{:T(128)S(6)} %select_n.248, bf16[512,1024]{1,0:T(8,128)(2,1)S(1)} %get-tuple-element.14, bf16[512,1024]{1,0:T(8,128)(2,1)S(1)} %get-tuple-element.13), kind=kOutput, calls=%fused_computation.40 | convolution fusion | flops 1080033280 | bytes 6291460 | tf_op jit(solution)/shard_map/dot_general | solution.py:20
  23.0 18.7 %collective-permute-done.5 = bf16[512,1024]{1,0:T(8,128)(2,1)} collective-permute-done((bf16[512,1024]{1,0:T(8,128)(2,1)S(1)}, bf16[512,1024]{1,0:T(8,128)(2,1)}, u32[]{:S(2)}, u32[]{:S(2)}) %collective-permute-start.5) | collective-permute-done | bytes 1048608 | tf_op jit(solution)/shard_map/ppermute | solution.py:35
  41.7 1.7 %broadcast_select_fusion.5 = (bf16[512,1024]{1,0:T(8,128)(2,1)S(1)}, bf16[512,1024]{1,0:T(8,128)(2,1)S(1)}, bf16[512,1024]{1,0:T(8,128)(2,1)S(1)}) fusion(bf16[512,1024]{1,0:T(8,128)(2,1)} %collective-permute-done.1, bf16[512,1024]{1,0:T(8,128)(2,1)S(1)} %copy-done.12, pred[]{:T(512)S(6)} %eq.73, bf16[512,1024]{1,0:T(8,128)(2,1)} %collective-permute-done.5, ...), kind=kLoop, calls=%fused_computation.73 | loop fusion | flops 1572864 | bytes 6291458 | tf_op jit(solution)/shard_map/jit(_where)/select_n | solution.py:44
  43.5 2.3 %fusion.25 = bf16[1024,1024]{1,0:T(8,128)(2,1)S(1)} fusion(bf16[512,1024]{1,0:T(8,128)(2,1)S(1)} %get-tuple-element.12, bf16[512,1024]{1,0:T(8,128)(2,1)S(1)} %get-tuple-element.11, bf16[512,1024]{1,0:T(8,128)(2,1)S(1)} %get-tuple-element.13, bf16[512,1024]{1,0:T(8,128)(2,1)S(1)} %get-tuple-element.14), kind=kOutput, calls=%fused_computation.38 | convolution fusion | flops 2156920832 | bytes 6291456 | tf_op jit(solution)/shard_map/dot_general | solution.py:16
  45.9 1.3 %add_convert_fusion = bf16[512,1024]{1,0:T(8,128)(2,1)S(1)} fusion(f32[512,1024]{1,0:T(8,128)S(1)} %fusion.29, bf16[1024,1024]{1,0:T(8,128)(2,1)S(1)} %fusion.25, s32[]{:T(128)S(6)} %select_n.248), kind=kOutput, calls=%fused_computation.36 | convolution fusion | flops 1074790400 | bytes 6291460 | tf_op jit(solution)/shard_map/dot_general | solution.py:20
  47.2 0.1 select_reduce_fusion.6
  47.3 0.1 fusion.44
  47.4 0.2 maximum_maximum_fusion
  47.6 0.7 collective-permute-start.7
  48.3 5.2 %collective-permute-start.8 = (bf16[1,520,512]{2,1,0:T(8,128)(2,1)S(1)}, bf16[1,520,512]{2,1,0:T(8,128)(2,1)S(1)}, u32[]{:S(2)}, u32[]{:S(2)}) collective-permute-start(bf16[1,520,512]{2,1,0:T(8,128)(2,1)S(1)} %bitcast.62), channel_id=1, source_target_pairs={{0,1},{1,0},{2,3},{3,2},{4,5},{5,4},{6,7},{7,6},{8,9},{9,8},{10,11... | collective-permute-start | bytes 1597448 | tf_op jit(solution)/shard_map/ppermute | solution.py:41
  53.5 0.2 select_reduce_fusion.7
  53.7 0.1 fusion.57
  53.8 0.5 collective-permute-start.6
  54.3 0.8 collective-permute-done.8
  55.0 0.1 broadcast_select_fusion.10
  55.1 0.8 slice_bitcast_fusion.1
  56.0 0.2 select_reduce_fusion.3
  56.2 1.0 copy.11
  57.2 2.0 %copy.10 = bf16[512,512]{0,1:T(8,128)(2,1)} copy(bf16[512,512]{1,0:T(8,128)(2,1)} %slice_bitcast_fusion.1) | data formatting | bytes 1048576 | tf_op jit(solution)/shard_map/squeeze | solution.py:87
  59.2 1.6 %fusion.43 = (bf16[512,512]{1,0:T(8,128)(2,1)S(1)}, bf16[512,512]{1,0:T(8,128)(2,1)S(1)}, bf16[512,512]{1,0:T(8,128)(2,1)S(1)}, bf16[512,512]{1,0:T(8,128)(2,1)S(1)}) fusion(bf16[512,512]{0,1:T(8,128)(2,1)} %copy.10, bf16[1,520,512]{2,1,0:T(8,128)(2,1)S(1)} %broadcast_select_fusion.10, bf16[512]{0:T(512)(128)(2,1)S(1)} %slice_reduce_fusion.1, ...), kind=kLoop, calls=%fused_computation.66 | loop fusion | flops 2359296 | bytes 4195328 | tf_op jit(solution)/shard_map/jit(_where)/select_n | solution.py:92
  60.9 0.3 copy-done.14
  61.2 2.3 %negate_convert_fusion.2 = bf16[1024,1024]{1,0:T(8,128)(2,1)S(1)} fusion(bf16[1024,1024]{1,0:T(8,128)(2,1)S(1)} %copy-done.14, bf16[512,512]{1,0:T(8,128)(2,1)S(1)} %get-tuple-element.24, bf16[512,512]{1,0:T(8,128)(2,1)S(1)} %get-tuple-element.23, bf16[512,512]{1,0:T(8,128)(2,1)S(1)} %get-tuple-element.22, bf16[512,512]{1,0:T(8,128)(2,1)S(1)} %get-tuple-element.21), kind=kOutput, calls=%fused_computation.7 | convolution fusion | flops 2157969408 | bytes 6291456 | tf_op jit(solution)/shard_map/dot_general | solution.py:16
  63.5 1.3 %subtract_convert_fusion.2 = bf16[512,1024]{1,0:T(8,128)(2,1)S(1)} fusion(f32[512,1024]{1,0:T(8,128)S(1)} %copy-done.20, bf16[1024,1024]{1,0:T(8,128)(2,1)S(1)} %negate_convert_fusion.2, bf16[1024,1024]{1,0:T(8,128)(2,1)S(1)} %copy-done.14, s32[]{:T(128)S(6)} %select_n.248), kind=kOutput, calls=%fused_computation.35 | convolution fusion | flops 1074790400 | bytes 6291460 | tf_op jit(solution)/shard_map/dot_general | solution.py:20
  64.8 0.0 copy-done.16
  64.8 0.1 select_reduce_fusion.5
  64.9 0.9 copy-done.6
  65.8 0.1 fusion.41
  65.9 1.0 maximum_maximum_fusion.1
  66.9 1.5 %collective-permute-start.10 = (bf16[520,512]{1,0:T(8,128)(2,1)}, bf16[520,512]{1,0:T(8,128)(2,1)}, u32[]{:S(2)}, u32[]{:S(2)}) collective-permute-start(bf16[520,512]{1,0:T(8,128)(2,1)} %maximum_maximum_fusion.1), channel_id=1, source_target_pairs={{4,2},{5,3},{12,10},{13,11},{20,18},{21,19},{28,26},{29,27}} | collective-permute-start | bytes 1597448 | tf_op jit(solution)/shard_map/ppermute | solution.py:35
  68.4 1.5 %collective-permute-start.9 = (bf16[520,512]{1,0:T(8,128)(2,1)}, bf16[520,512]{1,0:T(8,128)(2,1)}, u32[]{:S(2)}, u32[]{:S(2)}) collective-permute-start(bf16[520,512]{1,0:T(8,128)(2,1)} %maximum_maximum_fusion.1), channel_id=1, source_target_pairs={{4,0},{5,1},{12,8},{13,9},{20,16},{21,17},{28,24},{29,25}} | collective-permute-start | bytes 1597448 | tf_op jit(solution)/shard_map/ppermute | solution.py:35
  69.9 1.7 %multiply_reduce_fusion.1 = f32[1024]{0:T(1024)S(1)} fusion(bf16[512,1024]{1,0:T(8,128)(2,1)S(1)} %copy-done.2, bf16[512,1024]{1,0:T(8,128)(2,1)} %copy-done.3), kind=kLoop, calls=%fused_computation.3 | loop fusion | flops 6290432 | bytes 2101248 | tf_op jit(solution)/shard_map/reduce_sum | solution.py:111
  71.6 1.4 %broadcast_select_fusion.3 = (bf16[512,1024]{1,0:T(8,128)(2,1)S(1)}, bf16[512,1024]{1,0:T(8,128)(2,1)S(1)}) fusion(bf16[512,1024]{1,0:T(8,128)(2,1)} %collective-permute-done.4, bf16[512,1024]{1,0:T(8,128)(2,1)S(1)} %get-tuple-element.15, pred[]{:T(512)S(6)} %eq.73), kind=kLoop, calls=%fused_computation.71 | loop fusion | flops 1048576 | bytes 4194305 | tf_op jit(solution)/shard_map/jit(_where)/select_n | solution.py:44
  73.0 12.0 %collective-permute-done.9 = bf16[520,512]{1,0:T(8,128)(2,1)} collective-permute-done((bf16[520,512]{1,0:T(8,128)(2,1)}, bf16[520,512]{1,0:T(8,128)(2,1)}, u32[]{:S(2)}, u32[]{:S(2)}) %collective-permute-start.9) | collective-permute-done | bytes 532512 | tf_op jit(solution)/shard_map/ppermute | solution.py:35
  84.9 1.1 select_bitcast_fusion
  86.0 0.1 collective-permute-start.11
  86.1 1.4 %broadcast_select_fusion.1 = (bf16[512,1024]{1,0:T(8,128)(2,1)S(1)}, bf16[512,1024]{1,0:T(8,128)(2,1)S(1)}) fusion(bf16[512,1024]{1,0:T(8,128)(2,1)} %collective-permute-done.6, bf16[512,1024]{1,0:T(8,128)(2,1)S(1)} %get-tuple-element.18, pred[]{:T(512)S(6)} %eq.73), kind=kLoop, calls=%fused_computation.69 | loop fusion | flops 1048576 | bytes 4194305 | tf_op jit(solution)/shard_map/jit(_where)/select_n | solution.py:44
  87.5 3.7 %fusion.22 = bf16[1024,1024]{1,0:T(8,128)(2,1)} fusion(bf16[512,1024]{1,0:T(8,128)(2,1)S(1)} %get-tuple-element.10, bf16[512,1024]{1,0:T(8,128)(2,1)S(1)} %get-tuple-element.9, bf16[512,1024]{1,0:T(8,128)(2,1)S(1)} %get-tuple-element.8, bf16[512,1024]{1,0:T(8,128)(2,1)S(1)} %get-tuple-element.7), kind=kOutput, calls=%fused_computation.37 | convolution fusion | flops 2156920832 | bytes 6291456 | tf_op jit(solution)/shard_map/dot_general | solution.py:16
  91.2 0.1 broadcast_select_fusion.9
  91.3 0.1 select_reduce_fusion.2
  91.4 0.2 select_reduce_fusion.1
  91.6 0.2 copy.13
  91.8 0.2 copy.12
  92.1 0.3 fusion.40
  92.4 1.3 %copy-done.22 = bf16[1024,1024]{1,0:T(8,128)(2,1)S(1)} copy-done((bf16[1024,1024]{1,0:T(8,128)(2,1)S(1)}, bf16[1024,1024]{1,0:T(8,128)(2,1)}, u32[]{:S(2)}) %copy-start.22) | copy-done | bytes 2097176
  93.7 2.3 %negate_convert_fusion.1 = bf16[1024,1024]{1,0:T(8,128)(2,1)S(1)} fusion(bf16[1024,1024]{1,0:T(8,128)(2,1)S(1)} %copy-done.22, bf16[512,512]{1,0:T(8,128)(2,1)S(1)} %get-tuple-element.26, bf16[512,512]{1,0:T(8,128)(2,1)S(1)} %get-tuple-element.25, bf16[512,512]{1,0:T(8,128)(2,1)S(1)} %get-tuple-element.20, bf16[512,512]{1,0:T(8,128)(2,1)S(1)} %get-tuple-element.19), kind=kOutput, calls=%fused_computation.6 | convolution fusion | flops 2157969408 | bytes 6291456 | tf_op jit(solution)/shard_map/dot_general | solution.py:16
  96.0 2.4 %fusion.68 = f32[1024,1024]{1,0:T(8,128)S(1)} fusion(bf16[1024,1024]{1,0:T(8,128)(2,1)S(1)} %copy-done.22, bf16[1024,1024]{1,0:T(8,128)(2,1)S(1)} %negate_convert_fusion.1), kind=kOutput, calls=%fused_computation.122 | convolution fusion | flops 2147483648 | bytes 8388608 | tf_op jit(solution)/shard_map/dot_general | solution.py:20
  98.5 2.6 %select_reduce_fusion = (bf16[1024]{0:T(1024)(128)(2,1)S(1)}, bf16[1024,1024]{1,0:T(8,128)(2,1)S(1)}) fusion(f32[1024,1024]{1,0:T(8,128)S(1)} %fusion.68, bf16[512,1024]{1,0:T(8,128)(2,1)S(1)} %copy-done.11, bf16[512,1024]{1,0:T(8,128)(2,1)S(1)} %copy-done.9), kind=kOutput, calls=%fused_computation | convolution fusion | flops 2157968384 | bytes 8390656 | tf_op jit(solution)/shard_map/dot_general | solution.py:20
  101.1 2.4 %multiply_reduce_fusion = (f32[1024]{0:T(1024)S(1)}, bf16[1024,1024]{1,0:T(8,128)(2,1)S(1)}) fusion(bf16[1024,1024]{1,0:T(8,128)(2,1)S(1)} %copy-done.15, bf16[1024,1024]{1,0:T(8,128)(2,1)S(1)} %get-tuple-element.36), kind=kOutput, calls=%fused_computation.2 | convolution fusion | flops 2153774080 | bytes 6295552 | tf_op jit(solution)/shard_map/dot_general | solution.py:16
  103.6 1.3 %collective-permute-start.14 = (bf16[4,1024]{1,0:T(4,128)(2,1)S(1)}, bf16[4,1024]{1,0:T(4,128)(2,1)S(1)}, u32[]{:S(2)}, u32[]{:S(2)}) collective-permute-start(bf16[4,1024]{1,0:T(4,128)(2,1)S(1)} %pad_maximum_fusion.6), channel_id=1, source_target_pairs={{0,6},{1,7},{8,14},{9,15},{16,22},{17,23},{24,30},{25,31}} | collective-permute-start | bytes 24584 | tf_op jit(solution)/shard_map/ppermute | solution.py:35
  104.9 1.3 %collective-permute-start.13 = (bf16[4,1024]{1,0:T(4,128)(2,1)S(1)}, bf16[4,1024]{1,0:T(4,128)(2,1)S(1)}, u32[]{:S(2)}, u32[]{:S(2)}) collective-permute-start(bf16[4,1024]{1,0:T(4,128)(2,1)S(1)} %pad_maximum_fusion.6), channel_id=1, source_target_pairs={{0,4},{1,5},{8,12},{9,13},{16,20},{17,21},{24,28},{25,29}} | collective-permute-start | bytes 24584 | tf_op jit(solution)/shard_map/ppermute | solution.py:35
  106.2 1.3 %collective-permute-start.12 = (bf16[4,1024]{1,0:T(4,128)(2,1)S(1)}, bf16[4,1024]{1,0:T(4,128)(2,1)S(1)}, u32[]{:S(2)}, u32[]{:S(2)}) collective-permute-start(bf16[4,1024]{1,0:T(4,128)(2,1)S(1)} %pad_maximum_fusion.6), channel_id=1, source_target_pairs={{0,2},{1,3},{8,10},{9,11},{16,18},{17,19},{24,26},{25,27}} | collective-permute-start | bytes 24584 | tf_op jit(solution)/shard_map/ppermute | solution.py:35
  107.5 2.6 %select_select_fusion.1 = bf16[512,1024]{1,0:T(8,128)(2,1)} fusion(bf16[512,1024]{1,0:T(8,128)(2,1)S(1)} %copy-done.7, bf16[512,1024]{1,0:T(8,128)(2,1)S(1)} %copy-done.5, bf16[1024,1024]{1,0:T(8,128)(2,1)S(1)} %get-tuple-element.36, s32[]{:T(128)S(6)} %select_n.248, pred[]{:T(512)S(6)} %eq.75, pred[]{:T(512)S(6)} %eq.72, pred[]{:T(512)S(6)} %lt.54, ...), kind=kOutput, calls=%fused_computation.45 | convolution fusion | flops 1076363264 | bytes 9439744 | tf_op jit(solution)/shard_map/dot_general | solution.py:20
  110.1 1.9 %select_select_fusion = bf16[512,1024]{1,0:T(8,128)(2,1)} fusion(bf16[1024,1024]{1,0:T(8,128)(2,1)S(1)} %copy-done.15, s32[]{:T(128)S(6)} %select_n.248, bf16[1024,1024]{1,0:T(8,128)(2,1)S(1)} %copy-done.17, bf16[1024,1024]{1,0:T(8,128)(2,1)S(1)} %negate_convert_fusion.1, bf16[1024,1024]{1,0:T(8,128)(2,1)S(1)} %get-tuple-element.38, pred[]{:T(512)S(6)} %eq.75, ...), kind=kLoop, calls=%fused_computation.44 | loop fusion | flops 3145728 | bytes 5242887 | tf_op jit(solution)/shard_map/jit(_where)/select_n | solution.py:150
  112.1 0.7 select_add_fusion
  (75 shorter events, 0.4 us)
Async XLA Ops:
  0.6 18.7 %copy-start = (bf16[512,1024]{1,0:T(8,128)(2,1)S(1)}, bf16[512,1024]{1,0:T(8,128)(2,1)}, u32[]{:S(2)}) copy-start(bf16[512,1024]{1,0:T(8,128)(2,1)} %param.3) | copy-start | bytes 3145732
  0.6 4.6 %copy-start.12 = (bf16[512,1024]{1,0:T(8,128)(2,1)S(1)}, bf16[512,1024]{1,0:T(8,128)(2,1)}, u32[]{:S(2)}) copy-start(bf16[512,1024]{1,0:T(8,128)(2,1)} %param.4) | copy-start | bytes 3145732
  0.6 18.6 %collective-permute-start = (bf16[512,1024]{1,0:T(8,128)(2,1)}, bf16[512,1024]{1,0:T(8,128)(2,1)}, u32[]{:S(2)}, u32[]{:S(2)}) collective-permute-start(bf16[512,1024]{1,0:T(8,128)(2,1)} %param.3), channel_id=1, source_target_pairs={{0,1},{1,0},{2,3},{3,2},{4,5},{5,4},{6,7},{7,6},{8,9},{9,8},{10,11... | collective-permute-start | bytes 3145736 | tf_op jit(solution)/shard_map/ppermute | solution.py:41
  2.5 16.8 %collective-permute-start.2 = (bf16[512,512]{1,0:T(8,128)(2,1)S(1)}, bf16[512,512]{1,0:T(8,128)(2,1)}, u32[]{:S(2)}, u32[]{:S(2)}) collective-permute-start(bf16[512,512]{1,0:T(8,128)(2,1)S(1)} %get-tuple-element.16), channel_id=1, source_target_pairs={{2,0},{3,1},{10,8},{11,9},{18,16},{19,17},{26,24},{27,25}} | collective-permute-start | bytes 1572872 | tf_op jit(solution)/shard_map/ppermute | solution.py:35
  3.8 15.5 %collective-permute-start.3 = (bf16[512,512]{1,0:T(8,128)(2,1)S(1)}, bf16[512,512]{1,0:T(8,128)(2,1)}, u32[]{:S(2)}, u32[]{:S(2)}) collective-permute-start(bf16[512,512]{1,0:T(8,128)(2,1)S(1)} %get-tuple-element.17), channel_id=1, source_target_pairs={{3,1},{11,9},{19,17},{27,25}} | collective-permute-start | bytes 1572872 | tf_op jit(solution)/shard_map/ppermute | solution.py:35
  5.3 17.7 %collective-permute-start.1 = (bf16[512,1024]{1,0:T(8,128)(2,1)S(1)}, bf16[512,1024]{1,0:T(8,128)(2,1)}, u32[]{:S(2)}, u32[]{:S(2)}) collective-permute-start(bf16[512,1024]{1,0:T(8,128)(2,1)S(1)} %copy-done.12), channel_id=1, source_target_pairs={{0,1},{1,0},{2,3},{3,2},{4,5},{5,4},{6,7},{7,6},{8,9},{9,8},{10,11... | collective-permute-start | bytes 3145736 | tf_op jit(solution)/shard_map/ppermute | solution.py:41
  5.3 36.4 %collective-permute-start.5 = (bf16[512,1024]{1,0:T(8,128)(2,1)S(1)}, bf16[512,1024]{1,0:T(8,128)(2,1)}, u32[]{:S(2)}, u32[]{:S(2)}) collective-permute-start(bf16[512,1024]{1,0:T(8,128)(2,1)S(1)} %copy-done.12), channel_id=1, source_target_pairs={{2,0},{3,1},{10,8},{11,9},{18,16},{19,17},{26,24},{27,25}} | collective-permute-start | bytes 3145736 | tf_op jit(solution)/shard_map/ppermute | solution.py:35
  21.7 21.8 %copy-start.1 = (bf16[512,1024]{1,0:T(8,128)(2,1)}, bf16[512,1024]{1,0:T(8,128)(2,1)S(1)}, u32[]{:S(2)}) copy-start(bf16[512,1024]{1,0:T(8,128)(2,1)S(1)} %get-tuple-element.13) | copy-start | bytes 3145732
  21.7 21.8 %copy-start.3 = (bf16[512,1024]{1,0:T(8,128)(2,1)}, bf16[512,1024]{1,0:T(8,128)(2,1)S(1)}, u32[]{:S(2)}) copy-start(bf16[512,1024]{1,0:T(8,128)(2,1)S(1)} %get-tuple-element.14) | copy-start | bytes 3145732
  23.0 22.9 %copy-start.19 = (f32[512,1024]{1,0:T(8,128)}, f32[512,1024]{1,0:T(8,128)S(1)}, u32[]{:S(2)}) copy-start(f32[512,1024]{1,0:T(8,128)S(1)} %fusion.29) | copy-start | bytes 6291460
  45.9 1.3 %copy-start.13 = (bf16[1024,1024]{1,0:T(8,128)(2,1)}, bf16[1024,1024]{1,0:T(8,128)(2,1)S(1)}, u32[]{:S(2)}) copy-start(bf16[1024,1024]{1,0:T(8,128)(2,1)S(1)} %fusion.25) | copy-start | bytes 6291460
  47.2 7.9 %copy-start.4 = (bf16[512,1024]{1,0:T(8,128)(2,1)}, bf16[512,1024]{1,0:T(8,128)(2,1)S(1)}, u32[]{:S(2)}) copy-start(bf16[512,1024]{1,0:T(8,128)(2,1)S(1)} %add_convert_fusion) | copy-start | bytes 3145732
  47.2 6.3 %copy-start.18 = (s32[4]{0:T(128)S(1)}, s32[4]{0:T(128)}, u32[]{:S(2)}) copy-start(s32[4]{0:T(128)} %param.5) | copy-start | bytes 52
  47.6 0.7 collective-permute-start.7
  48.3 6.7 %collective-permute-start.8 = (bf16[1,520,512]{2,1,0:T(8,128)(2,1)S(1)}, bf16[1,520,512]{2,1,0:T(8,128)(2,1)S(1)}, u32[]{:S(2)}, u32[]{:S(2)}) collective-permute-start(bf16[1,520,512]{2,1,0:T(8,128)(2,1)S(1)} %bitcast.62), channel_id=1, source_target_pairs={{0,1},{1,0},{2,3},{3,2},{4,5},{5,4},{6,7},{7,6},{8,9},{9,8},{10,11... | collective-permute-start | bytes 1597448 | tf_op jit(solution)/shard_map/ppermute | solution.py:41
  53.7 17.8 %collective-permute-start.4 = (bf16[512,1024]{1,0:T(8,128)(2,1)S(1)}, bf16[512,1024]{1,0:T(8,128)(2,1)}, u32[]{:S(2)}, u32[]{:S(2)}) collective-permute-start(bf16[512,1024]{1,0:T(8,128)(2,1)S(1)} %get-tuple-element.15), channel_id=1, source_target_pairs={{0,1},{1,0},{2,3},{3,2},{4,5},{5,4},{6,7},{7,6},{8,9},{9,8},{10,11... | collective-permute-start | bytes 3145736 | tf_op jit(solution)/shard_map/ppermute | solution.py:41
  53.8 32.4 %collective-permute-start.6 = (bf16[512,1024]{1,0:T(8,128)(2,1)S(1)}, bf16[512,1024]{1,0:T(8,128)(2,1)}, u32[]{:S(2)}, u32[]{:S(2)}) collective-permute-start(bf16[512,1024]{1,0:T(8,128)(2,1)S(1)} %get-tuple-element.18), channel_id=1, source_target_pairs={{0,1},{1,0},{2,3},{3,2},{4,5},{5,4},{6,7},{7,6},{8,9},{9,8},{10,11... | collective-permute-start | bytes 3145736 | tf_op jit(solution)/shard_map/ppermute | solution.py:41
  59.2 1.9 %copy-start.14 = (bf16[1024,1024]{1,0:T(8,128)(2,1)S(1)}, bf16[1024,1024]{1,0:T(8,128)(2,1)}, u32[]{:S(2)}) copy-start(bf16[1024,1024]{1,0:T(8,128)(2,1)} %copy-done.13) | copy-start | bytes 6291460
  61.1 2.3 %copy-start.20 = (f32[512,1024]{1,0:T(8,128)S(1)}, f32[512,1024]{1,0:T(8,128)}, u32[]{:S(2)}) copy-start(f32[512,1024]{1,0:T(8,128)} %copy-done.19) | copy-start | bytes 6291460
  63.5 1.3 %copy-start.16 = (bf16[1024,1024]{1,0:T(8,128)(2,1)}, bf16[1024,1024]{1,0:T(8,128)(2,1)S(1)}, u32[]{:S(2)}) copy-start(bf16[1024,1024]{1,0:T(8,128)(2,1)S(1)} %negate_convert_fusion.2) | copy-start | bytes 6291460
  64.8 1.0 copy-start.6
  64.8 5.0 %copy-start.2 = (bf16[512,1024]{1,0:T(8,128)(2,1)S(1)}, bf16[512,1024]{1,0:T(8,128)(2,1)}, u32[]{:S(2)}) copy-start(bf16[512,1024]{1,0:T(8,128)(2,1)} %copy-done.1) | copy-start | bytes 3145732
  66.9 6.1 %collective-permute-start.10 = (bf16[520,512]{1,0:T(8,128)(2,1)}, bf16[520,512]{1,0:T(8,128)(2,1)}, u32[]{:S(2)}, u32[]{:S(2)}) collective-permute-start(bf16[520,512]{1,0:T(8,128)(2,1)} %maximum_maximum_fusion.1), channel_id=1, source_target_pairs={{4,2},{5,3},{12,10},{13,11},{20,18},{21,19},{28,26},{29,27}} | collective-permute-start | bytes 1597448 | tf_op jit(solution)/shard_map/ppermute | solution.py:35
  68.4 16.6 %collective-permute-start.9 = (bf16[520,512]{1,0:T(8,128)(2,1)}, bf16[520,512]{1,0:T(8,128)(2,1)}, u32[]{:S(2)}, u32[]{:S(2)}) collective-permute-start(bf16[520,512]{1,0:T(8,128)(2,1)} %maximum_maximum_fusion.1), channel_id=1, source_target_pairs={{4,0},{5,1},{12,8},{13,9},{20,16},{21,17},{28,24},{29,25}} | collective-permute-start | bytes 1597448 | tf_op jit(solution)/shard_map/ppermute | solution.py:35
  72.9 14.6 %copy-start.8 = (bf16[512,1024]{1,0:T(8,128)(2,1)}, bf16[512,1024]{1,0:T(8,128)(2,1)S(1)}, u32[]{:S(2)}) copy-start(bf16[512,1024]{1,0:T(8,128)(2,1)S(1)} %get-tuple-element.7) | copy-start | bytes 3145732
  73.0 14.6 %copy-start.10 = (bf16[512,1024]{1,0:T(8,128)(2,1)}, bf16[512,1024]{1,0:T(8,128)(2,1)S(1)}, u32[]{:S(2)}) copy-start(bf16[512,1024]{1,0:T(8,128)(2,1)S(1)} %get-tuple-element.8) | copy-start | bytes 3145732
  86.0 5.2 %collective-permute-start.11 = (bf16[1,520,512]{2,1,0:T(8,128)(2,1)S(1)}, bf16[1,520,512]{2,1,0:T(8,128)(2,1)S(1)}, u32[]{:S(2)}, u32[]{:S(2)}) collective-permute-start(bf16[1,520,512]{2,1,0:T(8,128)(2,1)S(1)} %select_bitcast_fusion), channel_id=1, source_target_pairs={{0,1},{1,0},{2,3},{3,2},{4,5},{5,4},{6,7},{7,6},{8,9},{9,8},{10,11... | collective-permute-start | bytes 1597448 | tf_op jit(solution)/shard_map/ppermute | solution.py:41
  92.1 1.6 %copy-start.22 = (bf16[1024,1024]{1,0:T(8,128)(2,1)S(1)}, bf16[1024,1024]{1,0:T(8,128)(2,1)}, u32[]{:S(2)}) copy-start(bf16[1024,1024]{1,0:T(8,128)(2,1)} %fusion.22) | copy-start | bytes 6291460
  96.0 2.4 %copy-start.9 = (bf16[512,1024]{1,0:T(8,128)(2,1)S(1)}, bf16[512,1024]{1,0:T(8,128)(2,1)}, u32[]{:S(2)}) copy-start(bf16[512,1024]{1,0:T(8,128)(2,1)} %copy-done.8) | copy-start | bytes 3145732
  96.0 2.4 %copy-start.11 = (bf16[512,1024]{1,0:T(8,128)(2,1)S(1)}, bf16[512,1024]{1,0:T(8,128)(2,1)}, u32[]{:S(2)}) copy-start(bf16[512,1024]{1,0:T(8,128)(2,1)} %copy-done.10) | copy-start | bytes 3145732
  98.5 2.6 %copy-start.15 = (bf16[1024,1024]{1,0:T(8,128)(2,1)S(1)}, bf16[1024,1024]{1,0:T(8,128)(2,1)}, u32[]{:S(2)}) copy-start(bf16[1024,1024]{1,0:T(8,128)(2,1)} %copy-done.13) | copy-start | bytes 6291460
  101.1 6.4 %copy-start.5 = (bf16[512,1024]{1,0:T(8,128)(2,1)S(1)}, bf16[512,1024]{1,0:T(8,128)(2,1)}, u32[]{:S(2)}) copy-start(bf16[512,1024]{1,0:T(8,128)(2,1)} %copy-done.4) | copy-start | bytes 3145732
  101.1 6.4 %copy-start.7 = (bf16[512,1024]{1,0:T(8,128)(2,1)S(1)}, bf16[512,1024]{1,0:T(8,128)(2,1)}, u32[]{:S(2)}) copy-start(bf16[512,1024]{1,0:T(8,128)(2,1)} %copy-done.6) | copy-start | bytes 3145732
  101.1 6.4 %copy-start.21 = (f32[512,1024]{1,0:T(8,128)S(1)}, f32[512,1024]{1,0:T(8,128)}, u32[]{:S(2)}) copy-start(f32[512,1024]{1,0:T(8,128)} %copy-done.19) | copy-start | bytes 6291460
  103.6 8.4 %collective-permute-start.14 = (bf16[4,1024]{1,0:T(4,128)(2,1)S(1)}, bf16[4,1024]{1,0:T(4,128)(2,1)S(1)}, u32[]{:S(2)}, u32[]{:S(2)}) collective-permute-start(bf16[4,1024]{1,0:T(4,128)(2,1)S(1)} %pad_maximum_fusion.6), channel_id=1, source_target_pairs={{0,6},{1,7},{8,14},{9,15},{16,22},{17,23},{24,30},{25,31}} | collective-permute-start | bytes 24584 | tf_op jit(solution)/shard_map/ppermute | solution.py:35
  104.9 7.1 %collective-permute-start.13 = (bf16[4,1024]{1,0:T(4,128)(2,1)S(1)}, bf16[4,1024]{1,0:T(4,128)(2,1)S(1)}, u32[]{:S(2)}, u32[]{:S(2)}) collective-permute-start(bf16[4,1024]{1,0:T(4,128)(2,1)S(1)} %pad_maximum_fusion.6), channel_id=1, source_target_pairs={{0,4},{1,5},{8,12},{9,13},{16,20},{17,21},{24,28},{25,29}} | collective-permute-start | bytes 24584 | tf_op jit(solution)/shard_map/ppermute | solution.py:35
  106.2 5.8 %collective-permute-start.12 = (bf16[4,1024]{1,0:T(4,128)(2,1)S(1)}, bf16[4,1024]{1,0:T(4,128)(2,1)S(1)}, u32[]{:S(2)}, u32[]{:S(2)}) collective-permute-start(bf16[4,1024]{1,0:T(4,128)(2,1)S(1)} %pad_maximum_fusion.6), channel_id=1, source_target_pairs={{0,2},{1,3},{8,10},{9,11},{16,18},{17,19},{24,26},{25,27}} | collective-permute-start | bytes 24584 | tf_op jit(solution)/shard_map/ppermute | solution.py:35
  107.5 2.6 %copy-start.17 = (bf16[1024,1024]{1,0:T(8,128)(2,1)S(1)}, bf16[1024,1024]{1,0:T(8,128)(2,1)}, u32[]{:S(2)}) copy-start(bf16[1024,1024]{1,0:T(8,128)(2,1)} %copy-done.16) | copy-start | bytes 6291460

commit v2 on v0

v2 whole, which is shorter than its diff:
```python
import functools

import jax
import jax.numpy as jnp
from jax import lax
from jax.experimental import pallas as pl
from jax.experimental.pallas import tpu as pltpu
from jax.sharding import PartitionSpec as P

TB = 4
SLOTS = 2
SPARE = 16
TILE = 128

CONTRACT_FIRST = (((0,), (0,)), ((), ()))
BF16 = jnp.bfloat16
F32 = jnp.float32

ANY = pl.BlockSpec(memory_space=pl.ANY)
VMEM = pl.BlockSpec(memory_space=pltpu.VMEM)
SMEM = pl.BlockSpec(memory_space=pltpu.SMEM)
PARAMS = pltpu.CompilerParams(vmem_limit_bytes=36 << 20)


def mm(a, b):
    return jnp.dot(a, b, preferred_element_type=F32)


def mm_t(a, b):
    return lax.dot_general(a, b, CONTRACT_FIRST, preferred_element_type=F32)


def iotas(size):
    r = lax.broadcasted_iota(jnp.int32, (size, size), 0)
    c = lax.broadcasted_iota(jnp.int32, (size, size), 1)
    return r, c


def load_rows(target, pieces, start, sems):
    n = target.shape[0]
    if len(pieces) == 1:
        copies = [pltpu.make_async_copy(pieces[0], target, sems.at[0])]
    else:
        rows = pieces[0].shape[0]
        other = n - rows - start
        copies = [
            pltpu.make_async_copy(pieces[0], target.at[pl.ds(start, rows)], sems.at[0]),
            pltpu.make_async_copy(pieces[1], target.at[pl.ds(other, rows)], sems.at[1]),
        ]
    for copy in copies:
        copy.start()
    return copies


def couple(target, lower, factor):
    n = factor.shape[0]
    half = n // 2
    target[:, :half] = mm(lower[...], factor[:, :half]).astype(BF16)
    target[:, half:] = mm(lower[:, half:], factor[half:, half:]).astype(BF16)


def tile_diag(tile):
    r, c = iotas(TILE)
    return jnp.sum(jnp.where(r == c, tile.astype(F32), 0.0), axis=0, keepdims=True)


def pack(packet, cov, start, passenger, paired):
    rows, n = cov.shape
    row = lax.broadcasted_iota(jnp.int32, (SPARE, n if not paired else rows), 0)
    if not paired:
        packet[:rows, :] = cov[...]
        packet[rows:, :] = jnp.where(row == 0, passenger, 0.0).astype(BF16)
        return
    other = n - rows - start
    r, c = iotas(TILE)
    for i in range(0, rows, TILE):
        for j in range(0, rows, TILE):
            mine = cov[i : i + TILE, pl.ds(pl.multiple_of(start + j, TILE), TILE)]
            cross = cov[i : i + TILE, pl.ds(pl.multiple_of(other + j, TILE), TILE)]
            if j > i:
                tile = mine
            elif j < i:
                tile = cross
            else:
                tile = jnp.where(c >= r, mine.astype(F32), cross.astype(F32)).astype(BF16)
                dx = tile_diag(cross)
                spare = jnp.where(row[:, :TILE] == 0, dx, 0.0)
                for k in range(n // rows):
                    at = k * rows + i
                    spare = jnp.where(
                        row[:, :TILE] == k + 1, passenger[:, at : at + TILE], spare
                    )
                packet[rows:, i : i + TILE] = spare.astype(BF16)
            packet[i : i + TILE, j : j + TILE] = tile


def unpack(full, diag, packets, start, paired):
    n = full.shape[0]
    if not paired:
        (packet,) = packets
        rows = packet.shape[1] - SPARE
        for k in range(packet.shape[0]):
            full[k * rows : (k + 1) * rows, :] = packet[k, :rows, :]
        for i in range(0, n, TILE):
            diag[:, i : i + TILE] = tile_diag(full[i : i + TILE, i : i + TILE])
        return packet[0, rows:, :].astype(F32)[0:1]
    rows = packets[0].shape[0] - SPARE
    base = (start, n - rows - start)
    r, c = iotas(TILE)

    def put(at_row, i, at_col, j, tile):
        full[
            pl.ds(pl.multiple_of(at_row + i, TILE), TILE),
            pl.ds(pl.multiple_of(at_col + j, TILE), TILE),
        ] = tile

    spare = packets[0][rows:, :].astype(F32)
    for mine, yours in ((0, 1), (1, 0)):
        for i in range(0, rows, TILE):
            for j in range(0, rows, TILE):
                tile = packets[mine][i : i + TILE, j : j + TILE]
                flip = tile.T
                if j > i:
                    put(base[mine], i, base[mine], j, tile)
                    put(base[mine], j, base[mine], i, flip)
                elif j < i:
                    put(base[mine], i, base[yours], j, tile)
                    put(base[yours], j, base[mine], i, flip)
                else:
                    tile = tile.astype(F32)
                    flip = flip.astype(F32)
                    theirs = packets[yours][i : i + TILE, i : i + TILE].T.astype(F32)
                    own = jnp.where(c >= r, tile, flip)
                    put(base[mine], i, base[mine], i, own.astype(BF16))
                    dx = spare[0:1, i : i + TILE]
                    cross = jnp.where(c < r, tile, jnp.where(c > r, theirs, dx))
                    put(base[mine], i, base[yours], i, cross.astype(BF16))
                    diag[:, pl.ds(pl.multiple_of(base[mine] + i, TILE), TILE)] = tile_diag(own)
    return jnp.concatenate([spare[k + 1 : k + 2] for k in range(n // rows)], 1)


def first_kernel(pieces, paired, ids, *refs):
    factors, lowers = refs[:pieces], refs[pieces : 2 * pieces]
    coupling, packet, cov, factor, lower, total, sems = refs[2 * pieces :]
    rows = cov.shape[0]
    start = pl.multiple_of(ids[0], rows)
    block = ids[1]
    copies = load_rows(factor, factors, start, sems.at[0])
    copies += load_rows(lower, lowers, start, sems.at[1])
    for copy in copies:
        copy.wait()
    couple(coupling, lower, factor)

    @pl.when(block == TB - 1)
    def _():
        own = pl.ds(start, rows)
        total[...] = mm_t(factor[:, own], factor[...])
        cov[...] = (total[...] + mm_t(coupling[:, own], coupling[...])).astype(BF16)
        pack(packet, cov, start, jnp.zeros((1, factor.shape[1]), F32), paired)


def gram_kernel(pieces, ids, *refs):
    factors = refs[:pieces]
    coupling, cov, gram, off_out, cov_out, factor, off, sems, out_sems = refs[pieces:]
    rows = cov.shape[0]
    start = pl.multiple_of(ids[0], rows)
    block = ids[1]
    copies = load_rows(factor, factors, start, sems.at[0])
    for copy in copies:
        copy.wait()
    gram[...] = mm_t(factor[:, pl.ds(start, rows)], factor[...])

    @pl.when(block == TB - 1)
    def _():
        off[...] = -coupling[pl.ds(start, rows), :]
        one = pltpu.make_async_copy(off, off_out, out_sems.at[0])
        two = pltpu.make_async_copy(cov, cov_out, out_sems.at[1])
        one.start()
        two.start()
        one.wait()
        two.wait()


def second_kernel(pieces, paired, ids, *refs):
    packets = refs[:pieces]
    coupling, gram, packet, off, cov, full, diag = refs[pieces:]
    rows = cov.shape[0]
    start = pl.multiple_of(ids[0], rows)
    block = ids[1]

    @pl.when(block == TB - 2)
    def _():
        unpack(full, diag, packets, start, paired)
        off[...] = (-mm(full[...], coupling[...])).astype(BF16)
        cov[...] = (gram[...] - mm_t(coupling[:, pl.ds(start, rows)], off[...])).astype(BF16)
        pack(packet, cov, start, diag[...], paired)


def ready_kernel(pieces, ids, *refs):
    factors, heard_factors = refs[:pieces], refs[pieces : 2 * pieces]
    heard_lowers = refs[2 * pieces : 3 * pieces]
    (coupling, off, cov, _, _, coupling_1, gram_1, coupling_0, diag_0, off_out, cov_out,
     factor, heard, lower, sems, out_sems) = refs[3 * pieces :]
    rows = cov.shape[0]
    start = pl.multiple_of(ids[0], rows)
    block = ids[1]

    @pl.when(block == TB - 2)
    def _():
        one = pltpu.make_async_copy(off.at[pl.ds(start, rows)], off_out, out_sems.at[0])
        two = pltpu.make_async_copy(cov, cov_out, out_sems.at[1])
        one.start()
        two.start()
        one.wait()
        two.wait()

    @pl.when(block < 2)
    def _():
        copies = load_rows(factor, factors, start, sems.at[0])
        copies += load_rows(heard, heard_factors, start, sems.at[1])
        copies += load_rows(lower, heard_lowers, start, sems.at[2])
        for copy in copies:
            copy.wait()

        def finish(factor_1, factor_0):
            gram_1[...] = mm_t(factor_1[...], factor_1[...])
            diag_0[...] = jnp.sum(
                jnp.square(factor_0[...].astype(F32)), axis=0, keepdims=True
            )

        @pl.when(block == 0)
        def _():
            couple(coupling_1, lower, heard)
            coupling_0[...] = coupling[...]
            finish(heard, factor)

        @pl.when(block == 1)
        def _():
            couple(coupling_0, lower, heard)
            coupling_1[...] = coupling[...]
            finish(factor, heard)


def third_kernel(pieces, paired, ids, *refs):
    packets = refs[:pieces]
    (coupling_1, gram_1, coupling_0, diag_0, off_0, off_1, cov_1, variances,
     full, diag) = refs[pieces:]
    n = full.shape[0]
    block = ids[1]
    start = ids[0]

    @pl.when(block < 2)
    def _():
        var_3 = unpack(full, diag, packets, start, paired)
        var_2 = diag[...]
        off_1[...] = (-mm(full[...], coupling_1[...])).astype(BF16)
        cov_1[...] = (gram_1[...] - mm_t(coupling_1[...], off_1[...])).astype(BF16)
        off_0[...] = (-mm(cov_1[...], coupling_0[...])).astype(BF16)
        for i in range(0, n, TILE):
            diag[:, i : i + TILE] = tile_diag(cov_1[i : i + TILE, i : i + TILE])
        product = coupling_0[...].astype(F32) * off_0[...].astype(F32)
        var_0 = diag_0[...] - jnp.sum(product, axis=0, keepdims=True)
        row = lax.broadcasted_iota(jnp.int32, variances.shape, 0)
        merged = jnp.where(row == 0, var_0, jnp.where(row == 1, diag[...], 0.0))
        merged = jnp.where(row == 2, var_2, jnp.where(row == 3, var_3, merged))
        variances[...] = merged.astype(BF16)


def last_kernel(ids, coupling_0, gram, off_0, off_1, cov_1, _, __, off_out, cov_out, cov, sems):
    rows = cov.shape[0]
    start = pl.multiple_of(ids[0], rows)
    block = ids[1]
    own = pl.ds(start, rows)

    @pl.when(block == 1)
    def _():
        one = pltpu.make_async_copy(off_1.at[own], off_out, sems.at[0])
        two = pltpu.make_async_copy(cov_1.at[own], cov_out, sems.at[1])
        one.start()
        two.start()
        one.wait()
        two.wait()

    @pl.when(block == 0)
    def _():
        one = pltpu.make_async_copy(off_0.at[own], off_out, sems.at[0])
        one.start()
        cov[...] = (gram[...] - mm_t(coupling_0[:, own], off_0[...])).astype(BF16)
        two = pltpu.make_async_copy(cov, cov_out, sems.at[1])
        two.start()
        one.wait()
        two.wait()


def deliver_kernel(ids, choice, mine, heard, out):
    block = ids[1]
    values = jnp.where(block < 2, mine[...].astype(F32), heard[...].astype(F32))
    for slot in range(SLOTS):
        line = jnp.zeros((1, out.shape[1]), F32)
        for t in range(TB):
            line += jnp.where(choice[slot * TB + t] == 1, values[t : t + 1], 0.0)
        out[slot : slot + 1, :] = line


def vmem(*arrays):
    return [pltpu.with_memory_space_constraint(a, pltpu.VMEM) for a in arrays]


def shards(linv, sub, owner):
    group = lax.axis_size("tm") // TB
    rows, n = linv.shape
    half = n // 2
    paired = group == 2
    dev = lax.axis_index("tm")
    member = dev % group
    block = dev // group
    ids = jnp.stack([member * rows, block]).astype(jnp.int32)

    def block_to_block(values, routes, members=range(group)):
        pairs = [(s * group + i, t * group + i) for s, t in routes for i in members]
        return lax.ppermute(values, "tm", pairs)

    def peer(piece, step=1):
        return lax.ppermute(piece, "tm", [(i, i ^ step) for i in range(TB * group)])

    def pieces_of(piece):
        if paired:
            return [piece, peer(piece)]
        step = 1
        while step < group:
            other = peer(piece, step)
            upper = (member // step) % 2 == 1
            piece = jnp.concatenate(
                [jnp.where(upper, other, piece), jnp.where(upper, piece, other)], 0
            )
            step *= 2
        return [piece]

    def packets_of(packet):
        return pieces_of(packet) if paired else pieces_of(packet[None])

    def after(values, *others):
        return lax.optimization_barrier((values, *others))[0]

    pieces = 2 if paired else 1
    packet_shape = (rows + SPARE, rows) if paired else (rows + SPARE, n)
    gathered = packet_shape if paired else (group, *packet_shape)
    whole = pltpu.VMEM((n, n), BF16)
    part = pltpu.VMEM((rows, n), BF16)
    hbm = jax.ShapeDtypeStruct((rows, n), BF16)
    square = pltpu.VMEM((n, n), BF16)

    factors = pieces_of(linv)
    lowers = pieces_of(sub)
    swap = [(1, 0), (0, 1)]
    heard_lower = block_to_block(sub, swap)

    coupling, packet, cov_3 = pl.pallas_call(
        functools.partial(first_kernel, pieces, paired),
        out_shape=(whole, pltpu.VMEM(packet_shape, BF16), part),
        in_specs=[SMEM] + [ANY] * (2 * pieces),
        out_specs=(VMEM, VMEM, VMEM),
        scratch_shapes=[
            square,
            square,
            pltpu.VMEM((rows, n), F32),
            pltpu.SemaphoreType.DMA((2, 2)),
        ],
        compiler_params=PARAMS,
        name="first",
    )(ids, *factors, *lowers)

    packet_2 = block_to_block(packet, [(3, 2)])
    late = after(linv, packet)
    heard_left = block_to_block(late[:, :half], swap)
    heard_right = block_to_block(late[:, half:], swap, range(group // 2, group))

    gram, off_rows, cov_rows = pl.pallas_call(
        functools.partial(gram_kernel, pieces),
        out_shape=(pltpu.VMEM((rows, n), F32), hbm, hbm),
        in_specs=[SMEM] + [ANY] * pieces + [VMEM, VMEM],
        out_specs=(VMEM, ANY, ANY),
        scratch_shapes=[
            square,
            pltpu.VMEM((rows, n), BF16),
            pltpu.SemaphoreType.DMA((1, 2)),
            pltpu.SemaphoreType.DMA((2,)),
        ],
        compiler_params=PARAMS,
        name="gram",
    )(ids, *factors, *vmem(coupling, cov_3))

    packet, off_2, cov_2 = pl.pallas_call(
        functools.partial(second_kernel, pieces, paired),
        out_shape=(pltpu.VMEM(packet_shape, BF16), whole, part),
        in_specs=[SMEM] + [VMEM] * (pieces + 2),
        out_specs=(VMEM, VMEM, VMEM),
        scratch_shapes=[square, pltpu.VMEM((1, n), F32)],
        compiler_params=PARAMS,
        name="second",
    )(ids, *vmem(*packets_of(packet_2), coupling, gram))

    packet_0 = block_to_block(packet, [(2, 0)])
    packet_1 = block_to_block(packet, [(2, 1)])

    heard_factor = jnp.concatenate([after(heard_left, packet), after(heard_right, packet)], 1)
    heard_factors = pieces_of(heard_factor)
    heard_lowers = pieces_of(after(heard_lower, packet))
    coupling_1, gram_1, coupling_0, diag_0, off_rows, cov_rows = pl.pallas_call(
        functools.partial(ready_kernel, pieces),
        out_shape=(
            whole,
            pltpu.VMEM((n, n), F32),
            whole,
            pltpu.VMEM((1, n), F32),
            hbm,
            hbm,
        ),
        in_specs=[SMEM] + [ANY] * (3 * pieces) + [VMEM] * 3 + [ANY, ANY],
        out_specs=(VMEM, VMEM, VMEM, VMEM, ANY, ANY),
        scratch_shapes=[
            square,
            square,
            square,
            pltpu.SemaphoreType.DMA((3, 2)),
            pltpu.SemaphoreType.DMA((2,)),
        ],
        input_output_aliases={3 * pieces + 4: 4, 3 * pieces + 5: 5},
        compiler_params=PARAMS,
        name="ready",
    )(
        ids,
        *factors,
        *heard_factors,
        *heard_lowers,
        *vmem(coupling, off_2, cov_2),
        off_rows,
        cov_rows,
    )

    carried = jnp.where(block == 0, packet_0, packet_1)
    off_0, off_1, cov_1, variances = pl.pallas_call(
        functools.partial(third_kernel, pieces, paired),
        out_shape=(whole, whole, whole, pltpu.VMEM((SPARE, n), BF16)),
        in_specs=[SMEM] + [VMEM] * (pieces + 4),
        out_specs=(VMEM, VMEM, VMEM, VMEM),
        scratch_shapes=[square, pltpu.VMEM((1, n), F32)],
        compiler_params=PARAMS,
        name="third",
    )(ids, *vmem(*packets_of(carried), coupling_1, gram_1, coupling_0, diag_0))

    heard = block_to_block(variances, [(0, 2), (1, 3)])

    off_rows, cov_rows = pl.pallas_call(
        last_kernel,
        out_shape=(hbm, hbm),
        in_specs=[SMEM] + [VMEM] * 5 + [ANY, ANY],
        out_specs=(ANY, ANY),
        scratch_shapes=[pltpu.VMEM((rows, n), BF16), pltpu.SemaphoreType.DMA((2,))],
        input_output_aliases={6: 0, 7: 1},
        compiler_params=PARAMS,
        name="last",
    )(ids, *vmem(coupling_0, gram, off_0, off_1, cov_1), off_rows, cov_rows)

    positions = lax.broadcasted_iota(jnp.int32, (TB, TB), 1)
    current = lax.broadcasted_iota(jnp.int32, (TB, TB), 0)
    same_owner = owner[:, None] == owner[None, :]
    slot_rank = jnp.sum(jnp.where(same_owner & (positions < current), 1, 0), axis=1)
    slot_iota = lax.broadcasted_iota(jnp.int32, (SLOTS, TB), 0)
    choice = (owner[None, :] == dev) & (slot_rank[None, :] == slot_iota)
    owned_var = pl.pallas_call(
        deliver_kernel,
        out_shape=jax.ShapeDtypeStruct((SLOTS, n), F32),
        in_specs=[SMEM, SMEM, VMEM, VMEM],
        out_specs=VMEM,
        compiler_params=PARAMS,
        name="deliver",
    )(ids, choice.astype(jnp.int32).reshape(SLOTS * TB), variances, heard)
    return (cov_rows, off_rows, owned_var)


def solution(mesh):
    return jax.shard_map(
        shards,
        mesh=mesh,
        in_specs=(P(("cfg", "tm"), None), P(("cfg", "tm"), None), P("cfg")),
        out_specs=(P(("cfg", "tm"), None), P(("cfg", "tm"), None), P(("cfg", "tm"), None)),
        check_vma=False,
    )
```

time: 135 us -> 99.3 us (0.74)
  waiting for transfers between devices: 91.9 us -> 29.7 us
  Pallas kernels: 0 us -> 26.7 us
  matrix products: 19.6 us -> 0 us
  local copies, waits for them, and re-layouts: 2.03 us -> 21 us
  starting transfers between devices: 5.27 us -> 18.9 us
  blocking collectives: 10 us -> 0 us
  other arithmetic: 4.45 us -> 1.47 us
    ppermute x8 -> x13, waiting for transfers between devices: 91.9 us -> 29.7 us  [the longest x7 23.7 us: block_to_block(): return lax.ppermute(values, 'tm', pairs)]
    pallas_call x0 -> x7, Pallas kernels: none -> 26.7 us  [the longest x1 8.1 us: shards(): pl.pallas_call(functools.partial(third_kernel, pieces, paired), out_shape...]
    dot_general x11 -> x0, matrix products: 19.6 us -> none  [the longest x4 7.15 us: shards(): jnp.dot(carried, coupling_full, preferred_element_type=jnp.float32)]
    unnamed x15 -> x43, local copies, waits for them, and re-layouts: 1.93 us -> 19.9 us
    ppermute x8 -> x13, starting transfers between devices: 5.27 us -> 18.9 us  [the longest x7 12.4 us: block_to_block(): return lax.ppermute(values, 'tm', pairs)]
    all_gather x1 -> x0, blocking collectives: 10 us -> none  [shards(): lax.all_gather(var_rows[None, :], 'tm', axis=0, tiled=True)]
    select_n x5 -> x1, other arithmetic: 4.05 us -> 1.2 us  [shards(): carried = jnp.where(block == 0, packet_0, packet_1)]
  transfers between devices with their start and end apart: 8 -> 13, of which waited for: 7 -> 5; matrix products, arithmetic and copies ran while one was open for 3% -> 3% of each run, Pallas kernels for 0% -> 14%
where the time goes in v2:
time: 99.3 us; the launch traced here: 98.7 us
  waiting for transfers between devices  29.7 us (30%)
  Pallas kernels  26.7 us (27%)
  local copies, waits for them, and re-layouts  21 us (21%)
  starting transfers between devices  18.9 us (19%)
  other arithmetic  1.47 us (1%)
    ppermute x7, waiting for transfers between devices, block_to_block(): return lax.ppermute(values, 'tm', pairs)  23.7 us
    unnamed x43, local copies, waits for them, and re-layouts  19.9 us
    ppermute x7, starting transfers between devices, block_to_block(): return lax.ppermute(values, 'tm', pairs)  12.4 us
    pallas_call x1, Pallas kernels, shards(): pl.pallas_call(functools.partial(third_kernel, pieces, paired), out_shape...  8.1 us
    pallas_call x1, Pallas kernels, shards(): pl.pallas_call(functools.partial(ready_kernel, pieces), out_shape=(whole,...  7.29 us
    ppermute x6, starting transfers between devices, peer(): return lax.ppermute(piece, 'tm', [(i, i ^ step) for i in range(TB * group)])  6.56 us
    ppermute x6, waiting for transfers between devices, peer(): return lax.ppermute(piece, 'tm', [(i, i ^ step) for i in range(TB * group)])  5.99 us
    pallas_call x1, Pallas kernels, shards(): pl.pallas_call(functools.partial(first_kernel, pieces, paired), out_shape...  3.74 us
  transfers between devices with their start and end apart: 13, of which 5 were waited for; matrix products, arithmetic and copies ran while one was open for 3% of the time, Pallas kernels for 14%

profile of v2, /device:TPU:0, one launch (start us, length us, event | category | flops | bytes accessed | tf_op | source)
XLA Modules:
  0.0 98.7 jit_solution(1854599528832268589)
XLA Ops:
  0.6 0.6 collective-permute-start
  1.2 0.1 collective-permute-start.1
  1.3 0.1 pad_add_fusion.ids
  1.3 2.3 %collective-permute-done.refs_1_ = bf16[512,1024]{1,0:T(8,128)(2,1)S(1)} collective-permute-done((bf16[512,1024]{1,0:T(8,128)(2,1)}, bf16[512,1024]{1,0:T(8,128)(2,1)S(1)}, u32[]{:S(2)}, u32[]{:S(2)}) %collective-permute-start) | collective-permute-done | bytes 1048608 | tf_op jit(solution)/shard_map/ppermute | solution.py:324
  3.7 1.5 %collective-permute-done.1.refs_3_ = bf16[512,1024]{1,0:T(8,128)(2,1)S(1)} collective-permute-done((bf16[512,1024]{1,0:T(8,128)(2,1)}, bf16[512,1024]{1,0:T(8,128)(2,1)S(1)}, u32[]{:S(2)}, u32[]{:S(2)}) %collective-permute-start.1) | collective-permute-done | bytes 1048608 | tf_op jit(solution)/shard_map/ppermute | solution.py:324
  5.2 1.0 copy-done.16
  6.2 1.2 %copy-done = bf16[512,1024]{1,0:T(8,128)(2,1)S(1)} copy-done((bf16[512,1024]{1,0:T(8,128)(2,1)S(1)}, bf16[512,1024]{1,0:T(8,128)(2,1)}, u32[]{:S(2)}) %copy-start) | copy-done | bytes 1048600
  7.4 1.2 %copy-done.17 = bf16[512,1024]{1,0:T(8,128)(2,1)S(1)} copy-done((bf16[512,1024]{1,0:T(8,128)(2,1)S(1)}, bf16[512,1024]{1,0:T(8,128)(2,1)}, u32[]{:S(2)}) %copy-start.17) | copy-done | bytes 1048600
  8.6 3.7 %first.1 = (bf16[1024,1024]{1,0:T(8,128)(2,1)S(1)}, bf16[528,512]{1,0:T(8,128)(2,1)S(1)}, bf16[512,1024]{1,0:T(8,128)(2,1)S(1)}) custom-call(s32[2]{0:T(128)S(1)} %pad_add_fusion.ids, bf16[512,1024]{1,0:T(8,128)(2,1)S(1)} %copy-done, bf16[512,1024]{1,0:T(8,128)(2,1)S(1)} %collective-permute-done.refs_1_, bf16[512,1024]{1,0:T(8,128)(2,1)} %refs_2_.1, ...), custom_call_target="tpu_custom_call" | custom-call | tf_op jit(solution)/shard_map/first/pallas_call | solution.py:358
  12.4 0.7 collective-permute-start.3
  13.1 4.8 %collective-permute-start.7 = (bf16[512,1024]{1,0:T(8,128)(2,1)}, bf16[512,1024]{1,0:T(8,128)(2,1)}, u32[]{:S(2)}, u32[]{:S(2)}) collective-permute-start(bf16[512,1024]{1,0:T(8,128)(2,1)} %refs_2_.1), channel_id=1, source_target_pairs={{2,0},{3,1},{0,2},{1,3},{10,8},{11,9},{8,10},{9,11},{18,16},{19,17... | collective-permute-start | bytes 3145736 | tf_op jit(solution)/shard_map/ppermute | solution.py:321
  17.8 0.0 collective-permute-done.3.refs_0_
  17.8 0.1 collective-permute-start.4
  17.9 0.1 fusion.1
  18.0 2.0 %collective-permute-start.2 = (bf16[512,512]{1,0:T(8,128)(2,1)S(1)}, bf16[512,512]{1,0:T(8,128)(2,1)S(1)}, u32[]{:S(2)}, u32[]{:S(2)}) collective-permute-start(bf16[512,512]{1,0:T(8,128)(2,1)S(1)} %get-tuple-element.54), channel_id=1, source_target_pairs={{2,0},{3,1},{0,2},{1,3},{10,8},{11,9},{8,10},{9,11},{18,16},{19,17... | collective-permute-start | bytes 1572872 | tf_op jit(solution)/shard_map/ppermute | solution.py:321
  20.0 0.7 collective-permute-start.5
  20.8 0.0 copy-done.2
  20.8 2.0 %gram.1 = (f32[512,1024]{1,0:T(8,128)S(1)}, bf16[512,1024]{1,0:T(8,128)(2,1)}, bf16[512,1024]{1,0:T(8,128)(2,1)}) custom-call(s32[2]{0:T(128)S(1)} %pad_add_fusion.ids, bf16[512,1024]{1,0:T(8,128)(2,1)S(1)} %copy-done, bf16[512,1024]{1,0:T(8,128)(2,1)S(1)} %collective-permute-done.refs_1_, bf16[1024,1024]{1,0:T(8,128)(2,1)S(1)} %get-tuple-element.30.refs_2_.refs_6_, ...), custom_call_target="tpu_custom_call" | custom-call | tf_op jit(solution)/shard_map/gram/pallas_call | solution.py:378
  22.8 0.0 copy-start.4
  22.8 0.0 collective-permute-done.4.refs_1_
  22.8 1.5 %second.1 = (bf16[528,512]{1,0:T(8,128)(2,1)}, bf16[1024,1024]{1,0:T(8,128)(2,1)S(1)}, bf16[512,1024]{1,0:T(8,128)(2,1)S(1)}) custom-call(s32[2]{0:T(128)S(1)} %pad_add_fusion.ids, bf16[528,512]{1,0:T(8,128)(2,1)S(1)} %collective-permute-done.3.refs_0_, bf16[528,512]{1,0:T(8,128)(2,1)S(1)} %collective-permute-done.4.refs_1_, ...), custom_call_target="tpu_custom_call" | custom-call | tf_op jit(solution)/shard_map/second/pallas_call | solution.py:393
  24.4 0.0 copy-done.4
  24.4 1.3 %copy-done.14 = bf16[1024,1024]{1,0:T(8,128)(2,1)} copy-done((bf16[1024,1024]{1,0:T(8,128)(2,1)}, bf16[1024,1024]{1,0:T(8,128)(2,1)S(1)}, u32[]{:S(2)}) %copy-start.14) | copy-done | bytes 2097176
  25.7 1.0 copy-done.18
  26.7 1.4 %collective-permute-start.9 = (bf16[528,512]{1,0:T(8,128)(2,1)}, bf16[528,512]{1,0:T(8,128)(2,1)}, u32[]{:S(2)}, u32[]{:S(2)}) collective-permute-start(bf16[528,512]{1,0:T(8,128)(2,1)} %get-tuple-element.33), channel_id=1, source_target_pairs={{4,0},{5,1},{12,8},{13,9},{20,16},{21,17},{28,24},{29,25}} | collective-permute-start | bytes 1622024 | tf_op jit(solution)/shard_map/ppermute | solution.py:321
  28.1 1.5 %collective-permute-start.10 = (bf16[528,512]{1,0:T(8,128)(2,1)}, bf16[528,512]{1,0:T(8,128)(2,1)}, u32[]{:S(2)}, u32[]{:S(2)}) collective-permute-start(bf16[528,512]{1,0:T(8,128)(2,1)} %get-tuple-element.33), channel_id=1, source_target_pairs={{4,2},{5,3},{12,10},{13,11},{20,18},{21,19},{28,26},{29,27}} | collective-permute-start | bytes 1622024 | tf_op jit(solution)/shard_map/ppermute | solution.py:321
  29.5 23.7 %collective-permute-done.2 = bf16[512,512]{1,0:T(8,128)(2,1)S(1)} collective-permute-done((bf16[512,512]{1,0:T(8,128)(2,1)S(1)}, bf16[512,512]{1,0:T(8,128)(2,1)S(1)}, u32[]{:S(2)}, u32[]{:S(2)}) %collective-permute-start.2) | collective-permute-done | bytes 524320 | tf_op jit(solution)/shard_map/ppermute | solution.py:321
  53.3 0.0 collective-permute-done.5
  53.3 0.9 constant_dynamic-update-slice_fusion.1
  54.1 0.9 constant_dynamic-update-slice_fusion.refs_2_
  55.0 5.3 %collective-permute-start.6 = (bf16[512,1024]{1,0:T(8,128)(2,1)}, bf16[512,1024]{1,0:T(8,128)(2,1)}, u32[]{:S(2)}, u32[]{:S(2)}) collective-permute-start(bf16[512,1024]{1,0:T(8,128)(2,1)} %constant_dynamic-update-slice_fusion.refs_2_), channel_id=1, source_target_pairs={{0,1},{1,0},{2,3},{3,2},{4,5},{5,4},{6,7},{7,6},{8,9},{9,8},{10,11... | collective-permute-start | bytes 3145736 | tf_op jit(solution)/shard_map/ppermute | solution.py:324
  60.3 0.0 collective-permute-done.7.refs_4_
  60.3 0.0 collective-permute-start.8
  60.3 0.0 collective-permute-done.9
  60.3 0.0 collective-permute-done.10
  60.4 1.2 %broadcast_select_fusion.refs_0_ = bf16[528,512]{1,0:T(8,128)(2,1)S(1)} fusion(bf16[528,512]{1,0:T(8,128)(2,1)} %collective-permute-done.9, bf16[528,512]{1,0:T(8,128)(2,1)} %collective-permute-done.10, pred[]{:T(512)S(6)} %eq.35), kind=kLoop, calls=%fused_computation | loop fusion | flops 270336 | bytes 1622017 | tf_op jit(solution)/shard_map/jit(_where)/select_n | solution.py:441
  61.6 0.6 collective-permute-start.11
  62.1 0.0 copy-done.20
  62.1 0.2 select_reduce_fusion
  62.3 0.6 collective-permute-done.6.refs_3_
  63.0 1.5 %collective-permute-done.8.refs_5_ = bf16[512,1024]{1,0:T(8,128)(2,1)} collective-permute-done((bf16[512,1024]{1,0:T(8,128)(2,1)}, bf16[512,1024]{1,0:T(8,128)(2,1)}, u32[]{:S(2)}, u32[]{:S(2)}) %collective-permute-start.8) | collective-permute-done | bytes 1048608 | tf_op jit(solution)/shard_map/ppermute | solution.py:324
  64.4 0.0 copy-done.1
  64.5 0.0 copy-done.3
  64.5 1.6 %copy-done.15 = bf16[1024,1024]{1,0:T(8,128)(2,1)S(1)} copy-done((bf16[1024,1024]{1,0:T(8,128)(2,1)S(1)}, bf16[1024,1024]{1,0:T(8,128)(2,1)}, u32[]{:S(2)}) %copy-start.15) | copy-done | bytes 2097176
  66.0 1.2 %copy-done.19 = bf16[512,1024]{1,0:T(8,128)(2,1)S(1)} copy-done((bf16[512,1024]{1,0:T(8,128)(2,1)S(1)}, bf16[512,1024]{1,0:T(8,128)(2,1)}, u32[]{:S(2)}) %copy-start.19) | copy-done | bytes 1048600
  67.3 7.3 %ready.1 = (bf16[1024,1024]{1,0:T(8,128)(2,1)S(1)}, f32[1024,1024]{1,0:T(8,128)S(1)}, bf16[1024,1024]{1,0:T(8,128)(2,1)S(1)}, f32[1,1024]{1,0:T(1,128)S(1)}, bf1...) custom-call(s32[2]{0:T(128)S(1)} %pad_add_fusion.ids, ...), custom_call_target="tpu_custom_call", output_to_operand_aliasing={{4}: (10, {}), {5}: (11, {})} | custom-call | tf_op jit(solution)/shard_map/ready/pallas_call | solution.py:409
  74.6 0.0 copy-start.6
  74.6 0.0 collective-permute-done.11.refs_1_
  74.6 0.0 copy-start.5
  74.6 8.1 %third.1 = (bf16[1024,1024]{1,0:T(8,128)(2,1)S(1)}, bf16[1024,1024]{1,0:T(8,128)(2,1)S(1)}, bf16[1024,1024]{1,0:T(8,128)(2,1)S(1)}, bf16[16,1024]{1,0:T(8,128)(2,1)S(1)}) custom-call(s32[2]{0:T(128)S(1)} %pad_add_fusion.ids, bf16[528,512]{1,0:T(8,128)(2,1)S(1)} %broadcast_select_fusion.refs_0_, bf16[528,512]{1,0:T(8,128)(2,1)S(1)} %collective-permute-done.11.refs_1_, ...), custom_call_target="tpu_custom_call" | custom-call | tf_op jit(solution)/shard_map/third/pallas_call | solution.py:442
  82.7 0.0 copy-done.6
  82.7 1.4 %copy-done.8 = bf16[1024,1024]{1,0:T(8,128)(2,1)} copy-done((bf16[1024,1024]{1,0:T(8,128)(2,1)}, bf16[1024,1024]{1,0:T(8,128)(2,1)S(1)}, u32[]{:S(2)}) %copy-start.8) | copy-done | bytes 2097176
  84.1 1.4 %copy-done.10 = bf16[1024,1024]{1,0:T(8,128)(2,1)} copy-done((bf16[1024,1024]{1,0:T(8,128)(2,1)}, bf16[1024,1024]{1,0:T(8,128)(2,1)S(1)}, u32[]{:S(2)}) %copy-start.10) | copy-done | bytes 2097176
  85.5 1.4 %copy-done.12 = bf16[1024,1024]{1,0:T(8,128)(2,1)} copy-done((bf16[1024,1024]{1,0:T(8,128)(2,1)}, bf16[1024,1024]{1,0:T(8,128)(2,1)S(1)}, u32[]{:S(2)}) %copy-start.12) | copy-done | bytes 2097176
  86.9 1.3 %collective-permute-start.12 = (bf16[16,1024]{1,0:T(8,128)(2,1)S(1)}, bf16[16,1024]{1,0:T(8,128)(2,1)S(1)}, u32[]{:S(2)}, u32[]{:S(2)}) collective-permute-start(bf16[16,1024]{1,0:T(8,128)(2,1)S(1)} %get-tuple-element.52.mine), channel_id=1, source_target_pairs={{0,4},{1,5},{2,6},{3,7},{8,12},{9,13},{10,14},{11,15},{16,20},{17,... | collective-permute-start | bytes 98312 | tf_op jit(solution)/shard_map/ppermute | solution.py:321
  88.2 0.1 reshape.19.choice
  88.3 0.0 copy-done.5
  88.3 1.6 %copy-done.7 = bf16[1024,1024]{1,0:T(8,128)(2,1)S(1)} copy-done((bf16[1024,1024]{1,0:T(8,128)(2,1)S(1)}, bf16[1024,1024]{1,0:T(8,128)(2,1)}, u32[]{:S(2)}) %copy-start.7) | copy-done | bytes 2097176
  89.9 1.6 %copy-done.9 = bf16[1024,1024]{1,0:T(8,128)(2,1)S(1)} copy-done((bf16[1024,1024]{1,0:T(8,128)(2,1)S(1)}, bf16[1024,1024]{1,0:T(8,128)(2,1)}, u32[]{:S(2)}) %copy-start.9) | copy-done | bytes 2097176
  91.5 1.6 %copy-done.11 = bf16[1024,1024]{1,0:T(8,128)(2,1)S(1)} copy-done((bf16[1024,1024]{1,0:T(8,128)(2,1)S(1)}, bf16[1024,1024]{1,0:T(8,128)(2,1)}, u32[]{:S(2)}) %copy-start.11) | copy-done | bytes 2097176
  93.0 1.6 %copy-done.13 = bf16[1024,1024]{1,0:T(8,128)(2,1)S(1)} copy-done((bf16[1024,1024]{1,0:T(8,128)(2,1)S(1)}, bf16[1024,1024]{1,0:T(8,128)(2,1)}, u32[]{:S(2)}) %copy-start.13) | copy-done | bytes 2097176
  94.6 2.8 %last.1 = (bf16[512,1024]{1,0:T(8,128)(2,1)}, bf16[512,1024]{1,0:T(8,128)(2,1)}) custom-call(s32[2]{0:T(128)S(1)} %pad_add_fusion.ids, bf16[1024,1024]{1,0:T(8,128)(2,1)S(1)} %copy-done.7, f32[512,1024]{1,0:T(8,128)S(1)} %copy-done.5, bf16[1024,1024]{1,0:T(8,128)(2,1)S(1)} %copy-done.9, ...), custom_call_target="tpu_custom_call", output_to_operand_aliasing={{0}: (6, {}), {1}: (7, {})} | custom-call | tf_op jit(solution)/shard_map/last/pallas_call | solution.py:454
  97.5 0.0 collective-permute-done.12.heard
  97.5 1.2 %deliver.1 = f32[2,1024]{1,0:T(2,128)} custom-call(s32[2]{0:T(128)S(1)} %pad_add_fusion.ids, s32[8]{0:T(128)S(1)} %reshape.19.choice, bf16[16,1024]{1,0:T(8,128)(2,1)S(1)} %get-tuple-element.52.mine, bf16[16,1024]{1,0:T(8,128)(2,1)S(1)} %collective-permute-done.12.heard), custom_call_target="tpu_custom_call" | custom-call | tf_op jit(solution)/shard_map/deliver/pallas_call | solution.py:471
  (20 shorter events, 0.0 us)
Async XLA Ops:
  0.6 3.1 %collective-permute-start = (bf16[512,1024]{1,0:T(8,128)(2,1)}, bf16[512,1024]{1,0:T(8,128)(2,1)S(1)}, u32[]{:S(2)}, u32[]{:S(2)}) collective-permute-start(bf16[512,1024]{1,0:T(8,128)(2,1)} %refs_0_.5), channel_id=1, source_target_pairs={{0,1},{1,0},{2,3},{3,2},{4,5},{5,4},{6,7},{7,6},{8,9},{9,8},{10,11... | collective-permute-start | bytes 3145736 | tf_op jit(solution)/shard_map/ppermute | solution.py:324
  1.2 4.0 %collective-permute-start.1 = (bf16[512,1024]{1,0:T(8,128)(2,1)}, bf16[512,1024]{1,0:T(8,128)(2,1)S(1)}, u32[]{:S(2)}, u32[]{:S(2)}) collective-permute-start(bf16[512,1024]{1,0:T(8,128)(2,1)} %refs_2_.1), channel_id=1, source_target_pairs={{0,1},{1,0},{2,3},{3,2},{4,5},{5,4},{6,7},{7,6},{8,9},{9,8},{10,11... | collective-permute-start | bytes 3145736 | tf_op jit(solution)/shard_map/ppermute | solution.py:324
  3.7 17.1 %copy-start.2 = (bf16[512,1024]{1,0:T(8,128)(2,1)}, bf16[512,1024]{1,0:T(8,128)(2,1)S(1)}, u32[]{:S(2)}) copy-start(bf16[512,1024]{1,0:T(8,128)(2,1)S(1)} %collective-permute-done.refs_1_) | copy-start | bytes 3145732
  5.2 1.0 copy-start.16
  6.2 1.2 %copy-start = (bf16[512,1024]{1,0:T(8,128)(2,1)S(1)}, bf16[512,1024]{1,0:T(8,128)(2,1)}, u32[]{:S(2)}) copy-start(bf16[512,1024]{1,0:T(8,128)(2,1)} %refs_0_.5) | copy-start | bytes 3145732
  7.4 1.2 %copy-start.17 = (bf16[512,1024]{1,0:T(8,128)(2,1)S(1)}, bf16[512,1024]{1,0:T(8,128)(2,1)}, u32[]{:S(2)}) copy-start(bf16[512,1024]{1,0:T(8,128)(2,1)} %copy-done.16) | copy-start | bytes 3145732
  12.4 5.5 %collective-permute-start.3 = (bf16[528,512]{1,0:T(8,128)(2,1)S(1)}, bf16[528,512]{1,0:T(8,128)(2,1)S(1)}, u32[]{:S(2)}, u32[]{:S(2)}) collective-permute-start(bf16[528,512]{1,0:T(8,128)(2,1)S(1)} %get-tuple-element.28), channel_id=1, source_target_pairs={{6,4},{7,5},{14,12},{15,13},{22,20},{23,21},{30,28},{31,29}} | collective-permute-start | bytes 1622024 | tf_op jit(solution)/shard_map/ppermute | solution.py:321
  13.1 47.3 %collective-permute-start.7 = (bf16[512,1024]{1,0:T(8,128)(2,1)}, bf16[512,1024]{1,0:T(8,128)(2,1)}, u32[]{:S(2)}, u32[]{:S(2)}) collective-permute-start(bf16[512,1024]{1,0:T(8,128)(2,1)} %refs_2_.1), channel_id=1, source_target_pairs={{2,0},{3,1},{0,2},{1,3},{10,8},{11,9},{8,10},{9,11},{18,16},{19,17... | collective-permute-start | bytes 3145736 | tf_op jit(solution)/shard_map/ppermute | solution.py:321
  17.8 5.0 %collective-permute-start.4 = (bf16[528,512]{1,0:T(8,128)(2,1)S(1)}, bf16[528,512]{1,0:T(8,128)(2,1)S(1)}, u32[]{:S(2)}, u32[]{:S(2)}) collective-permute-start(bf16[528,512]{1,0:T(8,128)(2,1)S(1)} %collective-permute-done.3.refs_0_), channel_id=1, source_target_pairs={{0,1},{1,0},{2,3},{3,2},{4,5},{5,4},{6,7},{7,6},{8,9},{9,8},{10,11... | collective-permute-start | bytes 1622024 | tf_op jit(solution)/shard_map/ppermute | solution.py:324
  18.0 35.3 %collective-permute-start.2 = (bf16[512,512]{1,0:T(8,128)(2,1)S(1)}, bf16[512,512]{1,0:T(8,128)(2,1)S(1)}, u32[]{:S(2)}, u32[]{:S(2)}) collective-permute-start(bf16[512,512]{1,0:T(8,128)(2,1)S(1)} %get-tuple-element.54), channel_id=1, source_target_pairs={{2,0},{3,1},{0,2},{1,3},{10,8},{11,9},{8,10},{9,11},{18,16},{19,17... | collective-permute-start | bytes 1572872 | tf_op jit(solution)/shard_map/ppermute | solution.py:321
  20.0 33.2 %collective-permute-start.5 = (bf16[512,512]{1,0:T(8,128)(2,1)S(1)}, bf16[512,512]{1,0:T(8,128)(2,1)S(1)}, u32[]{:S(2)}, u32[]{:S(2)}) collective-permute-start(bf16[512,512]{1,0:T(8,128)(2,1)S(1)} %get-tuple-element.53), channel_id=1, source_target_pairs={{3,1},{1,3},{11,9},{9,11},{19,17},{17,19},{27,25},{25,27}} | collective-permute-start | bytes 1572872 | tf_op jit(solution)/shard_map/ppermute | solution.py:321
  22.8 1.6 %copy-start.4 = (f32[512,1024]{1,0:T(8,128)}, f32[512,1024]{1,0:T(8,128)S(1)}, u32[]{:S(2)}) copy-start(f32[512,1024]{1,0:T(8,128)S(1)} %get-tuple-element.32.refs_3_.gram) | copy-start | bytes 6291460
  24.4 1.3 %copy-start.14 = (bf16[1024,1024]{1,0:T(8,128)(2,1)}, bf16[1024,1024]{1,0:T(8,128)(2,1)S(1)}, u32[]{:S(2)}) copy-start(bf16[1024,1024]{1,0:T(8,128)(2,1)S(1)} %get-tuple-element.37.refs_7_) | copy-start | bytes 6291460
  25.7 1.0 copy-start.18
  26.7 35.5 %copy-start.20 = (s32[4]{0:T(128)S(1)}, s32[4]{0:T(128)}, u32[]{:S(2)}) copy-start(s32[4]{0:T(128)} %param.5) | copy-start | bytes 52
  26.7 37.8 %copy-start.1 = (bf16[512,1024]{1,0:T(8,128)(2,1)S(1)}, bf16[512,1024]{1,0:T(8,128)(2,1)}, u32[]{:S(2)}) copy-start(bf16[512,1024]{1,0:T(8,128)(2,1)} %refs_0_.5) | copy-start | bytes 3145732
  26.7 33.7 %collective-permute-start.9 = (bf16[528,512]{1,0:T(8,128)(2,1)}, bf16[528,512]{1,0:T(8,128)(2,1)}, u32[]{:S(2)}, u32[]{:S(2)}) collective-permute-start(bf16[528,512]{1,0:T(8,128)(2,1)} %get-tuple-element.33), channel_id=1, source_target_pairs={{4,0},{5,1},{12,8},{13,9},{20,16},{21,17},{28,24},{29,25}} | collective-permute-start | bytes 1622024 | tf_op jit(solution)/shard_map/ppermute | solution.py:321
  28.1 32.3 %collective-permute-start.10 = (bf16[528,512]{1,0:T(8,128)(2,1)}, bf16[528,512]{1,0:T(8,128)(2,1)}, u32[]{:S(2)}, u32[]{:S(2)}) collective-permute-start(bf16[528,512]{1,0:T(8,128)(2,1)} %get-tuple-element.33), channel_id=1, source_target_pairs={{4,2},{5,3},{12,10},{13,11},{20,18},{21,19},{28,26},{29,27}} | collective-permute-start | bytes 1622024 | tf_op jit(solution)/shard_map/ppermute | solution.py:321
  55.0 7.9 %collective-permute-start.6 = (bf16[512,1024]{1,0:T(8,128)(2,1)}, bf16[512,1024]{1,0:T(8,128)(2,1)}, u32[]{:S(2)}, u32[]{:S(2)}) collective-permute-start(bf16[512,1024]{1,0:T(8,128)(2,1)} %constant_dynamic-update-slice_fusion.refs_2_), channel_id=1, source_target_pairs={{0,1},{1,0},{2,3},{3,2},{4,5},{5,4},{6,7},{7,6},{8,9},{9,8},{10,11... | collective-permute-start | bytes 3145736 | tf_op jit(solution)/shard_map/ppermute | solution.py:324
  60.3 4.1 %collective-permute-start.8 = (bf16[512,1024]{1,0:T(8,128)(2,1)}, bf16[512,1024]{1,0:T(8,128)(2,1)}, u32[]{:S(2)}, u32[]{:S(2)}) collective-permute-start(bf16[512,1024]{1,0:T(8,128)(2,1)} %collective-permute-done.7.refs_4_), channel_id=1, source_target_pairs={{0,1},{1,0},{2,3},{3,2},{4,5},{5,4},{6,7},{7,6},{8,9},{9,8},{10,11... | collective-permute-start | bytes 3145736 | tf_op jit(solution)/shard_map/ppermute | solution.py:324
  60.3 4.1 %copy-start.3 = (bf16[512,1024]{1,0:T(8,128)(2,1)S(1)}, bf16[512,1024]{1,0:T(8,128)(2,1)}, u32[]{:S(2)}) copy-start(bf16[512,1024]{1,0:T(8,128)(2,1)} %copy-done.2) | copy-start | bytes 3145732
  61.6 13.0 %collective-permute-start.11 = (bf16[528,512]{1,0:T(8,128)(2,1)S(1)}, bf16[528,512]{1,0:T(8,128)(2,1)S(1)}, u32[]{:S(2)}, u32[]{:S(2)}) collective-permute-start(bf16[528,512]{1,0:T(8,128)(2,1)S(1)} %broadcast_select_fusion.refs_0_), channel_id=1, source_target_pairs={{0,1},{1,0},{2,3},{3,2},{4,5},{5,4},{6,7},{7,6},{8,9},{9,8},{10,11... | collective-permute-start | bytes 1622024 | tf_op jit(solution)/shard_map/ppermute | solution.py:324
  64.5 1.6 %copy-start.15 = (bf16[1024,1024]{1,0:T(8,128)(2,1)S(1)}, bf16[1024,1024]{1,0:T(8,128)(2,1)}, u32[]{:S(2)}) copy-start(bf16[1024,1024]{1,0:T(8,128)(2,1)} %copy-done.14) | copy-start | bytes 6291460
  66.0 1.2 %copy-start.19 = (bf16[512,1024]{1,0:T(8,128)(2,1)S(1)}, bf16[512,1024]{1,0:T(8,128)(2,1)}, u32[]{:S(2)}) copy-start(bf16[512,1024]{1,0:T(8,128)(2,1)} %copy-done.18) | copy-start | bytes 3145732
  74.6 8.1 %copy-start.6 = (bf16[1024,1024]{1,0:T(8,128)(2,1)}, bf16[1024,1024]{1,0:T(8,128)(2,1)S(1)}, u32[]{:S(2)}) copy-start(bf16[1024,1024]{1,0:T(8,128)(2,1)S(1)} %get-tuple-element.41.refs_4_.coupling_0) | copy-start | bytes 6291460
  74.6 13.7 %copy-start.5 = (f32[512,1024]{1,0:T(8,128)S(1)}, f32[512,1024]{1,0:T(8,128)}, u32[]{:S(2)}) copy-start(f32[512,1024]{1,0:T(8,128)} %copy-done.4) | copy-start | bytes 6291460
  82.7 1.4 %copy-start.8 = (bf16[1024,1024]{1,0:T(8,128)(2,1)}, bf16[1024,1024]{1,0:T(8,128)(2,1)S(1)}, u32[]{:S(2)}) copy-start(bf16[1024,1024]{1,0:T(8,128)(2,1)S(1)} %get-tuple-element.45.off_0) | copy-start | bytes 6291460
  84.1 1.4 %copy-start.10 = (bf16[1024,1024]{1,0:T(8,128)(2,1)}, bf16[1024,1024]{1,0:T(8,128)(2,1)S(1)}, u32[]{:S(2)}) copy-start(bf16[1024,1024]{1,0:T(8,128)(2,1)S(1)} %get-tuple-element.46.off_1) | copy-start | bytes 6291460
  85.5 1.4 %copy-start.12 = (bf16[1024,1024]{1,0:T(8,128)(2,1)}, bf16[1024,1024]{1,0:T(8,128)(2,1)S(1)}, u32[]{:S(2)}) copy-start(bf16[1024,1024]{1,0:T(8,128)(2,1)S(1)} %get-tuple-element.47.cov_1) | copy-start | bytes 6291460
  86.9 10.6 %collective-permute-start.12 = (bf16[16,1024]{1,0:T(8,128)(2,1)S(1)}, bf16[16,1024]{1,0:T(8,128)(2,1)S(1)}, u32[]{:S(2)}, u32[]{:S(2)}) collective-permute-start(bf16[16,1024]{1,0:T(8,128)(2,1)S(1)} %get-tuple-element.52.mine), channel_id=1, source_target_pairs={{0,4},{1,5},{2,6},{3,7},{8,12},{9,13},{10,14},{11,15},{16,20},{17,... | collective-permute-start | bytes 98312 | tf_op jit(solution)/shard_map/ppermute | solution.py:321
  88.3 1.6 %copy-start.7 = (bf16[1024,1024]{1,0:T(8,128)(2,1)S(1)}, bf16[1024,1024]{1,0:T(8,128)(2,1)}, u32[]{:S(2)}) copy-start(bf16[1024,1024]{1,0:T(8,128)(2,1)} %copy-done.6) | copy-start | bytes 6291460
  89.9 1.6 %copy-start.9 = (bf16[1024,1024]{1,0:T(8,128)(2,1)S(1)}, bf16[1024,1024]{1,0:T(8,128)(2,1)}, u32[]{:S(2)}) copy-start(bf16[1024,1024]{1,0:T(8,128)(2,1)} %copy-done.8) | copy-start | bytes 6291460
  91.4 1.6 %copy-start.11 = (bf16[1024,1024]{1,0:T(8,128)(2,1)S(1)}, bf16[1024,1024]{1,0:T(8,128)(2,1)}, u32[]{:S(2)}) copy-start(bf16[1024,1024]{1,0:T(8,128)(2,1)} %copy-done.10) | copy-start | bytes 6291460
  93.0 1.6 %copy-start.13 = (bf16[1024,1024]{1,0:T(8,128)(2,1)S(1)}, bf16[1024,1024]{1,0:T(8,128)(2,1)}, u32[]{:S(2)}) copy-start(bf16[1024,1024]{1,0:T(8,128)(2,1)} %copy-done.12) | copy-start | bytes 6291460

commit v3 on v2

--- a/solution.py
+++ b/solution.py
@@ -7,6 +7,7 @@
 from jax.experimental.pallas import tpu as pltpu
 from jax.sharding import PartitionSpec as P
 
+
 TB = 4
 SLOTS = 2
 SPARE = 16
@@ -16,7 +17,7 @@
 BF16 = jnp.bfloat16
 F32 = jnp.float32
 
-ANY = pl.BlockSpec(memory_space=pl.ANY)
+HBM = pl.BlockSpec(memory_space=pltpu.HBM)
 VMEM = pl.BlockSpec(memory_space=pltpu.VMEM)
 SMEM = pl.BlockSpec(memory_space=pltpu.SMEM)
 PARAMS = pltpu.CompilerParams(vmem_limit_bytes=36 << 20)
@@ -139,6 +140,58 @@
     return jnp.concatenate([spare[k + 1 : k + 2] for k in range(n // rows)], 1)
 
 
+def fold_kernel(ids, factor, square, cross, sems):
+    rows = factor.shape[0]
+    half = rows // 2
+    quarter = rows // 4
+    start = pl.multiple_of(ids[0], rows)
+    moves = [
+        (factor.at[half:, pl.ds(start, rows)], square.at[:half]),
+        (factor.at[:quarter, pl.ds(start, half)], square.at[half:, :half]),
+        (factor.at[quarter:half, pl.ds(start, half)], square.at[half:, half:]),
+        (factor.at[:, :rows], cross),
+    ]
+    copies = [pltpu.make_async_copy(s, t, sems.at[i]) for i, (s, t) in enumerate(moves)]
+    for copy in copies:
+        copy.start()
+    for copy in copies:
+        copy.wait()
+
+
+def unfold(target, squares, crosses, start, sems):
+    rows = squares[0].shape[0] * 4 // 3
+    half = rows // 2
+    quarter = rows // 4
+    n = target.shape[0]
+    moves = []
+    for square, at in zip(squares, (start, n - rows - start)):
+        moves += [
+            (square.at[:half], target.at[pl.ds(at + half, half), pl.ds(at, rows)]),
+            (square.at[half:, :half], target.at[pl.ds(at, quarter), pl.ds(at, half)]),
+            (
+                square.at[half:, half:],
+                target.at[pl.ds(at + quarter, quarter), pl.ds(at, half)],
+            ),
+        ]
+        zeros = jnp.zeros((half, half), BF16)
+        target[pl.ds(at, half), pl.ds(pl.multiple_of(at + half, half), half)] = zeros
+    target[:rows, rows:] = jnp.zeros((rows, n - rows), BF16)
+    copies = [pltpu.make_async_copy(s, t, sems.at[i]) for i, (s, t) in enumerate(moves)]
+    for copy in copies:
+        copy.start()
+    low = target.at[rows:, :rows]
+
+    @pl.when(start == 0)
+    def _():
+        pltpu.make_async_copy(crosses[1], low, sems.at[len(moves)]).start()
+
+    @pl.when(start != 0)
+    def _():
+        pltpu.make_async_copy(crosses[0], low, sems.at[len(moves)]).start()
+
+    return copies + [pltpu.make_async_copy(crosses[0], low, sems.at[len(moves)])]
+
+
 def first_kernel(pieces, paired, ids, *refs):
     factors, lowers = refs[:pieces], refs[pieces : 2 * pieces]
     coupling, packet, cov, factor, lower, total, sems = refs[2 * pieces :]
@@ -181,6 +234,39 @@
         two.wait()
 
 
+def heard_kernel(pieces, paired, ids, *refs):
+    factors = refs[:pieces]
+    parts = refs[pieces : len(refs) - 5]
+    heard, gram_1, diag_0, factor, sems = refs[len(refs) - 5 :]
+    rows = factors[0].shape[0] if paired else factor.shape[0]
+    start = pl.multiple_of(ids[0], TILE)
+    if paired:
+        start = pl.multiple_of(ids[0], rows)
+    block = ids[1]
+
+    def finish(factor_1, factor_0):
+        gram_1[...] = mm_t(factor_1[...], factor_1[...])
+        diag_0[...] = jnp.sum(jnp.square(factor_0[...].astype(F32)), axis=0, keepdims=True)
+
+    @pl.when(block < 2)
+    def _():
+        copies = load_rows(factor, factors, start, sems.at[0])
+        if paired:
+            copies += unfold(heard, parts[:2], parts[2:], start, sems.at[1])
+        else:
+            copies += load_rows(heard, parts, start, sems.at[1])
+        for copy in copies:
+            copy.wait()
+
+        @pl.when(block == 0)
+        def _():
+            finish(heard, factor)
+
+        @pl.when(block == 1)
+        def _():
+            finish(factor, heard)
+
+
 def second_kernel(pieces, paired, ids, *refs):
     packets = refs[:pieces]
     coupling, gram, packet, off, cov, full, diag = refs[pieces:]
@@ -197,10 +283,9 @@
 
 
 def ready_kernel(pieces, ids, *refs):
-    factors, heard_factors = refs[:pieces], refs[pieces : 2 * pieces]
-    heard_lowers = refs[2 * pieces : 3 * pieces]
-    (coupling, off, cov, _, _, coupling_1, gram_1, coupling_0, diag_0, off_out, cov_out,
-     factor, heard, lower, sems, out_sems) = refs[3 * pieces :]
+    lowers = refs[:pieces]
+    (heard, coupling, off, cov, _, _, coupling_1, coupling_0, off_out, cov_out,
+     lower, sems, out_sems) = refs[pieces:]
     rows = cov.shape[0]
     start = pl.multiple_of(ids[0], rows)
     block = ids[1]
@@ -216,29 +301,42 @@
 
     @pl.when(block < 2)
     def _():
-        copies = load_rows(factor, factors, start, sems.at[0])
-        copies += load_rows(heard, heard_factors, start, sems.at[1])
-        copies += load_rows(lower, heard_lowers, start, sems.at[2])
+        copies = load_rows(lower, lowers, start, sems.at[0])
+
+        @pl.when(block == 0)
+        def _():
+            coupling_0[...] = coupling[...]
+
+        @pl.when(block == 1)
+        def _():
+            coupling_1[...] = coupling[...]
+
         for copy in copies:
             copy.wait()
-
-        def finish(factor_1, factor_0):
-            gram_1[...] = mm_t(factor_1[...], factor_1[...])
-            diag_0[...] = jnp.sum(
-                jnp.square(factor_0[...].astype(F32)), axis=0, keepdims=True
-            )
 
         @pl.when(block == 0)
         def _():
             couple(coupling_1, lower, heard)
-            coupling_0[...] = coupling[...]
-            finish(heard, factor)
 
         @pl.when(block == 1)
         def _():
             couple(coupling_0, lower, heard)
-            coupling_1[...] = coupling[...]
-            finish(factor, heard)
+
+
+def merge_kernel(ids, at_0, at_1, out, sem):
+    block = ids[1]
+
+    @pl.when(block == 0)
+    def _():
+        copy = pltpu.make_async_copy(at_0, out, sem.at[0])
+        copy.start()
+        copy.wait()
+
+    @pl.when(block == 1)
+    def _():
+        copy = pltpu.make_async_copy(at_1, out, sem.at[0])
+        copy.start()
+        copy.wait()
 
 
 def third_kernel(pieces, paired, ids, *refs):
@@ -246,8 +344,8 @@
     (coupling_1, gram_1, coupling_0, diag_0, off_0, off_1, cov_1, variances,
      full, diag) = refs[pieces:]
     n = full.shape[0]
-    block = ids[1]
     start = ids[0]
+    block = ids[1]
 
     @pl.when(block < 2)
     def _():
@@ -292,29 +390,30 @@
         two.wait()
 
 
-def deliver_kernel(ids, choice, mine, heard, out):
-    block = ids[1]
+def deliver_kernel(ids, owner, mine, heard, out):
+    block = ids[1]
+    dev = ids[2]
     values = jnp.where(block < 2, mine[...].astype(F32), heard[...].astype(F32))
+    lines = [jnp.zeros((1, out.shape[1]), F32) for _ in range(SLOTS)]
+    for t in range(TB):
+        rank = jnp.int32(0)
+        for before in range(t):
+            rank += (owner[before] == owner[t]).astype(jnp.int32)
+        for slot in range(SLOTS):
+            here = jnp.logical_and(owner[t] == dev, rank == slot)
+            lines[slot] += jnp.where(here, values[t : t + 1], 0.0)
     for slot in range(SLOTS):
-        line = jnp.zeros((1, out.shape[1]), F32)
-        for t in range(TB):
-            line += jnp.where(choice[slot * TB + t] == 1, values[t : t + 1], 0.0)
-        out[slot : slot + 1, :] = line
-
-
-def vmem(*arrays):
-    return [pltpu.with_memory_space_constraint(a, pltpu.VMEM) for a in arrays]
+        out[slot : slot + 1, :] = lines[slot]
 
 
 def shards(linv, sub, owner):
     group = lax.axis_size("tm") // TB
     rows, n = linv.shape
-    half = n // 2
     paired = group == 2
     dev = lax.axis_index("tm")
     member = dev % group
     block = dev // group
-    ids = jnp.stack([member * rows, block]).astype(jnp.int32)
+    ids = jnp.stack([member * rows, block, dev]).astype(jnp.int32)
 
     def block_to_block(values, routes, members=range(group)):
         pairs = [(s * group + i, t * group + i) for s, t in routes for i in members]
@@ -342,140 +441,126 @@
     def after(values, *others):
         return lax.optimization_barrier((values, *others))[0]
 
+    def call(kernel, out, inputs, spaces, scratch, aliases=None):
+        shapes = tuple(
+            pltpu.HBM(o[1], o[2]) if o[0] is HBM else pltpu.VMEM(o[1], o[2]) for o in out
+        )
+        placed = [
+            x if space is SMEM else pltpu.with_memory_space_constraint(x, space.memory_space)
+            for x, space in zip(inputs, spaces, strict=True)
+        ]
+        return pl.pallas_call(
+            kernel,
+            out_shape=shapes,
+            in_specs=list(spaces),
+            out_specs=tuple(o[0] for o in out),
+            scratch_shapes=scratch,
+            input_output_aliases=aliases or {},
+            compiler_params=PARAMS,
+        )(*placed)
+
+    def sems(*shape):
+        return pltpu.SemaphoreType.DMA(shape)
+
     pieces = 2 if paired else 1
     packet_shape = (rows + SPARE, rows) if paired else (rows + SPARE, n)
-    gathered = packet_shape if paired else (group, *packet_shape)
-    whole = pltpu.VMEM((n, n), BF16)
-    part = pltpu.VMEM((rows, n), BF16)
-    hbm = jax.ShapeDtypeStruct((rows, n), BF16)
+    whole = (VMEM, (n, n), BF16)
+    part = (VMEM, (rows, n), BF16)
+    out_rows = (HBM, (rows, n), BF16)
     square = pltpu.VMEM((n, n), BF16)
 
     factors = pieces_of(linv)
     lowers = pieces_of(sub)
     swap = [(1, 0), (0, 1)]
-    heard_lower = block_to_block(sub, swap)
-
-    coupling, packet, cov_3 = pl.pallas_call(
+    if paired:
+        folded, cross = call(
+            fold_kernel,
+            [(HBM, (rows * 3 // 4, rows), BF16), (HBM, (rows, rows), BF16)],
+            [ids, linv],
+            [SMEM, HBM],
+            [sems(4)],
+        )
+        raw = [block_to_block(folded, swap), block_to_block(cross, swap, range(1, 2))]
+    else:
+        raw = [block_to_block(linv, swap)]
+    raw_lower = block_to_block(sub, swap)
+
+    coupling, packet, cov_3 = call(
         functools.partial(first_kernel, pieces, paired),
-        out_shape=(whole, pltpu.VMEM(packet_shape, BF16), part),
-        in_specs=[SMEM] + [ANY] * (2 * pieces),
-        out_specs=(VMEM, VMEM, VMEM),
-        scratch_shapes=[
-            square,
-            square,
-            pltpu.VMEM((rows, n), F32),
-            pltpu.SemaphoreType.DMA((2, 2)),
-        ],
-        compiler_params=PARAMS,
-        name="first",
-    )(ids, *factors, *lowers)
-
+        [whole, (VMEM, packet_shape, BF16), part],
+        [ids, *factors, *lowers],
+        [SMEM] + [HBM] * (2 * pieces),
+        [square, square, pltpu.VMEM((rows, n), F32), sems(2, 2)],
+    )
     packet_2 = block_to_block(packet, [(3, 2)])
-    late = after(linv, packet)
-    heard_left = block_to_block(late[:, :half], swap)
-    heard_right = block_to_block(late[:, half:], swap, range(group // 2, group))
-
-    gram, off_rows, cov_rows = pl.pallas_call(
+
+    gram, off_rows, cov_rows = call(
         functools.partial(gram_kernel, pieces),
-        out_shape=(pltpu.VMEM((rows, n), F32), hbm, hbm),
-        in_specs=[SMEM] + [ANY] * pieces + [VMEM, VMEM],
-        out_specs=(VMEM, ANY, ANY),
-        scratch_shapes=[
-            square,
-            pltpu.VMEM((rows, n), BF16),
-            pltpu.SemaphoreType.DMA((1, 2)),
-            pltpu.SemaphoreType.DMA((2,)),
-        ],
-        compiler_params=PARAMS,
-        name="gram",
-    )(ids, *factors, *vmem(coupling, cov_3))
-
-    packet, off_2, cov_2 = pl.pallas_call(
+        [(VMEM, (rows, n), F32), out_rows, out_rows],
+        [ids, *factors, coupling, cov_3],
+        [SMEM] + [HBM] * pieces + [VMEM, VMEM],
+        [square, pltpu.VMEM((rows, n), BF16), sems(1, 2), sems(2)],
+    )
+    parts = [x for piece in raw for x in pieces_of(after(piece, gram))]
+    heard_factor, gram_1, diag_0 = call(
+        functools.partial(heard_kernel, pieces, paired),
+        [whole, (VMEM, (n, n), F32), (VMEM, (1, n), F32)],
+        [ids, *factors, *parts],
+        [SMEM] + [HBM] * (pieces + len(parts)),
+        [square, sems(2, 8)],
+    )
+
+    packet, off_2, cov_2 = call(
         functools.partial(second_kernel, pieces, paired),
-        out_shape=(pltpu.VMEM(packet_shape, BF16), whole, part),
-        in_specs=[SMEM] + [VMEM] * (pieces + 2),
-        out_specs=(VMEM, VMEM, VMEM),
-        scratch_shapes=[square, pltpu.VMEM((1, n), F32)],
-        compiler_params=PARAMS,
-        name="second",
-    )(ids, *vmem(*packets_of(packet_2), coupling, gram))
-
+        [(VMEM, packet_shape, BF16), whole, part],
+        [ids, *packets_of(packet_2), coupling, gram],
+        [SMEM] + [VMEM] * (pieces + 2),
+        [square, pltpu.VMEM((1, n), F32)],
+    )
     packet_0 = block_to_block(packet, [(2, 0)])
     packet_1 = block_to_block(packet, [(2, 1)])
 
-    heard_factor = jnp.concatenate([after(heard_left, packet), after(heard_right, packet)], 1)
-    heard_factors = pieces_of(heard_factor)
-    heard_lowers = pieces_of(after(heard_lower, packet))
-    coupling_1, gram_1, coupling_0, diag_0, off_rows, cov_rows = pl.pallas_call(
+    raw_lowers = pieces_of(after(raw_lower, packet))
+    coupling_1, coupling_0, off_rows, cov_rows = call(
         functools.partial(ready_kernel, pieces),
-        out_shape=(
-            whole,
-            pltpu.VMEM((n, n), F32),
-            whole,
-            pltpu.VMEM((1, n), F32),
-            hbm,
-            hbm,
-        ),
-        in_specs=[SMEM] + [ANY] * (3 * pieces) + [VMEM] * 3 + [ANY, ANY],
-        out_specs=(VMEM, VMEM, VMEM, VMEM, ANY, ANY),
-        scratch_shapes=[
-            square,
-            square,
-            square,
-            pltpu.SemaphoreType.DMA((3, 2)),
-            pltpu.SemaphoreType.DMA((2,)),
-        ],
-        input_output_aliases={3 * pieces + 4: 4, 3 * pieces + 5: 5},
-        compiler_params=PARAMS,
-        name="ready",
-    )(
-        ids,
-        *factors,
-        *heard_factors,
-        *heard_lowers,
-        *vmem(coupling, off_2, cov_2),
-        off_rows,
-        cov_rows,
-    )
-
-    carried = jnp.where(block == 0, packet_0, packet_1)
-    off_0, off_1, cov_1, variances = pl.pallas_call(
+        [whole, whole, out_rows, out_rows],
+        [ids, *raw_lowers, heard_factor, coupling, off_2, cov_2, off_rows, cov_rows],
+        [SMEM] + [HBM] * pieces + [VMEM] * 4 + [HBM, HBM],
+        [square, sems(1, 2), sems(2)],
+        {pieces + 5: 2, pieces + 6: 3},
+    )
+
+    (carried,) = call(
+        merge_kernel,
+        [(VMEM, packet_shape, BF16)],
+        [ids, packet_0, packet_1],
+        [SMEM, VMEM, VMEM],
+        [sems(1)],
+    )
+    off_0, off_1, cov_1, variances = call(
         functools.partial(third_kernel, pieces, paired),
-        out_shape=(whole, whole, whole, pltpu.VMEM((SPARE, n), BF16)),
-        in_specs=[SMEM] + [VMEM] * (pieces + 4),
-        out_specs=(VMEM, VMEM, VMEM, VMEM),
-        scratch_shapes=[square, pltpu.VMEM((1, n), F32)],
-        compiler_params=PARAMS,
-        name="third",
-    )(ids, *vmem(*packets_of(carried), coupling_1, gram_1, coupling_0, diag_0))
-
+        [whole, whole, whole, (VMEM, (SPARE, n), BF16)],
+        [ids, *packets_of(carried), coupling_1, gram_1, coupling_0, diag_0],
+        [SMEM] + [VMEM] * (pieces + 4),
+        [square, pltpu.VMEM((1, n), F32)],
+    )
     heard = block_to_block(variances, [(0, 2), (1, 3)])
 
-    off_rows, cov_rows = pl.pallas_call(
+    off_rows, cov_rows = call(
         last_kernel,
-        out_shape=(hbm, hbm),
-        in_specs=[SMEM] + [VMEM] * 5 + [ANY, ANY],
-        out_specs=(ANY, ANY),
-        scratch_shapes=[pltpu.VMEM((rows, n), BF16), pltpu.SemaphoreType.DMA((2,))],
-        input_output_aliases={6: 0, 7: 1},
-        compiler_params=PARAMS,
-        name="last",
-    )(ids, *vmem(coupling_0, gram, off_0, off_1, cov_1), off_rows, cov_rows)
-
-    positions = lax.broadcasted_iota(jnp.int32, (TB, TB), 1)
-    current = lax.broadcasted_iota(jnp.int32, (TB, TB), 0)
-    same_owner = owner[:, None] == owner[None, :]
-    slot_rank = jnp.sum(jnp.where(same_owner & (positions < current), 1, 0), axis=1)
-    slot_iota = lax.broadcasted_iota(jnp.int32, (SLOTS, TB), 0)
-    choice = (owner[None, :] == dev) & (slot_rank[None, :] == slot_iota)
-    owned_var = pl.pallas_call(
+        [out_rows, out_rows],
+        [ids, coupling_0, gram, off_0, off_1, cov_1, off_rows, cov_rows],
+        [SMEM] + [VMEM] * 5 + [HBM, HBM],
+        [pltpu.VMEM((rows, n), BF16), sems(2)],
+        {6: 0, 7: 1},
+    )
+    (owned_var,) = call(
         deliver_kernel,
-        out_shape=jax.ShapeDtypeStruct((SLOTS, n), F32),
-        in_specs=[SMEM, SMEM, VMEM, VMEM],
-        out_specs=VMEM,
-        compiler_params=PARAMS,
-        name="deliver",
-    )(ids, choice.astype(jnp.int32).reshape(SLOTS * TB), variances, heard)
+        [(VMEM, (SLOTS, n), F32)],
+        [ids, owner, variances, heard],
+        [SMEM, SMEM, VMEM, VMEM],
+        [],
+    )
     return (cov_rows, off_rows, owned_var)
 
 

time: 99.3 us -> 97.6 us (0.983)
  Pallas kernels: 26.7 us -> 59.2 us
  waiting for transfers between devices: 29.7 us -> 8.23 us
  local copies, waits for them, and re-layouts: 21 us -> 4.06 us
  starting transfers between devices: 18.9 us -> 24.8 us
  other arithmetic: 1.47 us -> 0.08 us
    pallas_call x7 -> x10, Pallas kernels: 26.7 us -> 59.2 us  [call(): pl.pallas_call(kernel, out_shape=shapes, in_specs=list(spaces), out_specs...]
    ppermute x7, waiting for transfers between devices: 23.7 us -> 3.03 us  [block_to_block(): return lax.ppermute(values, 'tm', pairs)]
    unnamed x43 -> x21, local copies, waits for them, and re-layouts: 19.9 us -> 4.06 us
    ppermute x6 -> x7, starting transfers between devices: 6.56 us -> 11.7 us  [peer(): return lax.ppermute(piece, 'tm', [(i, i ^ step) for i in range(TB * group)])]
    select_n x1 -> x0, other arithmetic: 1.2 us -> none  [shards(): carried = jnp.where(block == 0, packet_0, packet_1)]
    ppermute x6 -> x7, waiting for transfers between devices: 5.99 us -> 5.2 us  [peer(): return lax.ppermute(piece, 'tm', [(i, i ^ step) for i in range(TB * group)])]
  transfers between devices with their start and end apart: 13 -> 14, of which waited for: 5 -> 4; matrix products, arithmetic and copies ran while one was open for 3% -> 0% of each run, Pallas kernels for 14% -> 47%
where the time goes in v3:
time: 97.6 us; the launch traced here: 97.3 us
  Pallas kernels  59.2 us (61%)
  starting transfers between devices  24.8 us (25%)
  waiting for transfers between devices  8.23 us (8%)
  local copies, waits for them, and re-layouts  4.06 us (4%)
    pallas_call x10, Pallas kernels, call(): pl.pallas_call(kernel, out_shape=shapes, in_specs=list(spaces), out_specs...  59.2 us
    ppermute x7, starting transfers between devices, block_to_block(): return lax.ppermute(values, 'tm', pairs)  13.1 us
    ppermute x7, starting transfers between devices, peer(): return lax.ppermute(piece, 'tm', [(i, i ^ step) for i in range(TB * group)])  11.7 us
    ppermute x7, waiting for transfers between devices, peer(): return lax.ppermute(piece, 'tm', [(i, i ^ step) for i in range(TB * group)])  5.2 us
    unnamed x21, local copies, waits for them, and re-layouts  4.06 us
    ppermute x7, waiting for transfers between devices, block_to_block(): return lax.ppermute(values, 'tm', pairs)  3.03 us
  transfers between devices with their start and end apart: 14, of which 4 were waited for; matrix products, arithmetic and copies ran while one was open for 0% of the time, Pallas kernels for 47%

profile of v3, /device:TPU:0, one launch (start us, length us, event | category | flops | bytes accessed | tf_op | source)
XLA Modules:
  0.0 97.3 jit_solution(8819847869744073520)
XLA Ops:
  0.6 0.6 collective-permute-start.1
  1.2 0.1 collective-permute-start.2
  1.3 0.1 pad_add_fusion.ids
  1.3 0.0 copy-start.2
  1.3 2.3 %collective-permute-done.1.refs_1_ = bf16[512,1024]{1,0:T(8,128)(2,1)S(1)} collective-permute-done((bf16[512,1024]{1,0:T(8,128)(2,1)}, bf16[512,1024]{1,0:T(8,128)(2,1)S(1)}, u32[]{:S(2)}, u32[]{:S(2)}) %collective-permute-start.1) | collective-permute-done | bytes 1048608 | tf_op jit(solution)/shard_map/ppermute | solution.py:423
  3.7 0.0 copy-start.1
  3.7 1.5 %collective-permute-done.2.refs_3_ = bf16[512,1024]{1,0:T(8,128)(2,1)S(1)} collective-permute-done((bf16[512,1024]{1,0:T(8,128)(2,1)}, bf16[512,1024]{1,0:T(8,128)(2,1)S(1)}, u32[]{:S(2)}, u32[]{:S(2)}) %collective-permute-start.2) | collective-permute-done | bytes 1048608 | tf_op jit(solution)/shard_map/ppermute | solution.py:423
  5.2 0.0 copy-done.1
  5.2 0.0 copy-start.5
  5.2 1.0 copy-done.5
  6.2 4.5 %shard_map.58 = (bf16[1024,1024]{1,0:T(8,128)(2,1)S(1)}, bf16[528,512]{1,0:T(8,128)(2,1)S(1)}, bf16[512,1024]{1,0:T(8,128)(2,1)S(1)}) custom-call(s32[3]{0:T(128)S(1)} %pad_add_fusion.ids, bf16[512,1024]{1,0:T(8,128)(2,1)} %refs_0_.5, bf16[512,1024]{1,0:T(8,128)(2,1)} %copy-done.1, bf16[512,1024]{1,0:T(8,128)(2,1)} %refs_2_.1, bf16[512,1024]{1,0:T(8,128)(2,1)} %copy-done.5), custom_call_target="tpu_custom_call" | custom-call | tf_op jit(solution)/shard_map/pallas_call | solution.py:452
  10.7 0.7 collective-permute-start.3
  11.4 0.0 copy-done.2
  11.4 4.8 %collective-permute-start = (bf16[512,1024]{1,0:T(8,128)(2,1)S(1)}, bf16[512,1024]{1,0:T(8,128)(2,1)S(1)}, u32[]{:S(2)}, u32[]{:S(2)}) collective-permute-start(bf16[512,1024]{1,0:T(8,128)(2,1)S(1)} %copy-done.2), channel_id=1, source_target_pairs={{2,0},{3,1},{0,2},{1,3},{10,8},{11,9},{8,10},{9,11},{18,16},{19,17... | collective-permute-start | bytes 3145736 | tf_op jit(solution)/shard_map/ppermute | solution.py:420
  16.2 0.0 collective-permute-done.3.refs_0_
  16.2 0.1 collective-permute-start.4
  16.3 3.4 %shard_map.59 = (f32[512,1024]{1,0:T(8,128)S(1)}, bf16[512,1024]{1,0:T(8,128)(2,1)}, bf16[512,1024]{1,0:T(8,128)(2,1)}) custom-call(s32[3]{0:T(128)S(1)} %pad_add_fusion.ids, bf16[512,1024]{1,0:T(8,128)(2,1)} %refs_0_.5, bf16[512,1024]{1,0:T(8,128)(2,1)} %copy-done.1, bf16[1024,1024]{1,0:T(8,128)(2,1)S(1)} %get-tuple-element.31.refs_2_.refs_3_, ...), custom_call_target="tpu_custom_call" | custom-call | tf_op jit(solution)/shard_map/pallas_call | solution.py:452
  19.7 0.0 collective-permute-done.4.refs_1_
  19.7 0.6 shard_map.60
  20.3 1.3 %collective-permute-start.10 = (bf16[528,512]{1,0:T(8,128)(2,1)S(1)}, bf16[528,512]{1,0:T(8,128)(2,1)S(1)}, u32[]{:S(2)}, u32[]{:S(2)}) collective-permute-start(bf16[528,512]{1,0:T(8,128)(2,1)S(1)} %get-tuple-element.34), channel_id=1, source_target_pairs={{4,0},{5,1},{12,8},{13,9},{20,16},{21,17},{28,24},{29,25}} | collective-permute-start | bytes 1622024 | tf_op jit(solution)/shard_map/ppermute | solution.py:420
  21.6 0.7 collective-permute-start.11
  22.3 29.5 %shard_map.61 = (bf16[384,512]{1,0:T(8,128)(2,1)}, bf16[512,512]{1,0:T(8,128)(2,1)}) custom-call(s32[3]{0:T(128)S(1)} %pad_add_fusion.ids, bf16[512,1024]{1,0:T(8,128)(2,1)} %refs_0_.5), custom_call_target="tpu_custom_call" | custom-call | tf_op jit(solution)/shard_map/pallas_call | solution.py:452
  51.8 0.7 collective-permute-start.8
  52.5 0.0 collective-permute-done.refs_0_
  52.5 0.0 copy-start.3
  52.5 1.8 %collective-permute-start.5 = (bf16[512,1024]{1,0:T(8,128)(2,1)S(1)}, bf16[512,1024]{1,0:T(8,128)(2,1)S(1)}, u32[]{:S(2)}, u32[]{:S(2)}) collective-permute-start(bf16[512,1024]{1,0:T(8,128)(2,1)S(1)} %collective-permute-done.refs_0_), channel_id=1, source_target_pairs={{0,1},{1,0},{2,3},{3,2},{4,5},{5,4},{6,7},{7,6},{8,9},{9,8},{10,11... | collective-permute-start | bytes 3145736 | tf_op jit(solution)/shard_map/ppermute | solution.py:423
  54.3 3.6 %collective-permute-start.6 = (bf16[384,512]{1,0:T(8,128)(2,1)}, bf16[384,512]{1,0:T(8,128)(2,1)S(1)}, u32[]{:S(2)}, u32[]{:S(2)}) collective-permute-start(bf16[384,512]{1,0:T(8,128)(2,1)} %get-tuple-element.36), channel_id=1, source_target_pairs={{2,0},{3,1},{0,2},{1,3},{10,8},{11,9},{8,10},{9,11},{18,16},{19,17... | collective-permute-start | bytes 1179656 | tf_op jit(solution)/shard_map/ppermute | solution.py:420
  57.9 0.0 collective-permute-done.10.at_0
  57.9 0.0 collective-permute-done.11.at_1
  57.9 0.6 shard_map.64.refs_0_
  58.6 0.1 collective-permute-start.12
  58.6 0.0 collective-permute-done.8.refs_4_
  58.6 0.0 copy-start.6
  58.7 6.7 %collective-permute-start.9 = (bf16[512,512]{1,0:T(8,128)(2,1)S(1)}, bf16[512,512]{1,0:T(8,128)(2,1)S(1)}, u32[]{:S(2)}, u32[]{:S(2)}) collective-permute-start(bf16[512,512]{1,0:T(8,128)(2,1)S(1)} %collective-permute-done.8.refs_4_), channel_id=1, source_target_pairs={{0,1},{1,0},{2,3},{3,2},{4,5},{5,4},{6,7},{7,6},{8,9},{9,8},{10,11... | collective-permute-start | bytes 1572872 | tf_op jit(solution)/shard_map/ppermute | solution.py:423
  65.3 3.0 %collective-permute-done.6.refs_2_ = bf16[384,512]{1,0:T(8,128)(2,1)S(1)} collective-permute-done((bf16[384,512]{1,0:T(8,128)(2,1)}, bf16[384,512]{1,0:T(8,128)(2,1)S(1)}, u32[]{:S(2)}, u32[]{:S(2)}) %collective-permute-start.6) | collective-permute-done | bytes 393248 | tf_op jit(solution)/shard_map/ppermute | solution.py:420
  68.3 0.0 copy-start.8
  68.3 2.5 %collective-permute-start.7 = (bf16[384,512]{1,0:T(8,128)(2,1)S(1)}, bf16[384,512]{1,0:T(8,128)(2,1)S(1)}, u32[]{:S(2)}, u32[]{:S(2)}) collective-permute-start(bf16[384,512]{1,0:T(8,128)(2,1)S(1)} %collective-permute-done.6.refs_2_), channel_id=1, source_target_pairs={{0,1},{1,0},{2,3},{3,2},{4,5},{5,4},{6,7},{7,6},{8,9},{9,8},{10,11... | collective-permute-start | bytes 1179656 | tf_op jit(solution)/shard_map/ppermute | solution.py:423
  70.8 1.3 %collective-permute-done.7.refs_3_ = bf16[384,512]{1,0:T(8,128)(2,1)S(1)} collective-permute-done((bf16[384,512]{1,0:T(8,128)(2,1)S(1)}, bf16[384,512]{1,0:T(8,128)(2,1)S(1)}, u32[]{:S(2)}, u32[]{:S(2)}) %collective-permute-start.7) | collective-permute-done | bytes 393248 | tf_op jit(solution)/shard_map/ppermute | solution.py:423
  72.2 0.0 copy-start.9
  72.2 0.0 collective-permute-done.9.refs_5_
  72.2 0.0 copy-done.6
  72.2 0.0 copy-done.8
  72.2 0.7 copy-done.9
  72.9 0.0 copy-start.7
  72.9 0.8 copy-done.7
  73.7 5.0 %shard_map.62 = (bf16[1024,1024]{1,0:T(8,128)(2,1)S(1)}, f32[1024,1024]{1,0:T(8,128)S(1)}, f32[1,1024]{1,0:T(1,128)S(1)}) custom-call(s32[3]{0:T(128)S(1)} %pad_add_fusion.ids, bf16[512,1024]{1,0:T(8,128)(2,1)} %refs_0_.5, bf16[512,1024]{1,0:T(8,128)(2,1)} %copy-done.1, bf16[384,512]{1,0:T(8,128)(2,1)} %copy-done.8, bf16[384,512]{1,0:T(8,128)(2,1)} %copy-done.9, ...), custom_call_target="tpu_custom_call" | custom-call | tf_op jit(solution)/shard_map/pallas_call | solution.py:452
  78.7 0.0 copy-done.3
  78.7 0.0 collective-permute-done.5.refs_1_
  78.7 0.0 copy-start.4
  78.7 1.0 copy-done.4
  79.7 4.1 %shard_map.63 = (bf16[1024,1024]{1,0:T(8,128)(2,1)S(1)}, bf16[1024,1024]{1,0:T(8,128)(2,1)S(1)}, bf16[512,1024]{1,0:T(8,128)(2,1)}, bf16[512,1024]{1,0:T(8,128)(2,1)}) custom-call(s32[3]{0:T(128)S(1)} %pad_add_fusion.ids, bf16[512,1024]{1,0:T(8,128)(2,1)} %copy-done.3, bf16[512,1024]{1,0:T(8,128)(2,1)} %copy-done.4, ...), custom_call_target="tpu_custom_call", output_to_operand_aliasing={{2}: (7, {}), {3}: (8, {})} | custom-call | tf_op jit(solution)/shard_map/pallas_call | solution.py:452
  83.8 0.0 collective-permute-done.12.refs_1_
  83.8 8.1 %shard_map.65 = (bf16[1024,1024]{1,0:T(8,128)(2,1)S(1)}, bf16[1024,1024]{1,0:T(8,128)(2,1)S(1)}, bf16[1024,1024]{1,0:T(8,128)(2,1)S(1)}, bf16[16,1024]{1,0:T(8,128)(2,1)S(1)}) custom-call(s32[3]{0:T(128)S(1)} %pad_add_fusion.ids, bf16[528,512]{1,0:T(8,128)(2,1)S(1)} %shard_map.64.refs_0_, bf16[528,512]{1,0:T(8,128)(2,1)S(1)} %collective-permute-done.12.refs_1_, ...), custom_call_target="tpu_custom_call" | custom-call | tf_op jit(solution)/shard_map/pallas_call | solution.py:452
  91.9 1.3 %collective-permute-start.13 = (bf16[16,1024]{1,0:T(8,128)(2,1)S(1)}, bf16[16,1024]{1,0:T(8,128)(2,1)S(1)}, u32[]{:S(2)}, u32[]{:S(2)}) collective-permute-start(bf16[16,1024]{1,0:T(8,128)(2,1)S(1)} %get-tuple-element.56.mine), channel_id=1, source_target_pairs={{0,4},{1,5},{2,6},{3,7},{8,12},{9,13},{10,14},{11,15},{16,20},{17,... | collective-permute-start | bytes 98312 | tf_op jit(solution)/shard_map/ppermute | solution.py:420
  93.2 0.0 copy-start
  93.2 2.9 %shard_map.66 = (bf16[512,1024]{1,0:T(8,128)(2,1)}, bf16[512,1024]{1,0:T(8,128)(2,1)}) custom-call(s32[3]{0:T(128)S(1)} %pad_add_fusion.ids, bf16[1024,1024]{1,0:T(8,128)(2,1)S(1)} %get-tuple-element.45.refs_4_.coupling_0, f32[512,1024]{1,0:T(8,128)S(1)} %get-tuple-element.33.refs_3_.gram, ...), custom_call_target="tpu_custom_call", output_to_operand_aliasing={{0}: (6, {}), {1}: (7, {})} | custom-call | tf_op jit(solution)/shard_map/pallas_call | solution.py:452
  96.1 0.0 collective-permute-done.13.heard
  96.1 0.0 copy-done
  96.1 0.6 shard_map.67
  96.7 0.6 copy.14
Async XLA Ops:
  0.6 3.1 %collective-permute-start.1 = (bf16[512,1024]{1,0:T(8,128)(2,1)}, bf16[512,1024]{1,0:T(8,128)(2,1)S(1)}, u32[]{:S(2)}, u32[]{:S(2)}) collective-permute-start(bf16[512,1024]{1,0:T(8,128)(2,1)} %refs_0_.5), channel_id=1, source_target_pairs={{0,1},{1,0},{2,3},{3,2},{4,5},{5,4},{6,7},{7,6},{8,9},{9,8},{10,11... | collective-permute-start | bytes 3145736 | tf_op jit(solution)/shard_map/ppermute | solution.py:423
  1.2 4.0 %collective-permute-start.2 = (bf16[512,1024]{1,0:T(8,128)(2,1)}, bf16[512,1024]{1,0:T(8,128)(2,1)S(1)}, u32[]{:S(2)}, u32[]{:S(2)}) collective-permute-start(bf16[512,1024]{1,0:T(8,128)(2,1)} %refs_2_.1), channel_id=1, source_target_pairs={{0,1},{1,0},{2,3},{3,2},{4,5},{5,4},{6,7},{7,6},{8,9},{9,8},{10,11... | collective-permute-start | bytes 3145736 | tf_op jit(solution)/shard_map/ppermute | solution.py:423
  1.3 10.1 %copy-start.2 = (bf16[512,1024]{1,0:T(8,128)(2,1)S(1)}, bf16[512,1024]{1,0:T(8,128)(2,1)}, u32[]{:S(2)}) copy-start(bf16[512,1024]{1,0:T(8,128)(2,1)} %refs_2_.1) | copy-start | bytes 3145732
  3.7 1.5 %copy-start.1 = (bf16[512,1024]{1,0:T(8,128)(2,1)}, bf16[512,1024]{1,0:T(8,128)(2,1)S(1)}, u32[]{:S(2)}) copy-start(bf16[512,1024]{1,0:T(8,128)(2,1)S(1)} %collective-permute-done.1.refs_1_) | copy-start | bytes 3145732
  5.2 1.0 copy-start.5
  10.7 5.5 %collective-permute-start.3 = (bf16[528,512]{1,0:T(8,128)(2,1)S(1)}, bf16[528,512]{1,0:T(8,128)(2,1)S(1)}, u32[]{:S(2)}, u32[]{:S(2)}) collective-permute-start(bf16[528,512]{1,0:T(8,128)(2,1)S(1)} %get-tuple-element.30), channel_id=1, source_target_pairs={{6,4},{7,5},{14,12},{15,13},{22,20},{23,21},{30,28},{31,29}} | collective-permute-start | bytes 1622024 | tf_op jit(solution)/shard_map/ppermute | solution.py:420
  11.4 41.0 %collective-permute-start = (bf16[512,1024]{1,0:T(8,128)(2,1)S(1)}, bf16[512,1024]{1,0:T(8,128)(2,1)S(1)}, u32[]{:S(2)}, u32[]{:S(2)}) collective-permute-start(bf16[512,1024]{1,0:T(8,128)(2,1)S(1)} %copy-done.2), channel_id=1, source_target_pairs={{2,0},{3,1},{0,2},{1,3},{10,8},{11,9},{8,10},{9,11},{18,16},{19,17... | collective-permute-start | bytes 3145736 | tf_op jit(solution)/shard_map/ppermute | solution.py:420
  16.2 3.5 %collective-permute-start.4 = (bf16[528,512]{1,0:T(8,128)(2,1)S(1)}, bf16[528,512]{1,0:T(8,128)(2,1)S(1)}, u32[]{:S(2)}, u32[]{:S(2)}) collective-permute-start(bf16[528,512]{1,0:T(8,128)(2,1)S(1)} %collective-permute-done.3.refs_0_), channel_id=1, source_target_pairs={{0,1},{1,0},{2,3},{3,2},{4,5},{5,4},{6,7},{7,6},{8,9},{9,8},{10,11... | collective-permute-start | bytes 1622024 | tf_op jit(solution)/shard_map/ppermute | solution.py:423
  20.3 37.6 %collective-permute-start.10 = (bf16[528,512]{1,0:T(8,128)(2,1)S(1)}, bf16[528,512]{1,0:T(8,128)(2,1)S(1)}, u32[]{:S(2)}, u32[]{:S(2)}) collective-permute-start(bf16[528,512]{1,0:T(8,128)(2,1)S(1)} %get-tuple-element.34), channel_id=1, source_target_pairs={{4,0},{5,1},{12,8},{13,9},{20,16},{21,17},{28,24},{29,25}} | collective-permute-start | bytes 1622024 | tf_op jit(solution)/shard_map/ppermute | solution.py:420
  21.6 36.3 %collective-permute-start.11 = (bf16[528,512]{1,0:T(8,128)(2,1)S(1)}, bf16[528,512]{1,0:T(8,128)(2,1)S(1)}, u32[]{:S(2)}, u32[]{:S(2)}) collective-permute-start(bf16[528,512]{1,0:T(8,128)(2,1)S(1)} %get-tuple-element.34), channel_id=1, source_target_pairs={{4,2},{5,3},{12,10},{13,11},{20,18},{21,19},{28,26},{29,27}} | collective-permute-start | bytes 1622024 | tf_op jit(solution)/shard_map/ppermute | solution.py:420
  51.8 6.9 %collective-permute-start.8 = (bf16[512,512]{1,0:T(8,128)(2,1)}, bf16[512,512]{1,0:T(8,128)(2,1)S(1)}, u32[]{:S(2)}, u32[]{:S(2)}) collective-permute-start(bf16[512,512]{1,0:T(8,128)(2,1)} %get-tuple-element.38), channel_id=1, source_target_pairs={{3,1},{1,3},{11,9},{9,11},{19,17},{17,19},{27,25},{25,27}} | collective-permute-start | bytes 1572872 | tf_op jit(solution)/shard_map/ppermute | solution.py:420
  52.5 26.2 %copy-start.3 = (bf16[512,1024]{1,0:T(8,128)(2,1)}, bf16[512,1024]{1,0:T(8,128)(2,1)S(1)}, u32[]{:S(2)}) copy-start(bf16[512,1024]{1,0:T(8,128)(2,1)S(1)} %collective-permute-done.refs_0_) | copy-start | bytes 3145732
  52.5 26.2 %collective-permute-start.5 = (bf16[512,1024]{1,0:T(8,128)(2,1)S(1)}, bf16[512,1024]{1,0:T(8,128)(2,1)S(1)}, u32[]{:S(2)}, u32[]{:S(2)}) collective-permute-start(bf16[512,1024]{1,0:T(8,128)(2,1)S(1)} %collective-permute-done.refs_0_), channel_id=1, source_target_pairs={{0,1},{1,0},{2,3},{3,2},{4,5},{5,4},{6,7},{7,6},{8,9},{9,8},{10,11... | collective-permute-start | bytes 3145736 | tf_op jit(solution)/shard_map/ppermute | solution.py:423
  54.3 14.1 %collective-permute-start.6 = (bf16[384,512]{1,0:T(8,128)(2,1)}, bf16[384,512]{1,0:T(8,128)(2,1)S(1)}, u32[]{:S(2)}, u32[]{:S(2)}) collective-permute-start(bf16[384,512]{1,0:T(8,128)(2,1)} %get-tuple-element.36), channel_id=1, source_target_pairs={{2,0},{3,1},{0,2},{1,3},{10,8},{11,9},{8,10},{9,11},{18,16},{19,17... | collective-permute-start | bytes 1179656 | tf_op jit(solution)/shard_map/ppermute | solution.py:420
  58.6 25.2 %collective-permute-start.12 = (bf16[528,512]{1,0:T(8,128)(2,1)S(1)}, bf16[528,512]{1,0:T(8,128)(2,1)S(1)}, u32[]{:S(2)}, u32[]{:S(2)}) collective-permute-start(bf16[528,512]{1,0:T(8,128)(2,1)S(1)} %shard_map.64.refs_0_), channel_id=1, source_target_pairs={{0,1},{1,0},{2,3},{3,2},{4,5},{5,4},{6,7},{7,6},{8,9},{9,8},{10,11... | collective-permute-start | bytes 1622024 | tf_op jit(solution)/shard_map/ppermute | solution.py:423
  58.6 13.5 %copy-start.6 = (bf16[512,512]{1,0:T(8,128)(2,1)}, bf16[512,512]{1,0:T(8,128)(2,1)S(1)}, u32[]{:S(2)}) copy-start(bf16[512,512]{1,0:T(8,128)(2,1)S(1)} %collective-permute-done.8.refs_4_) | copy-start | bytes 1572868
  58.7 13.5 %collective-permute-start.9 = (bf16[512,512]{1,0:T(8,128)(2,1)S(1)}, bf16[512,512]{1,0:T(8,128)(2,1)S(1)}, u32[]{:S(2)}, u32[]{:S(2)}) collective-permute-start(bf16[512,512]{1,0:T(8,128)(2,1)S(1)} %collective-permute-done.8.refs_4_), channel_id=1, source_target_pairs={{0,1},{1,0},{2,3},{3,2},{4,5},{5,4},{6,7},{7,6},{8,9},{9,8},{10,11... | collective-permute-start | bytes 1572872 | tf_op jit(solution)/shard_map/ppermute | solution.py:423
  68.3 3.8 %copy-start.8 = (bf16[384,512]{1,0:T(8,128)(2,1)}, bf16[384,512]{1,0:T(8,128)(2,1)S(1)}, u32[]{:S(2)}) copy-start(bf16[384,512]{1,0:T(8,128)(2,1)S(1)} %collective-permute-done.6.refs_2_) | copy-start | bytes 1179652
  68.3 3.8 %collective-permute-start.7 = (bf16[384,512]{1,0:T(8,128)(2,1)S(1)}, bf16[384,512]{1,0:T(8,128)(2,1)S(1)}, u32[]{:S(2)}, u32[]{:S(2)}) collective-permute-start(bf16[384,512]{1,0:T(8,128)(2,1)S(1)} %collective-permute-done.6.refs_2_), channel_id=1, source_target_pairs={{0,1},{1,0},{2,3},{3,2},{4,5},{5,4},{6,7},{7,6},{8,9},{9,8},{10,11... | collective-permute-start | bytes 1179656 | tf_op jit(solution)/shard_map/ppermute | solution.py:423
  72.2 0.7 copy-start.9
  72.9 0.8 copy-start.7
  78.7 1.0 copy-start.4
  91.9 4.2 %collective-permute-start.13 = (bf16[16,1024]{1,0:T(8,128)(2,1)S(1)}, bf16[16,1024]{1,0:T(8,128)(2,1)S(1)}, u32[]{:S(2)}, u32[]{:S(2)}) collective-permute-start(bf16[16,1024]{1,0:T(8,128)(2,1)S(1)} %get-tuple-element.56.mine), channel_id=1, source_target_pairs={{0,4},{1,5},{2,6},{3,7},{8,12},{9,13},{10,14},{11,15},{16,20},{17,... | collective-permute-start | bytes 98312 | tf_op jit(solution)/shard_map/ppermute | solution.py:420
  93.2 2.9 %copy-start = (s32[4]{0:T(128)S(1)}, s32[4]{0:T(128)}, u32[]{:S(2)}) copy-start(s32[4]{0:T(128)} %owner.1) | copy-start | bytes 52

commit v4 on v3

--- a/solution.py
+++ b/solution.py
@@ -37,27 +37,24 @@
     return r, c
 
 
-def load_rows(target, pieces, start, sems):
-    n = target.shape[0]
-    if len(pieces) == 1:
-        copies = [pltpu.make_async_copy(pieces[0], target, sems.at[0])]
-    else:
-        rows = pieces[0].shape[0]
-        other = n - rows - start
-        copies = [
-            pltpu.make_async_copy(pieces[0], target.at[pl.ds(start, rows)], sems.at[0]),
-            pltpu.make_async_copy(pieces[1], target.at[pl.ds(other, rows)], sems.at[1]),
-        ]
+def couple(target, lowers, factor, start):
+    n = factor.shape[0]
+    half = n // 2
+    rows = lowers[0].shape[0]
+    for lower, at in zip(lowers, (start if rows < n else 0, n - rows - start)):
+        here = pl.ds(pl.multiple_of(at, rows), rows)
+        target[here, :half] = mm(lower[...], factor[:, :half]).astype(BF16)
+        target[here, half:] = mm(lower[:, half:], factor[half:, half:]).astype(BF16)
+
+
+def write_out(values, outs, sems):
+    copies = [
+        pltpu.make_async_copy(v, o, sems.at[i]) for i, (v, o) in enumerate(zip(values, outs))
+    ]
     for copy in copies:
         copy.start()
-    return copies
-
-
-def couple(target, lower, factor):
-    n = factor.shape[0]
-    half = n // 2
-    target[:, :half] = mm(lower[...], factor[:, :half]).astype(BF16)
-    target[:, half:] = mm(lower[:, half:], factor[half:, half:]).astype(BF16)
+    for copy in copies:
+        copy.wait()
 
 
 def tile_diag(tile):
@@ -192,71 +189,66 @@
     return copies + [pltpu.make_async_copy(crosses[0], low, sems.at[len(moves)])]
 
 
+def place(target, pieces, start):
+    n = target.shape[0]
+    if len(pieces) == 1:
+        target[...] = pieces[0][...]
+        return
+    rows = pieces[0].shape[0]
+    for piece, at in zip(pieces, (start, n - rows - start)):
+        target[pl.ds(pl.multiple_of(at, rows), rows), :] = piece[...]
+
+
+def gram_kernel(pieces, ids, *refs):
+    pieces, (factor, gram) = refs[:pieces], refs[pieces:]
+    rows, n = gram.shape
+    half = n // 2
+    start = pl.multiple_of(ids[0], rows)
+    own = pl.ds(start, rows)
+    place(factor, pieces, start)
+    gram[:, :half] = mm_t(factor[:, own], factor[:, :half])
+    gram[:, half:] = mm_t(factor[half:, own], factor[half:, half:])
+
+
 def first_kernel(pieces, paired, ids, *refs):
-    factors, lowers = refs[:pieces], refs[pieces : 2 * pieces]
-    coupling, packet, cov, factor, lower, total, sems = refs[2 * pieces :]
+    lowers = refs[:pieces]
+    factor, gram, coupling, packet, cov = refs[pieces:]
+    rows, n = cov.shape
+    start = pl.multiple_of(ids[0], rows)
+    block = ids[1]
+    couple(coupling, lowers, factor, start)
+
+    @pl.when(block == TB - 1)
+    def _():
+        own = pl.ds(start, rows)
+        cov[...] = (gram[...] + mm_t(coupling[:, own], coupling[...])).astype(BF16)
+        pack(packet, cov, start, jnp.zeros((1, n), F32), paired)
+
+
+def heard_kernel(parts, paired, ids, *refs):
+    parts, rest = refs[:parts], refs[parts:]
+    (factor, coupling, cov, heard, gram_1, diag_0, off_out, cov_out,
+     off, sems, out_sems) = rest
     rows = cov.shape[0]
     start = pl.multiple_of(ids[0], rows)
-    block = ids[1]
-    copies = load_rows(factor, factors, start, sems.at[0])
-    copies += load_rows(lower, lowers, start, sems.at[1])
-    for copy in copies:
-        copy.wait()
-    couple(coupling, lower, factor)
-
-    @pl.when(block == TB - 1)
-    def _():
-        own = pl.ds(start, rows)
-        total[...] = mm_t(factor[:, own], factor[...])
-        cov[...] = (total[...] + mm_t(coupling[:, own], coupling[...])).astype(BF16)
-        pack(packet, cov, start, jnp.zeros((1, factor.shape[1]), F32), paired)
-
-
-def gram_kernel(pieces, ids, *refs):
-    factors = refs[:pieces]
-    coupling, cov, gram, off_out, cov_out, factor, off, sems, out_sems = refs[pieces:]
-    rows = cov.shape[0]
-    start = pl.multiple_of(ids[0], rows)
-    block = ids[1]
-    copies = load_rows(factor, factors, start, sems.at[0])
-    for copy in copies:
-        copy.wait()
-    gram[...] = mm_t(factor[:, pl.ds(start, rows)], factor[...])
-
-    @pl.when(block == TB - 1)
-    def _():
-        off[...] = -coupling[pl.ds(start, rows), :]
-        one = pltpu.make_async_copy(off, off_out, out_sems.at[0])
-        two = pltpu.make_async_copy(cov, cov_out, out_sems.at[1])
-        one.start()
-        two.start()
-        one.wait()
-        two.wait()
-
-
-def heard_kernel(pieces, paired, ids, *refs):
-    factors = refs[:pieces]
-    parts = refs[pieces : len(refs) - 5]
-    heard, gram_1, diag_0, factor, sems = refs[len(refs) - 5 :]
-    rows = factors[0].shape[0] if paired else factor.shape[0]
-    start = pl.multiple_of(ids[0], TILE)
-    if paired:
-        start = pl.multiple_of(ids[0], rows)
     block = ids[1]
 
     def finish(factor_1, factor_0):
         gram_1[...] = mm_t(factor_1[...], factor_1[...])
         diag_0[...] = jnp.sum(jnp.square(factor_0[...].astype(F32)), axis=0, keepdims=True)
 
+    @pl.when(block == TB - 1)
+    def _():
+        off[...] = -coupling[pl.ds(start, rows), :]
+        write_out((off, cov), (off_out, cov_out), out_sems)
+
     @pl.when(block < 2)
     def _():
-        copies = load_rows(factor, factors, start, sems.at[0])
         if paired:
-            copies += unfold(heard, parts[:2], parts[2:], start, sems.at[1])
+            for copy in unfold(heard, parts[:2], parts[2:], start, sems):
+                copy.wait()
         else:
-            copies += load_rows(heard, parts, start, sems.at[1])
-        for copy in copies:
-            copy.wait()
+            place(heard, parts, start)
 
         @pl.when(block == 0)
         def _():
@@ -285,42 +277,24 @@
 def ready_kernel(pieces, ids, *refs):
     lowers = refs[:pieces]
     (heard, coupling, off, cov, _, _, coupling_1, coupling_0, off_out, cov_out,
-     lower, sems, out_sems) = refs[pieces:]
+     out_sems) = refs[pieces:]
     rows = cov.shape[0]
     start = pl.multiple_of(ids[0], rows)
     block = ids[1]
 
     @pl.when(block == TB - 2)
     def _():
-        one = pltpu.make_async_copy(off.at[pl.ds(start, rows)], off_out, out_sems.at[0])
-        two = pltpu.make_async_copy(cov, cov_out, out_sems.at[1])
-        one.start()
-        two.start()
-        one.wait()
-        two.wait()
-
-    @pl.when(block < 2)
-    def _():
-        copies = load_rows(lower, lowers, start, sems.at[0])
-
-        @pl.when(block == 0)
-        def _():
-            coupling_0[...] = coupling[...]
-
-        @pl.when(block == 1)
-        def _():
-            coupling_1[...] = coupling[...]
-
-        for copy in copies:
-            copy.wait()
-
-        @pl.when(block == 0)
-        def _():
-            couple(coupling_1, lower, heard)
-
-        @pl.when(block == 1)
-        def _():
-            couple(coupling_0, lower, heard)
+        write_out((off.at[pl.ds(start, rows)], cov), (off_out, cov_out), out_sems)
+
+    @pl.when(block == 0)
+    def _():
+        coupling_0[...] = coupling[...]
+        couple(coupling_1, lowers, heard, start)
+
+    @pl.when(block == 1)
+    def _():
+        coupling_1[...] = coupling[...]
+        couple(coupling_0, lowers, heard, start)
 
 
 def merge_kernel(ids, at_0, at_1, out, sem):
@@ -475,7 +449,7 @@
     if paired:
         folded, cross = call(
             fold_kernel,
-            [(HBM, (rows * 3 // 4, rows), BF16), (HBM, (rows, rows), BF16)],
+            [(VMEM, (rows * 3 // 4, rows), BF16), (VMEM, (rows, rows), BF16)],
             [ids, linv],
             [SMEM, HBM],
             [sems(4)],
@@ -485,29 +459,29 @@
         raw = [block_to_block(linv, swap)]
     raw_lower = block_to_block(sub, swap)
 
+    factor, gram = call(
+        functools.partial(gram_kernel, pieces),
+        [whole, (VMEM, (rows, n), F32)],
+        [ids, *factors],
+        [SMEM] + [VMEM] * pieces,
+        [],
+    )
     coupling, packet, cov_3 = call(
         functools.partial(first_kernel, pieces, paired),
         [whole, (VMEM, packet_shape, BF16), part],
-        [ids, *factors, *lowers],
-        [SMEM] + [HBM] * (2 * pieces),
-        [square, square, pltpu.VMEM((rows, n), F32), sems(2, 2)],
+        [ids, *lowers, factor, gram],
+        [SMEM] + [VMEM] * (pieces + 2),
+        [],
     )
     packet_2 = block_to_block(packet, [(3, 2)])
 
-    gram, off_rows, cov_rows = call(
-        functools.partial(gram_kernel, pieces),
-        [(VMEM, (rows, n), F32), out_rows, out_rows],
-        [ids, *factors, coupling, cov_3],
-        [SMEM] + [HBM] * pieces + [VMEM, VMEM],
-        [square, pltpu.VMEM((rows, n), BF16), sems(1, 2), sems(2)],
-    )
-    parts = [x for piece in raw for x in pieces_of(after(piece, gram))]
-    heard_factor, gram_1, diag_0 = call(
-        functools.partial(heard_kernel, pieces, paired),
-        [whole, (VMEM, (n, n), F32), (VMEM, (1, n), F32)],
-        [ids, *factors, *parts],
-        [SMEM] + [HBM] * (pieces + len(parts)),
-        [square, sems(2, 8)],
+    parts = [x for piece in raw for x in pieces_of(after(piece, packet))]
+    heard_factor, gram_1, diag_0, off_rows, cov_rows = call(
+        functools.partial(heard_kernel, len(parts), paired),
+        [whole, (VMEM, (n, n), F32), (VMEM, (1, n), F32), out_rows, out_rows],
+        [ids, *parts, factor, coupling, cov_3],
+        [SMEM] + [VMEM] * (len(parts) + 3),
+        [pltpu.VMEM((rows, n), BF16), sems(8), sems(2)],
     )
 
     packet, off_2, cov_2 = call(
@@ -525,8 +499,8 @@
         functools.partial(ready_kernel, pieces),
         [whole, whole, out_rows, out_rows],
         [ids, *raw_lowers, heard_factor, coupling, off_2, cov_2, off_rows, cov_rows],
-        [SMEM] + [HBM] * pieces + [VMEM] * 4 + [HBM, HBM],
-        [square, sems(1, 2), sems(2)],
+        [SMEM] + [VMEM] * (pieces + 4) + [HBM, HBM],
+        [sems(2)],
         {pieces + 5: 2, pieces + 6: 3},
     )
 

time: 97.6 us -> 76.6 us (0.78)
  Pallas kernels: 59.2 us -> 24.5 us
  waiting for transfers between devices: 8.23 us -> 31.5 us
  starting transfers between devices: 24.8 us -> 14.6 us
    pallas_call x10, Pallas kernels: 59.2 us -> 24.5 us  [call(): pl.pallas_call(kernel, out_shape=shapes, in_specs=list(spaces), out_specs...]
    ppermute x7, waiting for transfers between devices: 3.03 us -> 25.5 us  [block_to_block(): return lax.ppermute(values, 'tm', pairs)]
    ppermute x7, starting transfers between devices: 11.7 us -> 1.28 us  [peer(): return lax.ppermute(piece, 'tm', [(i, i ^ step) for i in range(TB * group)])]
    unnamed x21 -> x11, local copies, waits for them, and re-layouts: 4.06 us -> 4.75 us
  transfers between devices with their start and end apart: 14 -> 14, of which waited for: 4 -> 6; matrix products, arithmetic and copies ran while one was open for 0% -> 0% of each run, Pallas kernels for 47% -> 18%
where the time goes in v4:
time: 76.6 us; the launch traced here: 76.2 us
  waiting for transfers between devices  31.5 us (41%)
  Pallas kernels  24.5 us (32%)
  starting transfers between devices  14.6 us (19%)
  local copies, waits for them, and re-layouts  4.75 us (6%)
  between operations  0.85 us (1%)
    ppermute x7, waiting for transfers between devices, block_to_block(): return lax.ppermute(values, 'tm', pairs)  25.5 us
    pallas_call x10, Pallas kernels, call(): pl.pallas_call(kernel, out_shape=shapes, in_specs=list(spaces), out_specs...  24.5 us
    ppermute x7, starting transfers between devices, block_to_block(): return lax.ppermute(values, 'tm', pairs)  13.3 us
    ppermute x7, waiting for transfers between devices, peer(): return lax.ppermute(piece, 'tm', [(i, i ^ step) for i in range(TB * group)])  5.99 us
    unnamed x11, local copies, waits for them, and re-layouts  4.75 us
  transfers between devices with their start and end apart: 14, of which 6 were waited for; matrix products, arithmetic and copies ran while one was open for 0% of the time, Pallas kernels for 18%

profile of v4, /device:TPU:0, one launch (start us, length us, event | category | flops | bytes accessed | tf_op | source)
XLA Modules:
  0.0 76.2 jit_solution(13478465925432487392)
XLA Ops:
  0.6 0.6 collective-permute-start.2
  1.2 0.1 collective-permute-start.1
  1.3 0.1 pad_add_fusion.ids
  1.3 2.3 %collective-permute-done.2.refs_1_ = bf16[512,1024]{1,0:T(8,128)(2,1)S(1)} collective-permute-done((bf16[512,1024]{1,0:T(8,128)(2,1)}, bf16[512,1024]{1,0:T(8,128)(2,1)S(1)}, u32[]{:S(2)}, u32[]{:S(2)}) %collective-permute-start.2) | collective-permute-done | bytes 1048608 | tf_op jit(solution)/shard_map/ppermute | solution.py:397
  3.7 0.0 copy-start
  3.7 1.2 %copy-done = bf16[512,1024]{1,0:T(8,128)(2,1)S(1)} copy-done((bf16[512,1024]{1,0:T(8,128)(2,1)S(1)}, bf16[512,1024]{1,0:T(8,128)(2,1)}, u32[]{:S(2)}) %copy-start) | copy-done | bytes 1048600
  4.9 0.0 copy-start.3
  4.9 1.7 %shard_map.58 = (bf16[1024,1024]{1,0:T(8,128)(2,1)S(1)}, f32[512,1024]{1,0:T(8,128)S(1)}) custom-call(s32[3]{0:T(128)S(1)} %pad_add_fusion.ids, bf16[512,1024]{1,0:T(8,128)(2,1)S(1)} %copy-done, bf16[512,1024]{1,0:T(8,128)(2,1)S(1)} %collective-permute-done.2.refs_1_), custom_call_target="tpu_custom_call" | custom-call | tf_op jit(solution)/shard_map/pallas_call | solution.py:426
  6.6 0.0 collective-permute-done.1.refs_1_
  6.6 0.0 copy-done.3
  6.6 2.3 %shard_map.59 = (bf16[1024,1024]{1,0:T(8,128)(2,1)S(1)}, bf16[528,512]{1,0:T(8,128)(2,1)S(1)}, bf16[512,1024]{1,0:T(8,128)(2,1)S(1)}) custom-call(s32[3]{0:T(128)S(1)} %pad_add_fusion.ids, bf16[512,1024]{1,0:T(8,128)(2,1)S(1)} %copy-done.3, bf16[512,1024]{1,0:T(8,128)(2,1)S(1)} %collective-permute-done.1.refs_1_, ...), custom_call_target="tpu_custom_call" | custom-call | tf_op jit(solution)/shard_map/pallas_call | solution.py:426
  9.0 0.7 collective-permute-start.3
  9.7 4.8 %collective-permute-start = (bf16[512,1024]{1,0:T(8,128)(2,1)S(1)}, bf16[512,1024]{1,0:T(8,128)(2,1)S(1)}, u32[]{:S(2)}, u32[]{:S(2)}) collective-permute-start(bf16[512,1024]{1,0:T(8,128)(2,1)S(1)} %copy-done.3), channel_id=1, source_target_pairs={{2,0},{3,1},{0,2},{1,3},{10,8},{11,9},{8,10},{9,11},{18,16},{19,17... | collective-permute-start | bytes 3145736 | tf_op jit(solution)/shard_map/ppermute | solution.py:394
  14.5 0.0 collective-permute-done.3.refs_0_
  14.5 0.1 collective-permute-start.4
  14.5 1.9 %collective-permute-done.4.refs_1_ = bf16[528,512]{1,0:T(8,128)(2,1)S(1)} collective-permute-done((bf16[528,512]{1,0:T(8,128)(2,1)S(1)}, bf16[528,512]{1,0:T(8,128)(2,1)S(1)}, u32[]{:S(2)}, u32[]{:S(2)}) %collective-permute-start.4) | collective-permute-done | bytes 540704 | tf_op jit(solution)/shard_map/ppermute | solution.py:397
  16.5 0.5 shard_map.60
  17.0 1.3 %collective-permute-start.10 = (bf16[528,512]{1,0:T(8,128)(2,1)S(1)}, bf16[528,512]{1,0:T(8,128)(2,1)S(1)}, u32[]{:S(2)}, u32[]{:S(2)}) collective-permute-start(bf16[528,512]{1,0:T(8,128)(2,1)S(1)} %get-tuple-element.35), channel_id=1, source_target_pairs={{4,0},{5,1},{12,8},{13,9},{20,16},{21,17},{28,24},{29,25}} | collective-permute-start | bytes 1622024 | tf_op jit(solution)/shard_map/ppermute | solution.py:394
  18.3 0.7 collective-permute-start.11
  19.0 1.8 %shard_map.61 = (bf16[384,512]{1,0:T(8,128)(2,1)S(1)}, bf16[512,512]{1,0:T(8,128)(2,1)S(1)}) custom-call(s32[3]{0:T(128)S(1)} %pad_add_fusion.ids, bf16[512,1024]{1,0:T(8,128)(2,1)} %factor.1), custom_call_target="tpu_custom_call" | custom-call | tf_op jit(solution)/shard_map/pallas_call | solution.py:426
  20.8 0.7 collective-permute-start.8
  21.5 16.9 %collective-permute-done.refs_0_ = bf16[512,1024]{1,0:T(8,128)(2,1)S(1)} collective-permute-done((bf16[512,1024]{1,0:T(8,128)(2,1)S(1)}, bf16[512,1024]{1,0:T(8,128)(2,1)S(1)}, u32[]{:S(2)}, u32[]{:S(2)}) %collective-permute-start) | collective-permute-done | bytes 1048608 | tf_op jit(solution)/shard_map/ppermute | solution.py:394
  38.4 0.0 collective-permute-start.5
  38.5 3.9 %collective-permute-start.6 = (bf16[384,512]{1,0:T(8,128)(2,1)S(1)}, bf16[384,512]{1,0:T(8,128)(2,1)S(1)}, u32[]{:S(2)}, u32[]{:S(2)}) collective-permute-start(bf16[384,512]{1,0:T(8,128)(2,1)S(1)} %get-tuple-element.37), channel_id=1, source_target_pairs={{2,0},{3,1},{0,2},{1,3},{10,8},{11,9},{8,10},{9,11},{18,16},{19,17... | collective-permute-start | bytes 1179656 | tf_op jit(solution)/shard_map/ppermute | solution.py:394
  42.4 7.1 %collective-permute-done.10.at_0 = bf16[528,512]{1,0:T(8,128)(2,1)S(1)} collective-permute-done((bf16[528,512]{1,0:T(8,128)(2,1)S(1)}, bf16[528,512]{1,0:T(8,128)(2,1)S(1)}, u32[]{:S(2)}, u32[]{:S(2)}) %collective-permute-start.10) | collective-permute-done | bytes 540704 | tf_op jit(solution)/shard_map/ppermute | solution.py:394
  49.4 0.0 collective-permute-done.11.at_1
  49.4 0.6 shard_map.64.refs_0_
  50.1 0.1 collective-permute-start.12
  50.1 0.0 collective-permute-done.8.refs_2_
  50.2 0.5 collective-permute-start.9
  50.6 1.5 %collective-permute-done.6.refs_0_ = bf16[384,512]{1,0:T(8,128)(2,1)S(1)} collective-permute-done((bf16[384,512]{1,0:T(8,128)(2,1)S(1)}, bf16[384,512]{1,0:T(8,128)(2,1)S(1)}, u32[]{:S(2)}, u32[]{:S(2)}) %collective-permute-start.6) | collective-permute-done | bytes 393248 | tf_op jit(solution)/shard_map/ppermute | solution.py:394
  52.1 0.0 collective-permute-start.7
  52.1 1.7 %collective-permute-done.7.refs_1_ = bf16[384,512]{1,0:T(8,128)(2,1)S(1)} collective-permute-done((bf16[384,512]{1,0:T(8,128)(2,1)S(1)}, bf16[384,512]{1,0:T(8,128)(2,1)S(1)}, u32[]{:S(2)}, u32[]{:S(2)}) %collective-permute-start.7) | collective-permute-done | bytes 393248 | tf_op jit(solution)/shard_map/ppermute | solution.py:397
  53.9 0.0 collective-permute-done.9.refs_3_
  53.9 3.2 %shard_map.62 = (bf16[1024,1024]{1,0:T(8,128)(2,1)S(1)}, f32[1024,1024]{1,0:T(8,128)S(1)}, f32[1,1024]{1,0:T(1,128)S(1)}, bf16[512,1024]{1,0:T(8,128)(2,1)}, bf16[512,1024]{1,0:T(8,128)(2,1)}) custom-call(s32[3]{0:T(128)S(1)} %pad_add_fusion.ids, bf16[384,512]{1,0:T(8,128)(2,1)S(1)} %collective-permute-done.6.refs_0_, ...), custom_call_target="tpu_custom_call" | custom-call | tf_op jit(solution)/shard_map/pallas_call | solution.py:426
  57.1 0.0 collective-permute-done.5.refs_1_
  57.1 2.7 %shard_map.63 = (bf16[1024,1024]{1,0:T(8,128)(2,1)S(1)}, bf16[1024,1024]{1,0:T(8,128)(2,1)S(1)}, bf16[512,1024]{1,0:T(8,128)(2,1)}, bf16[512,1024]{1,0:T(8,128)(2,1)}) custom-call(s32[3]{0:T(128)S(1)} %pad_add_fusion.ids, bf16[512,1024]{1,0:T(8,128)(2,1)S(1)} %collective-permute-done.refs_0_, ...), custom_call_target="tpu_custom_call", output_to_operand_aliasing={{2}: (7, {}), {3}: (8, {})} | custom-call | tf_op jit(solution)/shard_map/pallas_call | solution.py:426
  59.8 0.0 copy-start.1
  59.8 1.3 %copy-done.1 = bf16[1024,1024]{1,0:T(8,128)(2,1)} copy-done((bf16[1024,1024]{1,0:T(8,128)(2,1)}, bf16[1024,1024]{1,0:T(8,128)(2,1)S(1)}, u32[]{:S(2)}) %copy-start.1) | copy-done | bytes 2097176
  61.2 0.0 collective-permute-done.12.refs_1_
  61.2 0.0 copy-start.2
  61.2 1.6 %copy-done.2 = bf16[1024,1024]{1,0:T(8,128)(2,1)S(1)} copy-done((bf16[1024,1024]{1,0:T(8,128)(2,1)S(1)}, bf16[1024,1024]{1,0:T(8,128)(2,1)}, u32[]{:S(2)}) %copy-start.2) | copy-done | bytes 2097176
  62.8 8.1 %shard_map.65 = (bf16[1024,1024]{1,0:T(8,128)(2,1)S(1)}, bf16[1024,1024]{1,0:T(8,128)(2,1)S(1)}, bf16[1024,1024]{1,0:T(8,128)(2,1)S(1)}, bf16[16,1024]{1,0:T(8,128)(2,1)S(1)}) custom-call(s32[3]{0:T(128)S(1)} %pad_add_fusion.ids, bf16[528,512]{1,0:T(8,128)(2,1)S(1)} %shard_map.64.refs_0_, bf16[528,512]{1,0:T(8,128)(2,1)S(1)} %collective-permute-done.12.refs_1_, ...), custom_call_target="tpu_custom_call" | custom-call | tf_op jit(solution)/shard_map/pallas_call | solution.py:426
  70.9 1.3 %collective-permute-start.13 = (bf16[16,1024]{1,0:T(8,128)(2,1)S(1)}, bf16[16,1024]{1,0:T(8,128)(2,1)S(1)}, u32[]{:S(2)}, u32[]{:S(2)}) collective-permute-start(bf16[16,1024]{1,0:T(8,128)(2,1)S(1)} %get-tuple-element.58.mine), channel_id=1, source_target_pairs={{0,4},{1,5},{2,6},{3,7},{8,12},{9,13},{10,14},{11,15},{16,20},{17,... | collective-permute-start | bytes 98312 | tf_op jit(solution)/shard_map/ppermute | solution.py:394
  72.2 0.0 copy-start.4
  72.2 2.9 %shard_map.66 = (bf16[512,1024]{1,0:T(8,128)(2,1)}, bf16[512,1024]{1,0:T(8,128)(2,1)}) custom-call(s32[3]{0:T(128)S(1)} %pad_add_fusion.ids, bf16[1024,1024]{1,0:T(8,128)(2,1)S(1)} %get-tuple-element.47.refs_4_.coupling_0, f32[512,1024]{1,0:T(8,128)S(1)} %get-tuple-element.32.refs_3_.gram, ...), custom_call_target="tpu_custom_call", output_to_operand_aliasing={{0}: (6, {}), {1}: (7, {})} | custom-call | tf_op jit(solution)/shard_map/pallas_call | solution.py:426
  75.0 0.0 collective-permute-done.13.heard
  75.0 0.0 copy-done.4
  75.1 0.6 shard_map.67
  75.6 0.6 copy.14
Async XLA Ops:
  0.6 3.1 %collective-permute-start.2 = (bf16[512,1024]{1,0:T(8,128)(2,1)}, bf16[512,1024]{1,0:T(8,128)(2,1)S(1)}, u32[]{:S(2)}, u32[]{:S(2)}) collective-permute-start(bf16[512,1024]{1,0:T(8,128)(2,1)} %factor.1), channel_id=1, source_target_pairs={{0,1},{1,0},{2,3},{3,2},{4,5},{5,4},{6,7},{7,6},{8,9},{9,8},{10,11... | collective-permute-start | bytes 3145736 | tf_op jit(solution)/shard_map/ppermute | solution.py:397
  1.2 5.4 %collective-permute-start.1 = (bf16[512,1024]{1,0:T(8,128)(2,1)}, bf16[512,1024]{1,0:T(8,128)(2,1)S(1)}, u32[]{:S(2)}, u32[]{:S(2)}) collective-permute-start(bf16[512,1024]{1,0:T(8,128)(2,1)} %refs_0_.3), channel_id=1, source_target_pairs={{0,1},{1,0},{2,3},{3,2},{4,5},{5,4},{6,7},{7,6},{8,9},{9,8},{10,11... | collective-permute-start | bytes 3145736 | tf_op jit(solution)/shard_map/ppermute | solution.py:397
  3.7 1.2 %copy-start = (bf16[512,1024]{1,0:T(8,128)(2,1)S(1)}, bf16[512,1024]{1,0:T(8,128)(2,1)}, u32[]{:S(2)}) copy-start(bf16[512,1024]{1,0:T(8,128)(2,1)} %factor.1) | copy-start | bytes 3145732
  4.9 1.7 %copy-start.3 = (bf16[512,1024]{1,0:T(8,128)(2,1)S(1)}, bf16[512,1024]{1,0:T(8,128)(2,1)}, u32[]{:S(2)}) copy-start(bf16[512,1024]{1,0:T(8,128)(2,1)} %refs_0_.3) | copy-start | bytes 3145732
  9.0 5.5 %collective-permute-start.3 = (bf16[528,512]{1,0:T(8,128)(2,1)S(1)}, bf16[528,512]{1,0:T(8,128)(2,1)S(1)}, u32[]{:S(2)}, u32[]{:S(2)}) collective-permute-start(bf16[528,512]{1,0:T(8,128)(2,1)S(1)} %get-tuple-element.33), channel_id=1, source_target_pairs={{6,4},{7,5},{14,12},{15,13},{22,20},{23,21},{30,28},{31,29}} | collective-permute-start | bytes 1622024 | tf_op jit(solution)/shard_map/ppermute | solution.py:394
  9.7 28.8 %collective-permute-start = (bf16[512,1024]{1,0:T(8,128)(2,1)S(1)}, bf16[512,1024]{1,0:T(8,128)(2,1)S(1)}, u32[]{:S(2)}, u32[]{:S(2)}) collective-permute-start(bf16[512,1024]{1,0:T(8,128)(2,1)S(1)} %copy-done.3), channel_id=1, source_target_pairs={{2,0},{3,1},{0,2},{1,3},{10,8},{11,9},{8,10},{9,11},{18,16},{19,17... | collective-permute-start | bytes 3145736 | tf_op jit(solution)/shard_map/ppermute | solution.py:394
  14.5 2.0 %collective-permute-start.4 = (bf16[528,512]{1,0:T(8,128)(2,1)S(1)}, bf16[528,512]{1,0:T(8,128)(2,1)S(1)}, u32[]{:S(2)}, u32[]{:S(2)}) collective-permute-start(bf16[528,512]{1,0:T(8,128)(2,1)S(1)} %collective-permute-done.3.refs_0_), channel_id=1, source_target_pairs={{0,1},{1,0},{2,3},{3,2},{4,5},{5,4},{6,7},{7,6},{8,9},{9,8},{10,11... | collective-permute-start | bytes 1622024 | tf_op jit(solution)/shard_map/ppermute | solution.py:397
  17.0 32.4 %collective-permute-start.10 = (bf16[528,512]{1,0:T(8,128)(2,1)S(1)}, bf16[528,512]{1,0:T(8,128)(2,1)S(1)}, u32[]{:S(2)}, u32[]{:S(2)}) collective-permute-start(bf16[528,512]{1,0:T(8,128)(2,1)S(1)} %get-tuple-element.35), channel_id=1, source_target_pairs={{4,0},{5,1},{12,8},{13,9},{20,16},{21,17},{28,24},{29,25}} | collective-permute-start | bytes 1622024 | tf_op jit(solution)/shard_map/ppermute | solution.py:394
  18.3 31.1 %collective-permute-start.11 = (bf16[528,512]{1,0:T(8,128)(2,1)S(1)}, bf16[528,512]{1,0:T(8,128)(2,1)S(1)}, u32[]{:S(2)}, u32[]{:S(2)}) collective-permute-start(bf16[528,512]{1,0:T(8,128)(2,1)S(1)} %get-tuple-element.35), channel_id=1, source_target_pairs={{4,2},{5,3},{12,10},{13,11},{20,18},{21,19},{28,26},{29,27}} | collective-permute-start | bytes 1622024 | tf_op jit(solution)/shard_map/ppermute | solution.py:394
  20.8 29.3 %collective-permute-start.8 = (bf16[512,512]{1,0:T(8,128)(2,1)S(1)}, bf16[512,512]{1,0:T(8,128)(2,1)S(1)}, u32[]{:S(2)}, u32[]{:S(2)}) collective-permute-start(bf16[512,512]{1,0:T(8,128)(2,1)S(1)} %get-tuple-element.39), channel_id=1, source_target_pairs={{3,1},{1,3},{11,9},{9,11},{19,17},{17,19},{27,25},{25,27}} | collective-permute-start | bytes 1572872 | tf_op jit(solution)/shard_map/ppermute | solution.py:394
  38.4 18.7 %collective-permute-start.5 = (bf16[512,1024]{1,0:T(8,128)(2,1)S(1)}, bf16[512,1024]{1,0:T(8,128)(2,1)S(1)}, u32[]{:S(2)}, u32[]{:S(2)}) collective-permute-start(bf16[512,1024]{1,0:T(8,128)(2,1)S(1)} %collective-permute-done.refs_0_), channel_id=1, source_target_pairs={{0,1},{1,0},{2,3},{3,2},{4,5},{5,4},{6,7},{7,6},{8,9},{9,8},{10,11... | collective-permute-start | bytes 3145736 | tf_op jit(solution)/shard_map/ppermute | solution.py:397
  38.5 13.7 %collective-permute-start.6 = (bf16[384,512]{1,0:T(8,128)(2,1)S(1)}, bf16[384,512]{1,0:T(8,128)(2,1)S(1)}, u32[]{:S(2)}, u32[]{:S(2)}) collective-permute-start(bf16[384,512]{1,0:T(8,128)(2,1)S(1)} %get-tuple-element.37), channel_id=1, source_target_pairs={{2,0},{3,1},{0,2},{1,3},{10,8},{11,9},{8,10},{9,11},{18,16},{19,17... | collective-permute-start | bytes 1179656 | tf_op jit(solution)/shard_map/ppermute | solution.py:394
  50.1 11.1 %collective-permute-start.12 = (bf16[528,512]{1,0:T(8,128)(2,1)S(1)}, bf16[528,512]{1,0:T(8,128)(2,1)S(1)}, u32[]{:S(2)}, u32[]{:S(2)}) collective-permute-start(bf16[528,512]{1,0:T(8,128)(2,1)S(1)} %shard_map.64.refs_0_), channel_id=1, source_target_pairs={{0,1},{1,0},{2,3},{3,2},{4,5},{5,4},{6,7},{7,6},{8,9},{9,8},{10,11... | collective-permute-start | bytes 1622024 | tf_op jit(solution)/shard_map/ppermute | solution.py:397
  50.2 3.7 %collective-permute-start.9 = (bf16[512,512]{1,0:T(8,128)(2,1)S(1)}, bf16[512,512]{1,0:T(8,128)(2,1)S(1)}, u32[]{:S(2)}, u32[]{:S(2)}) collective-permute-start(bf16[512,512]{1,0:T(8,128)(2,1)S(1)} %collective-permute-done.8.refs_2_), channel_id=1, source_target_pairs={{0,1},{1,0},{2,3},{3,2},{4,5},{5,4},{6,7},{7,6},{8,9},{9,8},{10,11... | collective-permute-start | bytes 1572872 | tf_op jit(solution)/shard_map/ppermute | solution.py:397
  52.1 1.7 %collective-permute-start.7 = (bf16[384,512]{1,0:T(8,128)(2,1)S(1)}, bf16[384,512]{1,0:T(8,128)(2,1)S(1)}, u32[]{:S(2)}, u32[]{:S(2)}) collective-permute-start(bf16[384,512]{1,0:T(8,128)(2,1)S(1)} %collective-permute-done.6.refs_0_), channel_id=1, source_target_pairs={{0,1},{1,0},{2,3},{3,2},{4,5},{5,4},{6,7},{7,6},{8,9},{9,8},{10,11... | collective-permute-start | bytes 1179656 | tf_op jit(solution)/shard_map/ppermute | solution.py:397
  59.8 1.3 %copy-start.1 = (bf16[1024,1024]{1,0:T(8,128)(2,1)}, bf16[1024,1024]{1,0:T(8,128)(2,1)S(1)}, u32[]{:S(2)}) copy-start(bf16[1024,1024]{1,0:T(8,128)(2,1)S(1)} %get-tuple-element.48.refs_2_) | copy-start | bytes 6291460
  61.2 1.6 %copy-start.2 = (bf16[1024,1024]{1,0:T(8,128)(2,1)S(1)}, bf16[1024,1024]{1,0:T(8,128)(2,1)}, u32[]{:S(2)}) copy-start(bf16[1024,1024]{1,0:T(8,128)(2,1)} %copy-done.1) | copy-start | bytes 6291460
  70.9 4.2 %collective-permute-start.13 = (bf16[16,1024]{1,0:T(8,128)(2,1)S(1)}, bf16[16,1024]{1,0:T(8,128)(2,1)S(1)}, u32[]{:S(2)}, u32[]{:S(2)}) collective-permute-start(bf16[16,1024]{1,0:T(8,128)(2,1)S(1)} %get-tuple-element.58.mine), channel_id=1, source_target_pairs={{0,4},{1,5},{2,6},{3,7},{8,12},{9,13},{10,14},{11,15},{16,20},{17,... | collective-permute-start | bytes 98312 | tf_op jit(solution)/shard_map/ppermute | solution.py:394
  72.2 2.9 %copy-start.4 = (s32[4]{0:T(128)S(1)}, s32[4]{0:T(128)}, u32[]{:S(2)}) copy-start(s32[4]{0:T(128)} %owner.1) | copy-start | bytes 52

commit v5 on v4

v5 whole, which is shorter than its diff:
```python
import functools

import jax
import jax.numpy as jnp
from jax import lax
from jax.experimental import pallas as pl
from jax.experimental.pallas import tpu as pltpu
from jax.sharding import PartitionSpec as P


TB = 4
SLOTS = 2
SPARE = 16
TILE = 128

CONTRACT_FIRST = (((0,), (0,)), ((), ()))
BF16 = jnp.bfloat16
F32 = jnp.float32

HBM = pl.BlockSpec(memory_space=pltpu.HBM)
VMEM = pl.BlockSpec(memory_space=pltpu.VMEM)
SMEM = pl.BlockSpec(memory_space=pltpu.SMEM)
PARAMS = pltpu.CompilerParams(vmem_limit_bytes=18 << 20)


def located(kernel, rows, group):
    def body(*refs):
        dev = lax.axis_index("tm")
        member = lax.rem(dev, jnp.int32(group))
        kernel((member * rows, lax.div(dev, jnp.int32(group)), dev), *refs)

    return body


def mm(a, b):
    return jnp.dot(a, b, preferred_element_type=F32)


def mm_t(a, b):
    return lax.dot_general(a, b, CONTRACT_FIRST, preferred_element_type=F32)


def iotas(size):
    r = lax.broadcasted_iota(jnp.int32, (size, size), 0)
    c = lax.broadcasted_iota(jnp.int32, (size, size), 1)
    return r, c


def couple(target, lowers, factor):
    half = factor.shape[0] // 2
    for lower, at in lowers:
        here = pl.ds(at, lower.shape[0])
        target[here, :half] = mm(lower[...], factor[:, :half]).astype(BF16)
        target[here, half:] = mm(lower[:, half:], factor[half:, half:]).astype(BF16)


def write_out(values, outs, sems):
    copies = [
        pltpu.make_async_copy(v, o, sems.at[i]) for i, (v, o) in enumerate(zip(values, outs))
    ]
    for copy in copies:
        copy.start()
    for copy in copies:
        copy.wait()


def tile_diag(tile):
    r, c = iotas(TILE)
    return jnp.sum(jnp.where(r == c, tile.astype(F32), 0.0), axis=0, keepdims=True)


def pack(packet, cov, start, passenger, chunk):
    rows, n = cov.shape
    paired = packet.shape[1] == rows
    row = lax.broadcasted_iota(jnp.int32, (SPARE, TILE if paired else n), 0)
    if not paired:
        packet[:rows, :] = cov[...]
        packet[rows:, :] = jnp.where(row == 0, passenger[...], 0.0).astype(BF16)
        return
    size = packet.shape[0] - SPARE
    other = n - rows - start
    r, c = iotas(TILE)
    for k in range(0, size, TILE):
        i = chunk * size + k
        for j in range(0, rows, TILE):
            mine = cov[i : i + TILE, pl.ds(pl.multiple_of(start + j, TILE), TILE)]
            cross = cov[i : i + TILE, pl.ds(pl.multiple_of(other + j, TILE), TILE)]
            if j > i:
                tile = mine
            elif j < i:
                tile = cross
            else:
                tile = jnp.where(c >= r, mine.astype(F32), cross.astype(F32)).astype(BF16)
                spare = jnp.where(row == 0, tile_diag(cross), 0.0)
                if passenger is not None:
                    for k_row in range(n // rows):
                        at = k_row * rows + i
                        spare = jnp.where(row == k_row + 1, passenger[:, at : at + TILE], spare)
                packet[size:, i : i + TILE] = spare.astype(BF16)
            packet[k : k + TILE, j : j + TILE] = tile


def unpack(full, diag, rider, packets, start, chunk):
    n = full.shape[0]
    if len(packets) == 1:
        (packet,) = packets
        rows = packet.shape[1] - SPARE
        for k in range(packet.shape[0]):
            full[k * rows : (k + 1) * rows, :] = packet[k, :rows, :]
        for i in range(0, n, TILE):
            diag[:, i : i + TILE] = tile_diag(full[i : i + TILE, i : i + TILE])
        rider[...] = packet[0, rows:, :].astype(F32)[0:1]
        return
    size = packets[0].shape[0] - SPARE
    rows = packets[0].shape[1]
    base = (start, n - rows - start)
    r, c = iotas(TILE)

    def put(at_row, i, at_col, j, tile):
        full[
            pl.ds(pl.multiple_of(at_row + i, TILE), TILE),
            pl.ds(pl.multiple_of(at_col + j, TILE), TILE),
        ] = tile

    for k in range(0, size, TILE):
        i = chunk * size + k
        spare = packets[0][size:, i : i + TILE].astype(F32)
        for k_row in range(n // rows):
            at = k_row * rows + i
            rider[:, at : at + TILE] = spare[k_row + 1 : k_row + 2]
        for mine, yours in ((0, 1), (1, 0)):
            for j in range(0, rows, TILE):
                tile = packets[mine][k : k + TILE, j : j + TILE]
                flip = tile.T
                if j > i:
                    put(base[mine], i, base[mine], j, tile)
                    put(base[mine], j, base[mine], i, flip)
                elif j < i:
                    put(base[mine], i, base[yours], j, tile)
                    put(base[yours], j, base[mine], i, flip)
                else:
                    tile = tile.astype(F32)
                    flip = flip.astype(F32)
                    theirs = packets[yours][k : k + TILE, i : i + TILE].T.astype(F32)
                    own = jnp.where(c >= r, tile, flip)
                    put(base[mine], i, base[mine], i, own.astype(BF16))
                    cross = jnp.where(c < r, tile, jnp.where(c > r, theirs, spare[0:1]))
                    put(base[mine], i, base[yours], i, cross.astype(BF16))
                    diag[:, pl.ds(pl.multiple_of(base[mine] + i, TILE), TILE)] = tile_diag(own)


def product_rows(cov, gram, coupling, right, start, chunk, chunks, sign):
    size = cov.shape[0] // chunks
    at = chunk * size
    here = pl.ds(pl.multiple_of(start + at, size), size)
    term = mm_t(coupling[:, here], right[...])
    cov[at : at + size, :] = (gram[at : at + size, :] + sign * term).astype(BF16)


def fold_kernel(ids, factor, lower, own, lower_a, lower_b, square, cross, sems):
    rows = factor.shape[0]
    half = rows // 2
    quarter = rows // 4
    start = pl.multiple_of(ids[0], rows)
    moves = [
        (lower.at[:half], lower_a),
        (factor, own),
        (factor.at[half:, pl.ds(start, rows)], square.at[:half]),
        (factor.at[:quarter, pl.ds(start, half)], square.at[half:, :half]),
        (factor.at[quarter:half, pl.ds(start, half)], square.at[half:, half:]),
        (factor.at[:, :rows], cross),
        (lower.at[half:], lower_b),
    ]
    copies = [pltpu.make_async_copy(s, t, sems.at[i]) for i, (s, t) in enumerate(moves)]
    for copy in copies:
        copy.start()
    for copy in copies:
        copy.wait()


def unfold(target, squares, crosses, start, sems):
    rows = squares[0].shape[0] * 4 // 3
    half = rows // 2
    quarter = rows // 4
    n = target.shape[0]
    moves = []
    for square, at in zip(squares, (start, n - rows - start)):
        moves += [
            (square.at[:half], target.at[pl.ds(at + half, half), pl.ds(at, rows)]),
            (square.at[half:, :half], target.at[pl.ds(at, quarter), pl.ds(at, half)]),
            (
                square.at[half:, half:],
                target.at[pl.ds(at + quarter, quarter), pl.ds(at, half)],
            ),
        ]
        zeros = jnp.zeros((half, half), BF16)
        target[pl.ds(at, half), pl.ds(pl.multiple_of(at + half, half), half)] = zeros
    target[:rows, rows:] = jnp.zeros((rows, n - rows), BF16)
    copies = [pltpu.make_async_copy(s, t, sems.at[i]) for i, (s, t) in enumerate(moves)]
    for copy in copies:
        copy.start()
    low = target.at[rows:, :rows]

    @pl.when(start == 0)
    def _():
        pltpu.make_async_copy(crosses[1], low, sems.at[len(moves)]).start()

    @pl.when(start != 0)
    def _():
        pltpu.make_async_copy(crosses[0], low, sems.at[len(moves)]).start()

    return copies + [pltpu.make_async_copy(crosses[0], low, sems.at[len(moves)])]


def place(target, pieces, start):
    n = target.shape[0]
    if len(pieces) == 1:
        target[...] = pieces[0][...]
        return
    rows = pieces[0].shape[0]
    for piece, at in zip(pieces, (start, n - rows - start)):
        target[pl.ds(pl.multiple_of(at, rows), rows), :] = piece[...]


def gram_kernel(pieces, ids, *refs):
    pieces, (factor, gram) = refs[:pieces], refs[pieces:]
    rows, n = gram.shape
    half = n // 2
    start = pl.multiple_of(ids[0], rows)
    own = pl.ds(start, rows)
    place(factor, pieces, start)
    gram[:, :half] = mm_t(factor[:, own], factor[:, :half])
    gram[:, half:] = mm_t(factor[half:, own], factor[half:, half:])


def first_kernel(pieces, chunks, ids, *refs):
    lowers = refs[:pieces]
    factor, gram, coupling, packet, cov = refs[pieces:]
    rows, n = cov.shape
    start = pl.multiple_of(ids[0], rows)
    size = rows // 2
    if pieces == 1:
        placed = [(lowers[0], 0)]
    else:
        first, second, other = lowers
        placed = [
            (first, start),
            (second, pl.multiple_of(start + size, size)),
            (other, pl.multiple_of(n - rows - start, rows)),
        ]
    couple(coupling, placed, factor)

    @pl.when(ids[1] == TB - 1)
    def _():
        product_rows(cov, gram, coupling, coupling, start, 0, chunks, 1)
        pack(packet, cov, start, None if chunks > 1 else jnp.zeros((1, n), F32), 0)


def rest_kernel(block, sign, ids, gram, coupling, *refs):
    packet, cov = refs[len(refs) - 2 :]
    right, passenger = (coupling, None) if len(refs) == 3 else refs[:2]
    start = pl.multiple_of(ids[0], cov.shape[0])

    @pl.when(ids[1] == block)
    def _():
        product_rows(cov, gram, coupling, right, start, 1, 2, sign)
        pack(packet, cov, start, passenger, 1)


def open_kernel(lowest, highest, ids, mine, yours, full, diag, rider):
    @pl.when(jnp.logical_and(ids[1] >= lowest, ids[1] <= highest))
    def _():
        unpack(full, diag, rider, (mine, yours), ids[0], 0)


def second_kernel(pieces, chunks, ids, *refs):
    packets = refs[:pieces]
    coupling, gram = refs[pieces : pieces + 2]
    packet, off, cov, full, diag, rider = refs[len(refs) - 6 :]
    rows = cov.shape[0]
    start = pl.multiple_of(ids[0], rows)

    @pl.when(ids[1] == TB - 2)
    def _():
        unpack(full, diag, rider, packets, start, chunks - 1)
        off[...] = (-mm(full[...], coupling[...])).astype(BF16)
        product_rows(cov, gram, coupling, off, start, 0, chunks, -1)
        pack(packet, cov, start, diag, 0)


def heard_kernel(parts, ids, *refs):
    parts, rest = refs[:parts], refs[parts:]
    (factor, coupling, cov_3, off_2, cov_2, heard, gram_1, diag_0, coupling_1, coupling_0,
     off_out, cov_out, off, sems, out_sems) = rest
    rows, _ = cov_3.shape
    start = pl.multiple_of(ids[0], rows)
    block = ids[1]

    @pl.when(block == TB - 1)
    def _():
        off[...] = -coupling[pl.ds(start, rows), :]
        write_out((off, cov_3), (off_out, cov_out), out_sems)

    @pl.when(block == TB - 2)
    def _():
        write_out((off_2.at[pl.ds(start, rows)], cov_2), (off_out, cov_out), out_sems)

    def finish(factor_1, factor_0, known):
        known[...] = coupling[...]
        gram_1[...] = mm_t(factor_1[...], factor_1[...])
        diag_0[...] = jnp.sum(jnp.square(factor_0[...].astype(F32)), axis=0, keepdims=True)

    @pl.when(block < 2)
    def _():
        if len(parts) > 1:
            for copy in unfold(heard, parts[:2], parts[2:], start, sems):
                copy.wait()
        else:
            heard[...] = parts[0][...]

        @pl.when(block == 0)
        def _():
            finish(heard, factor, coupling_0)

        @pl.when(block == 1)
        def _():
            finish(factor, heard, coupling_1)


def ready_kernel(pieces, first, ids, *refs):
    lowers, heard = refs[:pieces], refs[pieces]
    coupling_1, coupling_0 = refs[len(refs) - 2 :]
    n = heard.shape[0]
    size = lowers[0].shape[0]
    placed = [(lowers[0], 0)]
    if pieces > 1:
        bases = (ids[0], n - 2 * size - ids[0])
        placed = [(p, pl.multiple_of(b + first, size)) for p, b in zip(lowers, bases)]

    @pl.when(ids[1] == 0)
    def _():
        couple(coupling_1, placed, heard)

    @pl.when(ids[1] == 1)
    def _():
        couple(coupling_0, placed, heard)


def merge_kernel(ids, at_0, at_1, out, sem):
    block = ids[1]

    @pl.when(block == 0)
    def _():
        copy = pltpu.make_async_copy(at_0, out, sem.at[0])
        copy.start()
        copy.wait()

    @pl.when(block == 1)
    def _():
        copy = pltpu.make_async_copy(at_1, out, sem.at[0])
        copy.start()
        copy.wait()


def third_kernel(pieces, chunks, ids, *refs):
    packets = refs[:pieces]
    coupling_1, gram_1, coupling_0, diag_0 = refs[pieces : pieces + 4]
    off_0, off_1, cov_1, variances, full, diag, rider = refs[len(refs) - 7 :]
    n = full.shape[0]

    @pl.when(ids[1] < 2)
    def _():
        unpack(full, diag, rider, packets, ids[0], chunks - 1)
        var_2 = diag[...]
        var_3 = rider[...]
        off_1[...] = (-mm(full[...], coupling_1[...])).astype(BF16)
        cov_1[...] = (gram_1[...] - mm_t(coupling_1[...], off_1[...])).astype(BF16)
        off_0[...] = (-mm(cov_1[...], coupling_0[...])).astype(BF16)
        for i in range(0, n, TILE):
            diag[:, i : i + TILE] = tile_diag(cov_1[i : i + TILE, i : i + TILE])
        product = coupling_0[...].astype(F32) * off_0[...].astype(F32)
        var_0 = diag_0[...] - jnp.sum(product, axis=0, keepdims=True)
        row = lax.broadcasted_iota(jnp.int32, variances.shape, 0)
        merged = jnp.where(row == 0, var_0, jnp.where(row == 1, diag[...], 0.0))
        merged = jnp.where(row == 2, var_2, jnp.where(row == 3, var_3, merged))
        variances[...] = merged.astype(BF16)


def last_kernel(ids, coupling_0, gram, off_0, off_1, cov_1, _, __, off_out, cov_out, cov, sems):
    rows = cov.shape[0]
    start = pl.multiple_of(ids[0], rows)
    block = ids[1]
    own = pl.ds(start, rows)

    @pl.when(block == 1)
    def _():
        one = pltpu.make_async_copy(off_1.at[own], off_out, sems.at[0])
        two = pltpu.make_async_copy(cov_1.at[own], cov_out, sems.at[1])
        one.start()
        two.start()
        one.wait()
        two.wait()

    @pl.when(block == 0)
    def _():
        one = pltpu.make_async_copy(off_0.at[own], off_out, sems.at[0])
        one.start()
        copies = [one]
        parts = 2 if rows % (2 * TILE) == 0 else 1
        for k in range(parts):
            product_rows(cov, gram, coupling_0, off_0, start, k, parts, -1)
            here = pl.ds(k * rows // parts, rows // parts)
            copies.append(
                pltpu.make_async_copy(cov.at[here], cov_out.at[here], sems.at[k + 1])
            )
            copies[-1].start()
        for copy in copies:
            copy.wait()


def deliver_kernel(ids, owner, mine, heard, out):
    block = ids[1]
    dev = ids[2]
    values = jnp.where(block < 2, mine[...].astype(F32), heard[...].astype(F32))
    lines = [jnp.zeros((1, out.shape[1]), F32) for _ in range(SLOTS)]
    for t in range(TB):
        rank = jnp.int32(0)
        for before in range(t):
            rank += (owner[before] == owner[t]).astype(jnp.int32)
        for slot in range(SLOTS):
            here = jnp.logical_and(owner[t] == dev, rank == slot)
            lines[slot] += jnp.where(here, values[t : t + 1], 0.0)
    for slot in range(SLOTS):
        out[slot : slot + 1, :] = lines[slot]


def shards(linv, sub, owner):
    group = lax.axis_size("tm") // TB
    rows, n = linv.shape
    paired = group == 2
    dev = lax.axis_index("tm")
    member = dev % group

    def block_to_block(values, routes, members=range(group)):
        pairs = [(s * group + i, t * group + i) for s, t in routes for i in members]
        return lax.ppermute(values, "tm", pairs)

    def peer(piece, step=1):
        return lax.ppermute(piece, "tm", [(i, i ^ step) for i in range(TB * group)])

    def pieces_of(piece):
        if paired:
            return [piece, peer(piece)]
        step = 1
        while step < group:
            other = peer(piece, step)
            upper = (member // step) % 2 == 1
            piece = jnp.concatenate(
                [jnp.where(upper, other, piece), jnp.where(upper, piece, other)], 0
            )
            step *= 2
        return [piece]

    def packets_of(packet):
        return pieces_of(packet) if paired else pieces_of(packet[None])

    def after(values, *others):
        return lax.optimization_barrier((values, *others))[0]

    def call(kernel, out, inputs, spaces, scratch, aliases=None):
        shapes = tuple(
            pltpu.HBM(o[1], o[2]) if o[0] is HBM else pltpu.VMEM(o[1], o[2]) for o in out
        )
        placed = [
            x if space is SMEM else pltpu.with_memory_space_constraint(x, space.memory_space)
            for x, space in zip(inputs, spaces, strict=True)
        ]
        return pl.pallas_call(
            located(kernel, rows, group),
            out_shape=shapes,
            in_specs=list(spaces),
            out_specs=tuple(o[0] for o in out),
            scratch_shapes=scratch,
            input_output_aliases=aliases or {},
            compiler_params=PARAMS,
        )(*placed)

    def sems(*shape):
        return pltpu.SemaphoreType.DMA(shape)

    pieces = 2 if paired else 1
    chunks = 2 if paired else 1
    size = rows // chunks
    packet_shape = (size + SPARE, rows if paired else n)
    whole = (VMEM, (n, n), BF16)
    part = (VMEM, (rows, n), BF16)
    line = (VMEM, (1, n), F32)
    packed = (VMEM, packet_shape, BF16)
    out_rows = (HBM, (rows, n), BF16)

    def swapped(piece, *others):
        return pieces_of(after(piece, *others) if others else piece)

    swap = [(1, 0), (0, 1)]
    if paired:
        other_factor, other_lower = peer(linv), peer(sub)
        half_rows = (VMEM, (size, n), BF16)
        own, lower_a, lower_b, square, cross = call(
            fold_kernel,
            [part, half_rows, half_rows,
             (VMEM, (rows * 3 // 4, rows), BF16), (VMEM, (rows, rows), BF16)],
            [linv, sub],
            [HBM, HBM],
            [sems(7)],
        )
        factors = [own, other_factor]
        lowers = [lower_a, lower_b, other_lower]
        raw_lower = [block_to_block(lower_a, swap), block_to_block(lower_b, swap)]
        raw_factor = [
            block_to_block(square, swap), block_to_block(cross, swap, range(1, 2))
        ]
    else:
        factors = pieces_of(linv)
        lowers = pieces_of(sub)
        raw_lower = [block_to_block(sub, swap)]
        raw_factor = [block_to_block(linv, swap)]

    factor, gram = call(
        functools.partial(gram_kernel, pieces),
        [whole, (VMEM, (rows, n), F32)],
        [*factors],
        [VMEM] * pieces,
        [],
    )
    coupling, packet_a, cov_3 = call(
        functools.partial(first_kernel, len(lowers), chunks),
        [whole, packed, part],
        [*lowers, factor, gram],
        [VMEM] * (len(lowers) + 2),
        [],
    )
    packets_2 = [block_to_block(packet_a, [(3, 2)])]
    if chunks > 1:
        packet_b, cov_3 = call(
            functools.partial(rest_kernel, TB - 1, 1),
            [packed, part],
            [gram, coupling, cov_3],
            [VMEM] * 3,
            [],
            {2: 1},
        )
        packets_2.append(block_to_block(packet_b, [(3, 2)]))

    opened = []
    if chunks > 1:
        opened = call(
            functools.partial(open_kernel, 2, 2),
            [whole, line, line],
            [*packets_of(packets_2[0])],
            [VMEM, VMEM],
            [],
        )
    packet_a, off_2, cov_2, _, diag_2, _ = call(
        functools.partial(second_kernel, pieces, chunks),
        [packed, whole, part, whole, line, line],
        [*packets_of(packets_2[-1]), coupling, gram, *opened],
        [VMEM] * (pieces + 2 + len(opened)),
        [],
        {pieces + 2 + i: 3 + i for i in range(len(opened))},
    )
    packet = packet_a
    packets_0 = [block_to_block(packet_a, [(2, 0)])]
    packets_1 = [block_to_block(packet_a, [(2, 1)])]
    if chunks > 1:
        packet, cov_2 = call(
            functools.partial(rest_kernel, TB - 2, -1),
            [packed, part],
            [gram, coupling, off_2, diag_2, cov_2],
            [VMEM] * 5,
            [],
            {4: 1},
        )
        packets_0.append(block_to_block(packet, [(2, 0)]))
        packets_1.append(block_to_block(packet, [(2, 1)]))

    parts = [x for piece in raw_factor for x in swapped(piece, packet)]
    heard_factor, gram_1, diag_0, coupling_1, coupling_0, off_rows, cov_rows = call(
        functools.partial(heard_kernel, len(parts)),
        [whole, (VMEM, (n, n), F32), line, whole, whole, out_rows, out_rows],
        [*parts, factor, coupling, cov_3, off_2, cov_2],
        [VMEM] * (len(parts) + 5),
        [pltpu.VMEM((rows, n), BF16), sems(8), sems(2)],
    )
    for k, piece in enumerate(raw_lower):
        coupling_1, coupling_0 = call(
            functools.partial(ready_kernel, pieces, k * size),
            [whole, whole],
            [*swapped(piece, packet), heard_factor,
             coupling_1, coupling_0],
            [VMEM] * (pieces + 3),
            [],
            {pieces + 1: 0, pieces + 2: 1},
        )

    carried = [
        call(merge_kernel, [packed], [at_0, at_1], [VMEM, VMEM], [sems(1)])[0]
        for at_0, at_1 in zip(packets_0, packets_1)
    ]
    opened = []
    if chunks > 1:
        opened = call(
            functools.partial(open_kernel, 0, 1),
            [whole, line, line],
            [*packets_of(carried[0])],
            [VMEM, VMEM],
            [],
        )
    off_0, off_1, cov_1, variances, *_ = call(
        functools.partial(third_kernel, pieces, chunks),
        [whole, whole, whole, (VMEM, (SPARE, n), BF16), whole, line, line],
        [*packets_of(carried[-1]), coupling_1, gram_1, coupling_0, diag_0,
         *opened],
        [VMEM] * (pieces + 4 + len(opened)),
        [],
        {pieces + 4 + i: 4 + i for i in range(len(opened))},
    )
    heard = block_to_block(variances, [(0, 2), (1, 3)])

    off_rows, cov_rows = call(
        last_kernel,
        [out_rows, out_rows],
        [coupling_0, gram, off_0, off_1, cov_1, off_rows, cov_rows],
        [VMEM] * 5 + [HBM, HBM],
        [pltpu.VMEM((rows, n), BF16), sems(3)],
        {5: 0, 6: 1},
    )
    (owned_var,) = call(
        deliver_kernel,
        [(VMEM, (SLOTS, n), F32)],
        [owner, variances, heard],
        [SMEM, VMEM, VMEM],
        [],
    )
    return (cov_rows, off_rows, owned_var)


def solution(mesh):
    return jax.shard_map(
        shards,
        mesh=mesh,
        in_specs=(P(("cfg", "tm"), None), P(("cfg", "tm"), None), P("cfg")),
        out_specs=(P(("cfg", "tm"), None), P(("cfg", "tm"), None), P(("cfg", "tm"), None)),
        check_vma=False,
    )
```

time: 76.6 us -> 76.1 us (level)
  the two profiles are of different devices: /device:TPU:0 before, /device:TPU:23 now
where the time goes in v5:
time: 76.1 us; the launch traced here: 75.8 us
  waiting for transfers between devices  50.1 us (66%)
  starting transfers between devices  15.2 us (20%)
  Pallas kernels  8.96 us (12%)
  between operations  0.88 us (1%)
    ppermute x11, waiting for transfers between devices, block_to_block(): return lax.ppermute(values, 'tm', pairs)  47.7 us
    ppermute x11, starting transfers between devices, block_to_block(): return lax.ppermute(values, 'tm', pairs)  9.33 us
    pallas_call x16, Pallas kernels, call(): pl.pallas_call(located(kernel, rows, group), out_shape=shapes, in_specs=l...  8.96 us
    ppermute x10, starting transfers between devices, peer(): return lax.ppermute(piece, 'tm', [(i, i ^ step) for i in range(TB * group)])  5.89 us
    ppermute x10, waiting for transfers between devices, peer(): return lax.ppermute(piece, 'tm', [(i, i ^ step) for i in range(TB * group)])  2.48 us
  transfers between devices with their start and end apart: 21, of which 9 were waited for; matrix products, arithmetic and copies ran while one was open for 0% of the time, Pallas kernels for 8%

profile of v5, /device:TPU:23, one launch (start us, length us, event | category | flops | bytes accessed | tf_op | source)
XLA Modules:
  0.0 75.8 jit_solution(7190370149188825755)
XLA Ops:
  0.6 0.7 collective-permute-start.1
  1.4 0.1 collective-permute-start.2
  1.4 1.9 %shard_map.58 = (bf16[512,1024]{1,0:T(8,128)(2,1)S(1)}, bf16[256,1024]{1,0:T(8,128)(2,1)S(1)}, bf16[256,1024]{1,0:T(8,128)(2,1)S(1)}, bf16[384,512]{1,0:T(8,128)(2,1)S(1)}, bf16[512,512]{1,0:T(8,128)(2,1)S(1)}) custom-call(bf16[512,1024]{1,0:T(8,128)(2,1)} %refs_0_.2, bf16[512,1024]{1,0:T(8,128)(2,1)} %refs_1_.1), custom_call_target="tpu_custom_call" | custom-call | tf_op jit(solution)/shard_map/pallas_call | solution.py:478
  3.3 0.5 collective-permute-done.1.refs_1_
  3.9 1.3 %shard_map.59 = (bf16[1024,1024]{1,0:T(8,128)(2,1)S(1)}, f32[512,1024]{1,0:T(8,128)S(1)}) custom-call(bf16[512,1024]{1,0:T(8,128)(2,1)S(1)} %get-tuple-element.49.refs_0_, bf16[512,1024]{1,0:T(8,128)(2,1)S(1)} %collective-permute-done.1.refs_1_), custom_call_target="tpu_custom_call" | custom-call | tf_op jit(solution)/shard_map/pallas_call | solution.py:478
  5.2 0.2 collective-permute-done.2.refs_2_
  5.4 2.7 %shard_map.60 = (bf16[1024,1024]{1,0:T(8,128)(2,1)S(1)}, bf16[272,512]{1,0:T(8,128)(2,1)S(1)}, bf16[512,1024]{1,0:T(8,128)(2,1)S(1)}) custom-call(bf16[256,1024]{1,0:T(8,128)(2,1)S(1)} %get-tuple-element.51.refs_0_, bf16[256,1024]{1,0:T(8,128)(2,1)S(1)} %get-tuple-element.48.refs_1_, bf16[512,1024]{1,0:T(8,128)(2,1)S(1)} %collective-permute-done.2.refs_2_, ...), custom_call_target="tpu_custom_call" | custom-call | tf_op jit(solution)/shard_map/pallas_call | solution.py:478
  8.1 1.3 %collective-permute-start.5 = (bf16[272,512]{1,0:T(8,128)(2,1)S(1)}, bf16[272,512]{1,0:T(8,128)(2,1)S(1)}, u32[]{:S(2)}, u32[]{:S(2)}) collective-permute-start(bf16[272,512]{1,0:T(8,128)(2,1)S(1)} %get-tuple-element.56), channel_id=1, source_target_pairs={{6,4},{7,5},{14,12},{15,13},{22,20},{23,21},{30,28},{31,29}} | collective-permute-start | bytes 835592 | tf_op jit(solution)/shard_map/ppermute | solution.py:446
  9.4 0.9 %shard_map.61 = (bf16[272,512]{1,0:T(8,128)(2,1)S(1)}, bf16[512,1024]{1,0:T(8,128)(2,1)S(1)}) custom-call(f32[512,1024]{1,0:T(8,128)S(1)} %get-tuple-element.50.refs_4_.refs_0_.refs_3_.refs_1_, bf16[1024,1024]{1,0:T(8,128)(2,1)S(1)} %get-tuple-element.53.refs_1_.refs_2_.refs_5_, ...), custom_call_target="tpu_custom_call", output_to_operand_aliasing={{1}: (2, {})} | custom-call | tf_op jit(solution)/shard_map/pallas_call | solution.py:478
  10.3 1.3 %collective-permute-start.3 = (bf16[272,512]{1,0:T(8,128)(2,1)S(1)}, bf16[272,512]{1,0:T(8,128)(2,1)S(1)}, u32[]{:S(2)}, u32[]{:S(2)}) collective-permute-start(bf16[272,512]{1,0:T(8,128)(2,1)S(1)} %get-tuple-element.55), channel_id=1, source_target_pairs={{6,4},{7,5},{14,12},{15,13},{22,20},{23,21},{30,28},{31,29}} | collective-permute-start | bytes 835592 | tf_op jit(solution)/shard_map/ppermute | solution.py:446
  11.6 3.4 %collective-permute-done.5.refs_0_ = bf16[272,512]{1,0:T(8,128)(2,1)S(1)} collective-permute-done((bf16[272,512]{1,0:T(8,128)(2,1)S(1)}, bf16[272,512]{1,0:T(8,128)(2,1)S(1)}, u32[]{:S(2)}, u32[]{:S(2)}) %collective-permute-start.5) | collective-permute-done | bytes 278560 | tf_op jit(solution)/shard_map/ppermute | solution.py:446
  15.0 2.1 %collective-permute-start.6 = (bf16[272,512]{1,0:T(8,128)(2,1)S(1)}, bf16[272,512]{1,0:T(8,128)(2,1)S(1)}, u32[]{:S(2)}, u32[]{:S(2)}) collective-permute-start(bf16[272,512]{1,0:T(8,128)(2,1)S(1)} %collective-permute-done.5.refs_0_), channel_id=1, source_target_pairs={{0,1},{1,0},{2,3},{3,2},{4,5},{5,4},{6,7},{7,6},{8,9},{9,8},{10,11... | collective-permute-start | bytes 835592 | tf_op jit(solution)/shard_map/ppermute | solution.py:449
  17.0 0.7 collective-permute-start
  17.7 0.7 collective-permute-start.8
  18.4 0.7 collective-permute-start.10
  19.1 1.8 %collective-permute-done.3.refs_0_ = bf16[272,512]{1,0:T(8,128)(2,1)S(1)} collective-permute-done((bf16[272,512]{1,0:T(8,128)(2,1)S(1)}, bf16[272,512]{1,0:T(8,128)(2,1)S(1)}, u32[]{:S(2)}, u32[]{:S(2)}) %collective-permute-start.3) | collective-permute-done | bytes 278560 | tf_op jit(solution)/shard_map/ppermute | solution.py:446
  20.9 1.2 %collective-permute-start.4 = (bf16[272,512]{1,0:T(8,128)(2,1)S(1)}, bf16[272,512]{1,0:T(8,128)(2,1)S(1)}, u32[]{:S(2)}, u32[]{:S(2)}) collective-permute-start(bf16[272,512]{1,0:T(8,128)(2,1)S(1)} %collective-permute-done.3.refs_0_), channel_id=1, source_target_pairs={{0,1},{1,0},{2,3},{3,2},{4,5},{5,4},{6,7},{7,6},{8,9},{9,8},{10,11... | collective-permute-start | bytes 835592 | tf_op jit(solution)/shard_map/ppermute | solution.py:449
  22.2 0.0 collective-permute-done.6.refs_1_
  22.2 0.7 collective-permute-start.12
  22.9 0.5 collective-permute-done.4.refs_1_
  23.4 0.7 collective-permute-start.14
  24.0 0.0 collective-permute-done.8.refs_0_
  24.0 0.7 collective-permute-start.17
  24.7 0.0 collective-permute-done.refs_0_
  24.7 0.7 collective-permute-start.18
  25.4 0.0 collective-permute-done.10.refs_2_
  25.4 0.4 collective-permute-start.9
  25.9 0.0 collective-permute-done.12.refs_0_
  25.9 0.7 collective-permute-start.15
  26.6 0.0 collective-permute-done.14.refs_0_
  26.6 0.2 collective-permute-start.11
  26.8 0.0 collective-permute-done.17.refs_0_
  26.8 0.4 collective-permute-start.13
  27.1 0.0 collective-permute-done.18.refs_1_
  27.1 0.1 collective-permute-start.7
  27.3 0.0 collective-permute-done.15.refs_1_
  27.3 0.4 collective-permute-start.19
  27.8 0.0 collective-permute-done.9.refs_1_
  27.8 0.2 collective-permute-start.16
  28.0 0.6 collective-permute-done.11.refs_3_
  28.5 1.5 %shard_map.65 = (bf16[1024,1024]{1,0:T(8,128)(2,1)S(1)}, f32[1024,1024]{1,0:T(8,128)S(1)}, f32[1,1024]{1,0:T(1,128)S(1)}, bf16[1024,1024]{1,0:T(8,128)(2,1)S(1)}...) custom-call(bf16[384,512]{1,0:T(8,128)(2,1)S(1)} %collective-permute-done.8.refs_0_, ...), custom_call_target="tpu_custom_call" | custom-call | tf_op jit(solution)/shard_map/pallas_call | solution.py:478
  30.0 0.0 collective-permute-done.13.refs_1_
  30.1 0.0 collective-permute-done.7.refs_1_
  30.1 0.3 collective-permute-done.19.refs_1_
  30.4 0.4 collective-permute-done.16.refs_1_
  30.8 1.3 %collective-permute-start.20 = (bf16[16,1024]{1,0:T(8,128)(2,1)S(1)}, bf16[16,1024]{1,0:T(8,128)(2,1)S(1)}, u32[]{:S(2)}, u32[]{:S(2)}) collective-permute-start(bf16[16,1024]{1,0:T(8,128)(2,1)S(1)} %get-tuple-element.92.refs_1_), channel_id=1, source_target_pairs={{0,4},{1,5},{2,6},{3,7},{8,12},{9,13},{10,14},{11,15},{16,20},{17,... | collective-permute-start | bytes 98312 | tf_op jit(solution)/shard_map/ppermute | solution.py:446
  32.1 0.0 copy-start
  32.1 0.1 shard_map.72
  32.2 42.4 %collective-permute-done.20.refs_2_ = bf16[16,1024]{1,0:T(8,128)(2,1)S(1)} collective-permute-done((bf16[16,1024]{1,0:T(8,128)(2,1)S(1)}, bf16[16,1024]{1,0:T(8,128)(2,1)S(1)}, u32[]{:S(2)}, u32[]{:S(2)}) %collective-permute-start.20) | collective-permute-done | bytes 32800 | tf_op jit(solution)/shard_map/ppermute | solution.py:446
  74.6 0.0 copy-done
  74.6 0.6 shard_map.73
  75.2 0.6 copy.34
  (9 shorter events, 0.1 us)
Async XLA Ops:
  0.6 3.2 %collective-permute-start.1 = (bf16[512,1024]{1,0:T(8,128)(2,1)}, bf16[512,1024]{1,0:T(8,128)(2,1)S(1)}, u32[]{:S(2)}, u32[]{:S(2)}) collective-permute-start(bf16[512,1024]{1,0:T(8,128)(2,1)} %refs_0_.2), channel_id=1, source_target_pairs={{0,1},{1,0},{2,3},{3,2},{4,5},{5,4},{6,7},{7,6},{8,9},{9,8},{10,11... | collective-permute-start | bytes 3145736 | tf_op jit(solution)/shard_map/ppermute | solution.py:449
  1.4 4.0 %collective-permute-start.2 = (bf16[512,1024]{1,0:T(8,128)(2,1)}, bf16[512,1024]{1,0:T(8,128)(2,1)S(1)}, u32[]{:S(2)}, u32[]{:S(2)}) collective-permute-start(bf16[512,1024]{1,0:T(8,128)(2,1)} %refs_1_.1), channel_id=1, source_target_pairs={{0,1},{1,0},{2,3},{3,2},{4,5},{5,4},{6,7},{7,6},{8,9},{9,8},{10,11... | collective-permute-start | bytes 3145736 | tf_op jit(solution)/shard_map/ppermute | solution.py:449
  8.1 6.9 %collective-permute-start.5 = (bf16[272,512]{1,0:T(8,128)(2,1)S(1)}, bf16[272,512]{1,0:T(8,128)(2,1)S(1)}, u32[]{:S(2)}, u32[]{:S(2)}) collective-permute-start(bf16[272,512]{1,0:T(8,128)(2,1)S(1)} %get-tuple-element.56), channel_id=1, source_target_pairs={{6,4},{7,5},{14,12},{15,13},{22,20},{23,21},{30,28},{31,29}} | collective-permute-start | bytes 835592 | tf_op jit(solution)/shard_map/ppermute | solution.py:446
  10.3 10.7 %collective-permute-start.3 = (bf16[272,512]{1,0:T(8,128)(2,1)S(1)}, bf16[272,512]{1,0:T(8,128)(2,1)S(1)}, u32[]{:S(2)}, u32[]{:S(2)}) collective-permute-start(bf16[272,512]{1,0:T(8,128)(2,1)S(1)} %get-tuple-element.55), channel_id=1, source_target_pairs={{6,4},{7,5},{14,12},{15,13},{22,20},{23,21},{30,28},{31,29}} | collective-permute-start | bytes 835592 | tf_op jit(solution)/shard_map/ppermute | solution.py:446
  15.0 7.2 %collective-permute-start.6 = (bf16[272,512]{1,0:T(8,128)(2,1)S(1)}, bf16[272,512]{1,0:T(8,128)(2,1)S(1)}, u32[]{:S(2)}, u32[]{:S(2)}) collective-permute-start(bf16[272,512]{1,0:T(8,128)(2,1)S(1)} %collective-permute-done.5.refs_0_), channel_id=1, source_target_pairs={{0,1},{1,0},{2,3},{3,2},{4,5},{5,4},{6,7},{7,6},{8,9},{9,8},{10,11... | collective-permute-start | bytes 835592 | tf_op jit(solution)/shard_map/ppermute | solution.py:449
  17.0 7.7 %collective-permute-start = (bf16[256,1024]{1,0:T(8,128)(2,1)S(1)}, bf16[256,1024]{1,0:T(8,128)(2,1)S(1)}, u32[]{:S(2)}, u32[]{:S(2)}) collective-permute-start(bf16[256,1024]{1,0:T(8,128)(2,1)S(1)} %get-tuple-element.48.refs_1_), channel_id=1, source_target_pairs={{2,0},{3,1},{0,2},{1,3},{10,8},{11,9},{8,10},{9,11},{18,16},{19,17... | collective-permute-start | bytes 1572872 | tf_op jit(solution)/shard_map/ppermute | solution.py:446
  17.7 6.3 %collective-permute-start.8 = (bf16[384,512]{1,0:T(8,128)(2,1)S(1)}, bf16[384,512]{1,0:T(8,128)(2,1)S(1)}, u32[]{:S(2)}, u32[]{:S(2)}) collective-permute-start(bf16[384,512]{1,0:T(8,128)(2,1)S(1)} %get-tuple-element.65), channel_id=1, source_target_pairs={{2,0},{3,1},{0,2},{1,3},{10,8},{11,9},{8,10},{9,11},{18,16},{19,17... | collective-permute-start | bytes 1179656 | tf_op jit(solution)/shard_map/ppermute | solution.py:446
  18.4 7.0 %collective-permute-start.10 = (bf16[512,512]{1,0:T(8,128)(2,1)S(1)}, bf16[512,512]{1,0:T(8,128)(2,1)S(1)}, u32[]{:S(2)}, u32[]{:S(2)}) collective-permute-start(bf16[512,512]{1,0:T(8,128)(2,1)S(1)} %get-tuple-element.67), channel_id=1, source_target_pairs={{3,1},{1,3},{11,9},{9,11},{19,17},{17,19},{27,25},{25,27}} | collective-permute-start | bytes 1572872 | tf_op jit(solution)/shard_map/ppermute | solution.py:446
  20.9 2.4 %collective-permute-start.4 = (bf16[272,512]{1,0:T(8,128)(2,1)S(1)}, bf16[272,512]{1,0:T(8,128)(2,1)S(1)}, u32[]{:S(2)}, u32[]{:S(2)}) collective-permute-start(bf16[272,512]{1,0:T(8,128)(2,1)S(1)} %collective-permute-done.3.refs_0_), channel_id=1, source_target_pairs={{0,1},{1,0},{2,3},{3,2},{4,5},{5,4},{6,7},{7,6},{8,9},{9,8},{10,11... | collective-permute-start | bytes 835592 | tf_op jit(solution)/shard_map/ppermute | solution.py:449
  22.2 3.7 %collective-permute-start.12 = (bf16[256,1024]{1,0:T(8,128)(2,1)S(1)}, bf16[256,1024]{1,0:T(8,128)(2,1)S(1)}, u32[]{:S(2)}, u32[]{:S(2)}) collective-permute-start(bf16[256,1024]{1,0:T(8,128)(2,1)S(1)} %get-tuple-element.51.refs_0_), channel_id=1, source_target_pairs={{2,0},{3,1},{0,2},{1,3},{10,8},{11,9},{8,10},{9,11},{18,16},{19,17... | collective-permute-start | bytes 1572872 | tf_op jit(solution)/shard_map/ppermute | solution.py:446
  23.4 3.2 %collective-permute-start.14 = (bf16[272,512]{1,0:T(8,128)(2,1)S(1)}, bf16[272,512]{1,0:T(8,128)(2,1)S(1)}, u32[]{:S(2)}, u32[]{:S(2)}) collective-permute-start(bf16[272,512]{1,0:T(8,128)(2,1)S(1)} %get-tuple-element.63), channel_id=1, source_target_pairs={{4,0},{5,1},{12,8},{13,9},{20,16},{21,17},{28,24},{29,25}} | collective-permute-start | bytes 835592 | tf_op jit(solution)/shard_map/ppermute | solution.py:446
  24.0 2.7 %collective-permute-start.17 = (bf16[272,512]{1,0:T(8,128)(2,1)S(1)}, bf16[272,512]{1,0:T(8,128)(2,1)S(1)}, u32[]{:S(2)}, u32[]{:S(2)}) collective-permute-start(bf16[272,512]{1,0:T(8,128)(2,1)S(1)} %get-tuple-element.81), channel_id=1, source_target_pairs={{4,0},{5,1},{12,8},{13,9},{20,16},{21,17},{28,24},{29,25}} | collective-permute-start | bytes 835592 | tf_op jit(solution)/shard_map/ppermute | solution.py:446
  24.7 2.4 %collective-permute-start.18 = (bf16[272,512]{1,0:T(8,128)(2,1)S(1)}, bf16[272,512]{1,0:T(8,128)(2,1)S(1)}, u32[]{:S(2)}, u32[]{:S(2)}) collective-permute-start(bf16[272,512]{1,0:T(8,128)(2,1)S(1)} %get-tuple-element.81), channel_id=1, source_target_pairs={{4,2},{5,3},{12,10},{13,11},{20,18},{21,19},{28,26},{29,27}} | collective-permute-start | bytes 835592 | tf_op jit(solution)/shard_map/ppermute | solution.py:446
  25.4 2.3 %collective-permute-start.9 = (bf16[384,512]{1,0:T(8,128)(2,1)S(1)}, bf16[384,512]{1,0:T(8,128)(2,1)S(1)}, u32[]{:S(2)}, u32[]{:S(2)}) collective-permute-start(bf16[384,512]{1,0:T(8,128)(2,1)S(1)} %collective-permute-done.8.refs_0_), channel_id=1, source_target_pairs={{0,1},{1,0},{2,3},{3,2},{4,5},{5,4},{6,7},{7,6},{8,9},{9,8},{10,11... | collective-permute-start | bytes 1179656 | tf_op jit(solution)/shard_map/ppermute | solution.py:449
  25.9 1.4 %collective-permute-start.15 = (bf16[272,512]{1,0:T(8,128)(2,1)S(1)}, bf16[272,512]{1,0:T(8,128)(2,1)S(1)}, u32[]{:S(2)}, u32[]{:S(2)}) collective-permute-start(bf16[272,512]{1,0:T(8,128)(2,1)S(1)} %get-tuple-element.63), channel_id=1, source_target_pairs={{4,2},{5,3},{12,10},{13,11},{20,18},{21,19},{28,26},{29,27}} | collective-permute-start | bytes 835592 | tf_op jit(solution)/shard_map/ppermute | solution.py:446
  26.6 2.0 %collective-permute-start.11 = (bf16[512,512]{1,0:T(8,128)(2,1)S(1)}, bf16[512,512]{1,0:T(8,128)(2,1)S(1)}, u32[]{:S(2)}, u32[]{:S(2)}) collective-permute-start(bf16[512,512]{1,0:T(8,128)(2,1)S(1)} %collective-permute-done.10.refs_2_), channel_id=1, source_target_pairs={{0,1},{1,0},{2,3},{3,2},{4,5},{5,4},{6,7},{7,6},{8,9},{9,8},{10,11... | collective-permute-start | bytes 1572872 | tf_op jit(solution)/shard_map/ppermute | solution.py:449
  26.8 3.3 %collective-permute-start.13 = (bf16[256,1024]{1,0:T(8,128)(2,1)S(1)}, bf16[256,1024]{1,0:T(8,128)(2,1)S(1)}, u32[]{:S(2)}, u32[]{:S(2)}) collective-permute-start(bf16[256,1024]{1,0:T(8,128)(2,1)S(1)} %collective-permute-done.12.refs_0_), channel_id=1, source_target_pairs={{0,1},{1,0},{2,3},{3,2},{4,5},{5,4},{6,7},{7,6},{8,9},{9,8},{10,11... | collective-permute-start | bytes 1572872 | tf_op jit(solution)/shard_map/ppermute | solution.py:449
  27.1 2.9 %collective-permute-start.7 = (bf16[256,1024]{1,0:T(8,128)(2,1)S(1)}, bf16[256,1024]{1,0:T(8,128)(2,1)S(1)}, u32[]{:S(2)}, u32[]{:S(2)}) collective-permute-start(bf16[256,1024]{1,0:T(8,128)(2,1)S(1)} %collective-permute-done.refs_0_), channel_id=1, source_target_pairs={{0,1},{1,0},{2,3},{3,2},{4,5},{5,4},{6,7},{7,6},{8,9},{9,8},{10,11... | collective-permute-start | bytes 1572872 | tf_op jit(solution)/shard_map/ppermute | solution.py:449
  27.3 3.1 %collective-permute-start.19 = (bf16[272,512]{1,0:T(8,128)(2,1)S(1)}, bf16[272,512]{1,0:T(8,128)(2,1)S(1)}, u32[]{:S(2)}, u32[]{:S(2)}) collective-permute-start(bf16[272,512]{1,0:T(8,128)(2,1)S(1)} %shard_map.69.refs_0_), channel_id=1, source_target_pairs={{0,1},{1,0},{2,3},{3,2},{4,5},{5,4},{6,7},{7,6},{8,9},{9,8},{10,11... | collective-permute-start | bytes 835592 | tf_op jit(solution)/shard_map/ppermute | solution.py:449
  27.8 3.1 %collective-permute-start.16 = (bf16[272,512]{1,0:T(8,128)(2,1)S(1)}, bf16[272,512]{1,0:T(8,128)(2,1)S(1)}, u32[]{:S(2)}, u32[]{:S(2)}) collective-permute-start(bf16[272,512]{1,0:T(8,128)(2,1)S(1)} %shard_map.68.refs_0_), channel_id=1, source_target_pairs={{0,1},{1,0},{2,3},{3,2},{4,5},{5,4},{6,7},{7,6},{8,9},{9,8},{10,11... | collective-permute-start | bytes 835592 | tf_op jit(solution)/shard_map/ppermute | solution.py:449
  30.8 43.8 %collective-permute-start.20 = (bf16[16,1024]{1,0:T(8,128)(2,1)S(1)}, bf16[16,1024]{1,0:T(8,128)(2,1)S(1)}, u32[]{:S(2)}, u32[]{:S(2)}) collective-permute-start(bf16[16,1024]{1,0:T(8,128)(2,1)S(1)} %get-tuple-element.92.refs_1_), channel_id=1, source_target_pairs={{0,4},{1,5},{2,6},{3,7},{8,12},{9,13},{10,14},{11,15},{16,20},{17,... | collective-permute-start | bytes 98312 | tf_op jit(solution)/shard_map/ppermute | solution.py:446
  32.1 42.5 %copy-start = (s32[4]{0:T(128)S(1)}, s32[4]{0:T(128)}, u32[]{:S(2)}) copy-start(s32[4]{0:T(128)} %refs_0_.3) | copy-start | bytes 52

commit v6 on v5

--- a/solution.py
+++ b/solution.py
@@ -157,19 +157,23 @@
     cov[at : at + size, :] = (gram[at : at + size, :] + sign * term).astype(BF16)
 
 
+def strips(rows):
+    return [(k * TILE, (k + 1) * TILE, k * (k + 1) // 2 * TILE) for k in range(rows // TILE)]
+
+
 def fold_kernel(ids, factor, lower, own, lower_a, lower_b, square, cross, sems):
     rows = factor.shape[0]
-    half = rows // 2
-    quarter = rows // 4
+    cut = lower_a.shape[0]
     start = pl.multiple_of(ids[0], rows)
-    moves = [
-        (lower.at[:half], lower_a),
-        (factor, own),
-        (factor.at[half:, pl.ds(start, rows)], square.at[:half]),
-        (factor.at[:quarter, pl.ds(start, half)], square.at[half:, :half]),
-        (factor.at[quarter:half, pl.ds(start, half)], square.at[half:, half:]),
+    moves = [(factor, own)]
+    for row, width, at in strips(rows):
+        moves.append(
+            (factor.at[row : row + TILE, pl.ds(start, width)], square.at[:, at : at + width])
+        )
+    moves += [
+        (lower.at[:cut], lower_a),
+        (lower.at[cut:], lower_b),
         (factor.at[:, :rows], cross),
-        (lower.at[half:], lower_b),
     ]
     copies = [pltpu.make_async_copy(s, t, sems.at[i]) for i, (s, t) in enumerate(moves)]
     for copy in copies:
@@ -179,22 +183,17 @@
 
 
 def unfold(target, squares, crosses, start, sems):
-    rows = squares[0].shape[0] * 4 // 3
-    half = rows // 2
-    quarter = rows // 4
     n = target.shape[0]
+    rows = n // 2
     moves = []
-    for square, at in zip(squares, (start, n - rows - start)):
-        moves += [
-            (square.at[:half], target.at[pl.ds(at + half, half), pl.ds(at, rows)]),
-            (square.at[half:, :half], target.at[pl.ds(at, quarter), pl.ds(at, half)]),
-            (
-                square.at[half:, half:],
-                target.at[pl.ds(at + quarter, quarter), pl.ds(at, half)],
-            ),
-        ]
-        zeros = jnp.zeros((half, half), BF16)
-        target[pl.ds(at, half), pl.ds(pl.multiple_of(at + half, half), half)] = zeros
+    for square, base in zip(squares, (start, n - rows - start)):
+        for row, width, at in strips(rows):
+            here = pl.ds(pl.multiple_of(base + row, TILE), TILE)
+            cols = pl.ds(pl.multiple_of(base, rows), width)
+            moves.append((square.at[:, at : at + width], target.at[here, cols]))
+            if width < rows:
+                rest = pl.ds(pl.multiple_of(base + width, TILE), rows - width)
+                target[here, rest] = jnp.zeros((TILE, rows - width), BF16)
     target[:rows, rows:] = jnp.zeros((rows, n - rows), BF16)
     copies = [pltpu.make_async_copy(s, t, sems.at[i]) for i, (s, t) in enumerate(moves)]
     for copy in copies:
@@ -238,14 +237,13 @@
     factor, gram, coupling, packet, cov = refs[pieces:]
     rows, n = cov.shape
     start = pl.multiple_of(ids[0], rows)
-    size = rows // 2
     if pieces == 1:
         placed = [(lowers[0], 0)]
     else:
         first, second, other = lowers
         placed = [
             (first, start),
-            (second, pl.multiple_of(start + size, size)),
+            (second, pl.multiple_of(start + first.shape[0], TILE)),
             (other, pl.multiple_of(n - rows - start, rows)),
         ]
     couple(coupling, placed, factor)
@@ -327,15 +325,14 @@
             finish(factor, heard, coupling_1)
 
 
-def ready_kernel(pieces, first, ids, *refs):
+def ready_kernel(pieces, rows, first, ids, *refs):
     lowers, heard = refs[:pieces], refs[pieces]
     coupling_1, coupling_0 = refs[len(refs) - 2 :]
     n = heard.shape[0]
-    size = lowers[0].shape[0]
     placed = [(lowers[0], 0)]
     if pieces > 1:
-        bases = (ids[0], n - 2 * size - ids[0])
-        placed = [(p, pl.multiple_of(b + first, size)) for p, b in zip(lowers, bases)]
+        bases = (ids[0], n - rows - ids[0])
+        placed = [(p, pl.multiple_of(b + first, TILE)) for p, b in zip(lowers, bases)]
 
     @pl.when(ids[1] == 0)
     def _():
@@ -375,9 +372,9 @@
         var_3 = rider[...]
         off_1[...] = (-mm(full[...], coupling_1[...])).astype(BF16)
         cov_1[...] = (gram_1[...] - mm_t(coupling_1[...], off_1[...])).astype(BF16)
-        off_0[...] = (-mm(cov_1[...], coupling_0[...])).astype(BF16)
         for i in range(0, n, TILE):
             diag[:, i : i + TILE] = tile_diag(cov_1[i : i + TILE, i : i + TILE])
+        off_0[...] = (-mm(cov_1[...], coupling_0[...])).astype(BF16)
         product = coupling_0[...].astype(F32) * off_0[...].astype(F32)
         var_0 = diag_0[...] - jnp.sum(product, axis=0, keepdims=True)
         row = lax.broadcasted_iota(jnp.int32, variances.shape, 0)
@@ -386,52 +383,72 @@
         variances[...] = merged.astype(BF16)
 
 
-def last_kernel(ids, coupling_0, gram, off_0, off_1, cov_1, _, __, off_out, cov_out, cov, sems):
-    rows = cov.shape[0]
-    start = pl.multiple_of(ids[0], rows)
-    block = ids[1]
-    own = pl.ds(start, rows)
-
-    @pl.when(block == 1)
-    def _():
-        one = pltpu.make_async_copy(off_1.at[own], off_out, sems.at[0])
-        two = pltpu.make_async_copy(cov_1.at[own], cov_out, sems.at[1])
-        one.start()
-        two.start()
-        one.wait()
-        two.wait()
-
-    @pl.when(block == 0)
-    def _():
-        one = pltpu.make_async_copy(off_0.at[own], off_out, sems.at[0])
-        one.start()
-        copies = [one]
-        parts = 2 if rows % (2 * TILE) == 0 else 1
-        for k in range(parts):
-            product_rows(cov, gram, coupling_0, off_0, start, k, parts, -1)
-            here = pl.ds(k * rows // parts, rows // parts)
-            copies.append(
-                pltpu.make_async_copy(cov.at[here], cov_out.at[here], sems.at[k + 1])
-            )
-            copies[-1].start()
-        for copy in copies:
-            copy.wait()
-
-
-def deliver_kernel(ids, owner, mine, heard, out):
-    block = ids[1]
-    dev = ids[2]
-    values = jnp.where(block < 2, mine[...].astype(F32), heard[...].astype(F32))
-    lines = [jnp.zeros((1, out.shape[1]), F32) for _ in range(SLOTS)]
+def owned_lines(mask, variances):
+    values = variances[...].astype(F32)
+    lines = []
+    for slot in range(SLOTS):
+        line = jnp.zeros((1, values.shape[1]), F32)
+        for t in range(TB):
+            at = slot * TB + t
+            line += jnp.where(mask[at : at + 1, :] > 0, values[t : t + 1], 0.0)
+        lines.append(line)
+    return lines
+
+
+def choose_kernel(ids, owner, mask):
     for t in range(TB):
         rank = jnp.int32(0)
         for before in range(t):
             rank += (owner[before] == owner[t]).astype(jnp.int32)
         for slot in range(SLOTS):
-            here = jnp.logical_and(owner[t] == dev, rank == slot)
-            lines[slot] += jnp.where(here, values[t : t + 1], 0.0)
-    for slot in range(SLOTS):
-        out[slot : slot + 1, :] = lines[slot]
+            here = jnp.logical_and(owner[t] == ids[2], rank == slot)
+            at = slot * TB + t
+            mask[at : at + 1, :] = jnp.full((1, mask.shape[1]), jnp.where(here, 1.0, 0.0), F32)
+
+
+def last_kernel(ids, coupling_0, gram, off_0, off_1, cov_1, variances, mask, _, __,
+                off_out, cov_out, own_out, cov, lines, sems):
+    rows = cov.shape[0]
+    start = pl.multiple_of(ids[0], rows)
+    block = ids[1]
+    own = pl.ds(start, rows)
+
+    def begin(source, target, sem):
+        copy = pltpu.make_async_copy(source, target, sems.at[sem])
+        copy.start()
+        return copy
+
+    def owned():
+        for slot, line in enumerate(owned_lines(mask, variances)):
+            lines[slot : slot + 1, :] = line
+        return begin(lines, own_out, 0)
+
+    @pl.when(block == 1)
+    def _():
+        copies = [begin(off_1.at[own], off_out, 1), begin(cov_1.at[own], cov_out, 2), owned()]
+        for copy in copies:
+            copy.wait()
+
+    @pl.when(block == 0)
+    def _():
+        copies = [begin(off_0.at[own], off_out, 1), owned()]
+        parts = 2 if rows % (2 * TILE) == 0 else 1
+        for k in range(parts):
+            product_rows(cov, gram, coupling_0, off_0, start, k, parts, -1)
+            here = pl.ds(k * rows // parts, rows // parts)
+            copies.append(begin(cov.at[here], cov_out.at[here], k + 2))
+        for copy in copies:
+            copy.wait()
+
+
+def deliver_kernel(ids, mask, heard, _, own_out, lines, sems):
+    @pl.when(ids[1] >= 2)
+    def _():
+        for slot, line in enumerate(owned_lines(mask, heard)):
+            lines[slot : slot + 1, :] = line
+        copy = pltpu.make_async_copy(lines, own_out, sems.at[0])
+        copy.start()
+        copy.wait()
 
 
 def shards(linv, sub, owner):
@@ -504,21 +521,20 @@
     swap = [(1, 0), (0, 1)]
     if paired:
         other_factor, other_lower = peer(linv), peer(sub)
-        half_rows = (VMEM, (size, n), BF16)
+        cut = rows // 2
         own, lower_a, lower_b, square, cross = call(
             fold_kernel,
-            [part, half_rows, half_rows,
-             (VMEM, (rows * 3 // 4, rows), BF16), (VMEM, (rows, rows), BF16)],
+            [part, (VMEM, (cut, n), BF16), (VMEM, (rows - cut, n), BF16),
+             (VMEM, (TILE, sum(w for _, w, _ in strips(rows))), BF16),
+             (VMEM, (rows, rows), BF16)],
             [linv, sub],
             [HBM, HBM],
-            [sems(7)],
+            [sems(4 + len(strips(rows)))],
         )
         factors = [own, other_factor]
         lowers = [lower_a, lower_b, other_lower]
         raw_lower = [block_to_block(lower_a, swap), block_to_block(lower_b, swap)]
-        raw_factor = [
-            block_to_block(square, swap), block_to_block(cross, swap, range(1, 2))
-        ]
+        raw_factor = [block_to_block(square, swap), block_to_block(cross, swap, range(1, 2))]
     else:
         factors = pieces_of(linv)
         lowers = pieces_of(sub)
@@ -550,6 +566,8 @@
             {2: 1},
         )
         packets_2.append(block_to_block(packet_b, [(3, 2)]))
+
+    (mask,) = call(choose_kernel, [(VMEM, (SLOTS * TB, n), F32)], [owner], [SMEM], [])
 
     opened = []
     if chunks > 1:
@@ -589,11 +607,11 @@
         [whole, (VMEM, (n, n), F32), line, whole, whole, out_rows, out_rows],
         [*parts, factor, coupling, cov_3, off_2, cov_2],
         [VMEM] * (len(parts) + 5),
-        [pltpu.VMEM((rows, n), BF16), sems(8), sems(2)],
+        [pltpu.VMEM((rows, n), BF16), sems(2 * (rows // TILE) + 1), sems(2)],
     )
     for k, piece in enumerate(raw_lower):
         coupling_1, coupling_0 = call(
-            functools.partial(ready_kernel, pieces, k * size),
+            functools.partial(ready_kernel, pieces, rows, k * rows // 2),
             [whole, whole],
             [*swapped(piece, packet), heard_factor,
              coupling_1, coupling_0],
@@ -626,20 +644,23 @@
     )
     heard = block_to_block(variances, [(0, 2), (1, 3)])
 
-    off_rows, cov_rows = call(
+    own_rows = (HBM, (SLOTS, n), F32)
+    lines = pltpu.VMEM((SLOTS, n), F32)
+    off_rows, cov_rows, owned_var = call(
         last_kernel,
-        [out_rows, out_rows],
-        [coupling_0, gram, off_0, off_1, cov_1, off_rows, cov_rows],
-        [VMEM] * 5 + [HBM, HBM],
-        [pltpu.VMEM((rows, n), BF16), sems(3)],
-        {5: 0, 6: 1},
+        [out_rows, out_rows, own_rows],
+        [coupling_0, gram, off_0, off_1, cov_1, variances, mask, off_rows, cov_rows],
+        [VMEM] * 7 + [HBM, HBM],
+        [pltpu.VMEM((rows, n), BF16), lines, sems(4)],
+        {7: 0, 8: 1},
     )
     (owned_var,) = call(
         deliver_kernel,
-        [(VMEM, (SLOTS, n), F32)],
-        [owner, variances, heard],
-        [SMEM, VMEM, VMEM],
-        [],
+        [own_rows],
+        [mask, heard, owned_var],
+        [VMEM, VMEM, HBM],
+        [lines, sems(1)],
+        {2: 0},
     )
     return (cov_rows, off_rows, owned_var)
 

time: 76.1 us -> 74.4 us (0.978)
  the two profiles are of different devices: /device:TPU:23 before, /device:TPU:31 now
where the time goes in v6:
time: 74.4 us; the launch traced here: 74.1 us
  waiting for transfers between devices  48.1 us (65%)
  starting transfers between devices  15.4 us (21%)
  Pallas kernels  9.57 us (13%)
  between operations  1.05 us (1%)
    ppermute x11, waiting for transfers between devices, block_to_block(): return lax.ppermute(values, 'tm', pairs)  45.6 us
    pallas_call x17, Pallas kernels, call(): pl.pallas_call(located(kernel, rows, group), out_shape=shapes, in_specs=l...  9.57 us
    ppermute x11, starting transfers between devices, block_to_block(): return lax.ppermute(values, 'tm', pairs)  9.46 us
    ppermute x10, starting transfers between devices, peer(): return lax.ppermute(piece, 'tm', [(i, i ^ step) for i in range(TB * group)])  5.89 us
    ppermute x10, waiting for transfers between devices, peer(): return lax.ppermute(piece, 'tm', [(i, i ^ step) for i in range(TB * group)])  2.49 us
  transfers between devices with their start and end apart: 21, of which 9 were waited for; matrix products, arithmetic and copies ran while one was open for 0% of the time, Pallas kernels for 8%

profile of v6, /device:TPU:31, one launch (start us, length us, event | category | flops | bytes accessed | tf_op | source)
XLA Modules:
  0.0 74.1 jit_solution(515654538959818199)
XLA Ops:
  0.6 0.7 collective-permute-start.1
  1.4 0.1 collective-permute-start.2
  1.4 1.9 %shard_map.58 = (bf16[512,1024]{1,0:T(8,128)(2,1)S(1)}, bf16[256,1024]{1,0:T(8,128)(2,1)S(1)}, bf16[256,1024]{1,0:T(8,128)(2,1)S(1)}, bf16[128,1280]{1,0:T(8,128)(2,1)S(1)}, bf16[512,512]{1,0:T(8,128)(2,1)S(1)}) custom-call(bf16[512,1024]{1,0:T(8,128)(2,1)} %refs_0_.2, bf16[512,1024]{1,0:T(8,128)(2,1)} %refs_1_.1), custom_call_target="tpu_custom_call" | custom-call | tf_op jit(solution)/shard_map/pallas_call | solution.py:495
  3.3 0.5 collective-permute-done.1.refs_1_
  3.9 1.3 %shard_map.59 = (bf16[1024,1024]{1,0:T(8,128)(2,1)S(1)}, f32[512,1024]{1,0:T(8,128)S(1)}) custom-call(bf16[512,1024]{1,0:T(8,128)(2,1)S(1)} %get-tuple-element.50.refs_0_, bf16[512,1024]{1,0:T(8,128)(2,1)S(1)} %collective-permute-done.1.refs_1_), custom_call_target="tpu_custom_call" | custom-call | tf_op jit(solution)/shard_map/pallas_call | solution.py:495
  5.2 0.2 collective-permute-done.2.refs_2_
  5.4 2.7 %shard_map.60 = (bf16[1024,1024]{1,0:T(8,128)(2,1)S(1)}, bf16[272,512]{1,0:T(8,128)(2,1)S(1)}, bf16[512,1024]{1,0:T(8,128)(2,1)S(1)}) custom-call(bf16[256,1024]{1,0:T(8,128)(2,1)S(1)} %get-tuple-element.52.refs_0_, bf16[256,1024]{1,0:T(8,128)(2,1)S(1)} %get-tuple-element.49.refs_1_, bf16[512,1024]{1,0:T(8,128)(2,1)S(1)} %collective-permute-done.2.refs_2_, ...), custom_call_target="tpu_custom_call" | custom-call | tf_op jit(solution)/shard_map/pallas_call | solution.py:495
  8.1 1.3 %collective-permute-start.5 = (bf16[272,512]{1,0:T(8,128)(2,1)S(1)}, bf16[272,512]{1,0:T(8,128)(2,1)S(1)}, u32[]{:S(2)}, u32[]{:S(2)}) collective-permute-start(bf16[272,512]{1,0:T(8,128)(2,1)S(1)} %get-tuple-element.57), channel_id=1, source_target_pairs={{6,4},{7,5},{14,12},{15,13},{22,20},{23,21},{30,28},{31,29}} | collective-permute-start | bytes 835592 | tf_op jit(solution)/shard_map/ppermute | solution.py:463
  9.4 0.9 %shard_map.61 = (bf16[272,512]{1,0:T(8,128)(2,1)S(1)}, bf16[512,1024]{1,0:T(8,128)(2,1)S(1)}) custom-call(f32[512,1024]{1,0:T(8,128)S(1)} %get-tuple-element.51.refs_4_.refs_0_.refs_3_.refs_1_, bf16[1024,1024]{1,0:T(8,128)(2,1)S(1)} %get-tuple-element.54.refs_1_.refs_2_.refs_5_, ...), custom_call_target="tpu_custom_call", output_to_operand_aliasing={{1}: (2, {})} | custom-call | tf_op jit(solution)/shard_map/pallas_call | solution.py:495
  10.3 1.3 %collective-permute-start.3 = (bf16[272,512]{1,0:T(8,128)(2,1)S(1)}, bf16[272,512]{1,0:T(8,128)(2,1)S(1)}, u32[]{:S(2)}, u32[]{:S(2)}) collective-permute-start(bf16[272,512]{1,0:T(8,128)(2,1)S(1)} %get-tuple-element.56), channel_id=1, source_target_pairs={{6,4},{7,5},{14,12},{15,13},{22,20},{23,21},{30,28},{31,29}} | collective-permute-start | bytes 835592 | tf_op jit(solution)/shard_map/ppermute | solution.py:463
  11.6 3.4 %collective-permute-done.5.refs_0_ = bf16[272,512]{1,0:T(8,128)(2,1)S(1)} collective-permute-done((bf16[272,512]{1,0:T(8,128)(2,1)S(1)}, bf16[272,512]{1,0:T(8,128)(2,1)S(1)}, u32[]{:S(2)}, u32[]{:S(2)}) %collective-permute-start.5) | collective-permute-done | bytes 278560 | tf_op jit(solution)/shard_map/ppermute | solution.py:463
  15.0 2.1 %collective-permute-start.6 = (bf16[272,512]{1,0:T(8,128)(2,1)S(1)}, bf16[272,512]{1,0:T(8,128)(2,1)S(1)}, u32[]{:S(2)}, u32[]{:S(2)}) collective-permute-start(bf16[272,512]{1,0:T(8,128)(2,1)S(1)} %collective-permute-done.5.refs_0_), channel_id=1, source_target_pairs={{0,1},{1,0},{2,3},{3,2},{4,5},{5,4},{6,7},{7,6},{8,9},{9,8},{10,11... | collective-permute-start | bytes 835592 | tf_op jit(solution)/shard_map/ppermute | solution.py:466
  17.0 0.7 collective-permute-start
  17.7 0.7 collective-permute-start.8
  18.4 0.7 collective-permute-start.10
  19.1 1.8 %collective-permute-done.3.refs_0_ = bf16[272,512]{1,0:T(8,128)(2,1)S(1)} collective-permute-done((bf16[272,512]{1,0:T(8,128)(2,1)S(1)}, bf16[272,512]{1,0:T(8,128)(2,1)S(1)}, u32[]{:S(2)}, u32[]{:S(2)}) %collective-permute-start.3) | collective-permute-done | bytes 278560 | tf_op jit(solution)/shard_map/ppermute | solution.py:463
  20.9 1.2 %collective-permute-start.4 = (bf16[272,512]{1,0:T(8,128)(2,1)S(1)}, bf16[272,512]{1,0:T(8,128)(2,1)S(1)}, u32[]{:S(2)}, u32[]{:S(2)}) collective-permute-start(bf16[272,512]{1,0:T(8,128)(2,1)S(1)} %collective-permute-done.3.refs_0_), channel_id=1, source_target_pairs={{0,1},{1,0},{2,3},{3,2},{4,5},{5,4},{6,7},{7,6},{8,9},{9,8},{10,11... | collective-permute-start | bytes 835592 | tf_op jit(solution)/shard_map/ppermute | solution.py:466
  22.2 0.0 collective-permute-done.6.refs_1_
  22.2 0.7 collective-permute-start.12
  22.9 0.5 collective-permute-done.4.refs_1_
  23.4 0.7 collective-permute-start.14
  24.0 0.0 collective-permute-done.8.refs_0_
  24.0 0.7 collective-permute-start.17
  24.7 0.0 collective-permute-done.refs_0_
  24.7 0.7 collective-permute-start.18
  25.4 0.0 collective-permute-done.10.refs_2_
  25.4 0.4 collective-permute-start.9
  25.9 0.0 collective-permute-done.12.refs_0_
  25.9 0.7 collective-permute-start.15
  26.6 0.0 collective-permute-done.14.refs_0_
  26.6 0.2 collective-permute-start.11
  26.8 0.0 collective-permute-done.17.refs_0_
  26.8 0.4 collective-permute-start.13
  27.1 0.0 collective-permute-done.18.refs_1_
  27.2 0.1 collective-permute-start.7
  27.3 0.0 collective-permute-done.15.refs_1_
  27.3 0.4 collective-permute-start.19
  27.8 0.0 collective-permute-done.9.refs_1_
  27.8 0.2 collective-permute-start.16
  28.0 0.6 collective-permute-done.11.refs_3_
  28.5 1.5 %shard_map.65 = (bf16[1024,1024]{1,0:T(8,128)(2,1)S(1)}, f32[1024,1024]{1,0:T(8,128)S(1)}, f32[1,1024]{1,0:T(1,128)S(1)}, bf16[1024,1024]{1,0:T(8,128)(2,1)S(1)}...) custom-call(bf16[128,1280]{1,0:T(8,128)(2,1)S(1)} %collective-permute-done.8.refs_0_, ...), custom_call_target="tpu_custom_call" | custom-call | tf_op jit(solution)/shard_map/pallas_call | solution.py:495
  30.0 0.0 collective-permute-done.13.refs_1_
  30.1 0.0 collective-permute-done.7.refs_1_
  30.1 0.3 collective-permute-done.19.refs_1_
  30.4 0.4 collective-permute-done.16.refs_1_
  30.8 0.0 copy-start
  30.8 1.4 %collective-permute-start.20 = (bf16[16,1024]{1,0:T(8,128)(2,1)S(1)}, bf16[16,1024]{1,0:T(8,128)(2,1)S(1)}, u32[]{:S(2)}, u32[]{:S(2)}) collective-permute-start(bf16[16,1024]{1,0:T(8,128)(2,1)S(1)} %get-tuple-element.89.refs_5_), channel_id=1, source_target_pairs={{0,4},{1,5},{2,6},{3,7},{8,12},{9,13},{10,14},{11,15},{16,20},{17,... | collective-permute-start | bytes 98312 | tf_op jit(solution)/shard_map/ppermute | solution.py:463
  32.3 0.0 copy-done
  32.3 0.6 shard_map.72.refs_6_.refs_0_
  32.8 0.1 shard_map.73
  32.9 40.4 %collective-permute-done.20.refs_1_ = bf16[16,1024]{1,0:T(8,128)(2,1)S(1)} collective-permute-done((bf16[16,1024]{1,0:T(8,128)(2,1)S(1)}, bf16[16,1024]{1,0:T(8,128)(2,1)S(1)}, u32[]{:S(2)}, u32[]{:S(2)}) %collective-permute-start.20) | collective-permute-done | bytes 32800 | tf_op jit(solution)/shard_map/ppermute | solution.py:463
  73.3 0.6 shard_map.74
  (9 shorter events, 0.1 us)
Async XLA Ops:
  0.6 3.2 %collective-permute-start.1 = (bf16[512,1024]{1,0:T(8,128)(2,1)}, bf16[512,1024]{1,0:T(8,128)(2,1)S(1)}, u32[]{:S(2)}, u32[]{:S(2)}) collective-permute-start(bf16[512,1024]{1,0:T(8,128)(2,1)} %refs_0_.2), channel_id=1, source_target_pairs={{0,1},{1,0},{2,3},{3,2},{4,5},{5,4},{6,7},{7,6},{8,9},{9,8},{10,11... | collective-permute-start | bytes 3145736 | tf_op jit(solution)/shard_map/ppermute | solution.py:466
  1.4 4.0 %collective-permute-start.2 = (bf16[512,1024]{1,0:T(8,128)(2,1)}, bf16[512,1024]{1,0:T(8,128)(2,1)S(1)}, u32[]{:S(2)}, u32[]{:S(2)}) collective-permute-start(bf16[512,1024]{1,0:T(8,128)(2,1)} %refs_1_.1), channel_id=1, source_target_pairs={{0,1},{1,0},{2,3},{3,2},{4,5},{5,4},{6,7},{7,6},{8,9},{9,8},{10,11... | collective-permute-start | bytes 3145736 | tf_op jit(solution)/shard_map/ppermute | solution.py:466
  8.1 6.9 %collective-permute-start.5 = (bf16[272,512]{1,0:T(8,128)(2,1)S(1)}, bf16[272,512]{1,0:T(8,128)(2,1)S(1)}, u32[]{:S(2)}, u32[]{:S(2)}) collective-permute-start(bf16[272,512]{1,0:T(8,128)(2,1)S(1)} %get-tuple-element.57), channel_id=1, source_target_pairs={{6,4},{7,5},{14,12},{15,13},{22,20},{23,21},{30,28},{31,29}} | collective-permute-start | bytes 835592 | tf_op jit(solution)/shard_map/ppermute | solution.py:463
  10.3 10.7 %collective-permute-start.3 = (bf16[272,512]{1,0:T(8,128)(2,1)S(1)}, bf16[272,512]{1,0:T(8,128)(2,1)S(1)}, u32[]{:S(2)}, u32[]{:S(2)}) collective-permute-start(bf16[272,512]{1,0:T(8,128)(2,1)S(1)} %get-tuple-element.56), channel_id=1, source_target_pairs={{6,4},{7,5},{14,12},{15,13},{22,20},{23,21},{30,28},{31,29}} | collective-permute-start | bytes 835592 | tf_op jit(solution)/shard_map/ppermute | solution.py:463
  15.0 7.2 %collective-permute-start.6 = (bf16[272,512]{1,0:T(8,128)(2,1)S(1)}, bf16[272,512]{1,0:T(8,128)(2,1)S(1)}, u32[]{:S(2)}, u32[]{:S(2)}) collective-permute-start(bf16[272,512]{1,0:T(8,128)(2,1)S(1)} %collective-permute-done.5.refs_0_), channel_id=1, source_target_pairs={{0,1},{1,0},{2,3},{3,2},{4,5},{5,4},{6,7},{7,6},{8,9},{9,8},{10,11... | collective-permute-start | bytes 835592 | tf_op jit(solution)/shard_map/ppermute | solution.py:466
  17.0 7.7 %collective-permute-start = (bf16[256,1024]{1,0:T(8,128)(2,1)S(1)}, bf16[256,1024]{1,0:T(8,128)(2,1)S(1)}, u32[]{:S(2)}, u32[]{:S(2)}) collective-permute-start(bf16[256,1024]{1,0:T(8,128)(2,1)S(1)} %get-tuple-element.49.refs_1_), channel_id=1, source_target_pairs={{2,0},{3,1},{0,2},{1,3},{10,8},{11,9},{8,10},{9,11},{18,16},{19,17... | collective-permute-start | bytes 1572872 | tf_op jit(solution)/shard_map/ppermute | solution.py:463
  17.7 6.3 %collective-permute-start.8 = (bf16[128,1280]{1,0:T(8,128)(2,1)S(1)}, bf16[128,1280]{1,0:T(8,128)(2,1)S(1)}, u32[]{:S(2)}, u32[]{:S(2)}) collective-permute-start(bf16[128,1280]{1,0:T(8,128)(2,1)S(1)} %get-tuple-element.66), channel_id=1, source_target_pairs={{2,0},{3,1},{0,2},{1,3},{10,8},{11,9},{8,10},{9,11},{18,16},{19,17... | collective-permute-start | bytes 983048 | tf_op jit(solution)/shard_map/ppermute | solution.py:463
  18.4 7.0 %collective-permute-start.10 = (bf16[512,512]{1,0:T(8,128)(2,1)S(1)}, bf16[512,512]{1,0:T(8,128)(2,1)S(1)}, u32[]{:S(2)}, u32[]{:S(2)}) collective-permute-start(bf16[512,512]{1,0:T(8,128)(2,1)S(1)} %get-tuple-element.68), channel_id=1, source_target_pairs={{3,1},{1,3},{11,9},{9,11},{19,17},{17,19},{27,25},{25,27}} | collective-permute-start | bytes 1572872 | tf_op jit(solution)/shard_map/ppermute | solution.py:463
  20.9 2.4 %collective-permute-start.4 = (bf16[272,512]{1,0:T(8,128)(2,1)S(1)}, bf16[272,512]{1,0:T(8,128)(2,1)S(1)}, u32[]{:S(2)}, u32[]{:S(2)}) collective-permute-start(bf16[272,512]{1,0:T(8,128)(2,1)S(1)} %collective-permute-done.3.refs_0_), channel_id=1, source_target_pairs={{0,1},{1,0},{2,3},{3,2},{4,5},{5,4},{6,7},{7,6},{8,9},{9,8},{10,11... | collective-permute-start | bytes 835592 | tf_op jit(solution)/shard_map/ppermute | solution.py:466
  22.2 3.7 %collective-permute-start.12 = (bf16[256,1024]{1,0:T(8,128)(2,1)S(1)}, bf16[256,1024]{1,0:T(8,128)(2,1)S(1)}, u32[]{:S(2)}, u32[]{:S(2)}) collective-permute-start(bf16[256,1024]{1,0:T(8,128)(2,1)S(1)} %get-tuple-element.52.refs_0_), channel_id=1, source_target_pairs={{2,0},{3,1},{0,2},{1,3},{10,8},{11,9},{8,10},{9,11},{18,16},{19,17... | collective-permute-start | bytes 1572872 | tf_op jit(solution)/shard_map/ppermute | solution.py:463
  23.4 3.2 %collective-permute-start.14 = (bf16[272,512]{1,0:T(8,128)(2,1)S(1)}, bf16[272,512]{1,0:T(8,128)(2,1)S(1)}, u32[]{:S(2)}, u32[]{:S(2)}) collective-permute-start(bf16[272,512]{1,0:T(8,128)(2,1)S(1)} %get-tuple-element.64), channel_id=1, source_target_pairs={{4,0},{5,1},{12,8},{13,9},{20,16},{21,17},{28,24},{29,25}} | collective-permute-start | bytes 835592 | tf_op jit(solution)/shard_map/ppermute | solution.py:463
  24.0 2.7 %collective-permute-start.17 = (bf16[272,512]{1,0:T(8,128)(2,1)S(1)}, bf16[272,512]{1,0:T(8,128)(2,1)S(1)}, u32[]{:S(2)}, u32[]{:S(2)}) collective-permute-start(bf16[272,512]{1,0:T(8,128)(2,1)S(1)} %get-tuple-element.82), channel_id=1, source_target_pairs={{4,0},{5,1},{12,8},{13,9},{20,16},{21,17},{28,24},{29,25}} | collective-permute-start | bytes 835592 | tf_op jit(solution)/shard_map/ppermute | solution.py:463
  24.7 2.4 %collective-permute-start.18 = (bf16[272,512]{1,0:T(8,128)(2,1)S(1)}, bf16[272,512]{1,0:T(8,128)(2,1)S(1)}, u32[]{:S(2)}, u32[]{:S(2)}) collective-permute-start(bf16[272,512]{1,0:T(8,128)(2,1)S(1)} %get-tuple-element.82), channel_id=1, source_target_pairs={{4,2},{5,3},{12,10},{13,11},{20,18},{21,19},{28,26},{29,27}} | collective-permute-start | bytes 835592 | tf_op jit(solution)/shard_map/ppermute | solution.py:463
  25.4 2.3 %collective-permute-start.9 = (bf16[128,1280]{1,0:T(8,128)(2,1)S(1)}, bf16[128,1280]{1,0:T(8,128)(2,1)S(1)}, u32[]{:S(2)}, u32[]{:S(2)}) collective-permute-start(bf16[128,1280]{1,0:T(8,128)(2,1)S(1)} %collective-permute-done.8.refs_0_), channel_id=1, source_target_pairs={{0,1},{1,0},{2,3},{3,2},{4,5},{5,4},{6,7},{7,6},{8,9},{9,8},{10,11... | collective-permute-start | bytes 983048 | tf_op jit(solution)/shard_map/ppermute | solution.py:466
  25.9 1.4 %collective-permute-start.15 = (bf16[272,512]{1,0:T(8,128)(2,1)S(1)}, bf16[272,512]{1,0:T(8,128)(2,1)S(1)}, u32[]{:S(2)}, u32[]{:S(2)}) collective-permute-start(bf16[272,512]{1,0:T(8,128)(2,1)S(1)} %get-tuple-element.64), channel_id=1, source_target_pairs={{4,2},{5,3},{12,10},{13,11},{20,18},{21,19},{28,26},{29,27}} | collective-permute-start | bytes 835592 | tf_op jit(solution)/shard_map/ppermute | solution.py:463
  26.6 2.0 %collective-permute-start.11 = (bf16[512,512]{1,0:T(8,128)(2,1)S(1)}, bf16[512,512]{1,0:T(8,128)(2,1)S(1)}, u32[]{:S(2)}, u32[]{:S(2)}) collective-permute-start(bf16[512,512]{1,0:T(8,128)(2,1)S(1)} %collective-permute-done.10.refs_2_), channel_id=1, source_target_pairs={{0,1},{1,0},{2,3},{3,2},{4,5},{5,4},{6,7},{7,6},{8,9},{9,8},{10,11... | collective-permute-start | bytes 1572872 | tf_op jit(solution)/shard_map/ppermute | solution.py:466
  26.8 3.3 %collective-permute-start.13 = (bf16[256,1024]{1,0:T(8,128)(2,1)S(1)}, bf16[256,1024]{1,0:T(8,128)(2,1)S(1)}, u32[]{:S(2)}, u32[]{:S(2)}) collective-permute-start(bf16[256,1024]{1,0:T(8,128)(2,1)S(1)} %collective-permute-done.12.refs_0_), channel_id=1, source_target_pairs={{0,1},{1,0},{2,3},{3,2},{4,5},{5,4},{6,7},{7,6},{8,9},{9,8},{10,11... | collective-permute-start | bytes 1572872 | tf_op jit(solution)/shard_map/ppermute | solution.py:466
  27.2 2.9 %collective-permute-start.7 = (bf16[256,1024]{1,0:T(8,128)(2,1)S(1)}, bf16[256,1024]{1,0:T(8,128)(2,1)S(1)}, u32[]{:S(2)}, u32[]{:S(2)}) collective-permute-start(bf16[256,1024]{1,0:T(8,128)(2,1)S(1)} %collective-permute-done.refs_0_), channel_id=1, source_target_pairs={{0,1},{1,0},{2,3},{3,2},{4,5},{5,4},{6,7},{7,6},{8,9},{9,8},{10,11... | collective-permute-start | bytes 1572872 | tf_op jit(solution)/shard_map/ppermute | solution.py:466
  27.3 3.1 %collective-permute-start.19 = (bf16[272,512]{1,0:T(8,128)(2,1)S(1)}, bf16[272,512]{1,0:T(8,128)(2,1)S(1)}, u32[]{:S(2)}, u32[]{:S(2)}) collective-permute-start(bf16[272,512]{1,0:T(8,128)(2,1)S(1)} %shard_map.69.refs_0_), channel_id=1, source_target_pairs={{0,1},{1,0},{2,3},{3,2},{4,5},{5,4},{6,7},{7,6},{8,9},{9,8},{10,11... | collective-permute-start | bytes 835592 | tf_op jit(solution)/shard_map/ppermute | solution.py:466
  27.8 3.1 %collective-permute-start.16 = (bf16[272,512]{1,0:T(8,128)(2,1)S(1)}, bf16[272,512]{1,0:T(8,128)(2,1)S(1)}, u32[]{:S(2)}, u32[]{:S(2)}) collective-permute-start(bf16[272,512]{1,0:T(8,128)(2,1)S(1)} %shard_map.68.refs_0_), channel_id=1, source_target_pairs={{0,1},{1,0},{2,3},{3,2},{4,5},{5,4},{6,7},{7,6},{8,9},{9,8},{10,11... | collective-permute-start | bytes 835592 | tf_op jit(solution)/shard_map/ppermute | solution.py:466
  30.8 1.4 %copy-start = (s32[4]{0:T(128)S(1)}, s32[4]{0:T(128)}, u32[]{:S(2)}) copy-start(s32[4]{0:T(128)} %refs_0_.3) | copy-start | bytes 52
  30.8 42.4 %collective-permute-start.20 = (bf16[16,1024]{1,0:T(8,128)(2,1)S(1)}, bf16[16,1024]{1,0:T(8,128)(2,1)S(1)}, u32[]{:S(2)}, u32[]{:S(2)}) collective-permute-start(bf16[16,1024]{1,0:T(8,128)(2,1)S(1)} %get-tuple-element.89.refs_5_), channel_id=1, source_target_pairs={{0,4},{1,5},{2,6},{3,7},{8,12},{9,13},{10,14},{11,15},{16,20},{17,... | collective-permute-start | bytes 98312 | tf_op jit(solution)/shard_map/ppermute | solution.py:463

commit v7 on v6

--- a/solution.py
+++ b/solution.py
@@ -149,12 +149,12 @@
                     diag[:, pl.ds(pl.multiple_of(base[mine] + i, TILE), TILE)] = tile_diag(own)
 
 
-def product_rows(cov, gram, coupling, right, start, chunk, chunks, sign):
+def product_rows(cov, gram, left, at, right, chunk, chunks):
     size = cov.shape[0] // chunks
-    at = chunk * size
-    here = pl.ds(pl.multiple_of(start + at, size), size)
-    term = mm_t(coupling[:, here], right[...])
-    cov[at : at + size, :] = (gram[at : at + size, :] + sign * term).astype(BF16)
+    row = chunk * size
+    here = pl.ds(pl.multiple_of(at + row, size), size)
+    term = mm_t(left[:, here], right[...])
+    cov[row : row + size, :] = (gram[row : row + size, :] + term).astype(BF16)
 
 
 def strips(rows):
@@ -250,18 +250,20 @@
 
     @pl.when(ids[1] == TB - 1)
     def _():
-        product_rows(cov, gram, coupling, coupling, start, 0, chunks, 1)
+        product_rows(cov, gram, coupling, start, coupling, 0, chunks)
         pack(packet, cov, start, None if chunks > 1 else jnp.zeros((1, n), F32), 0)
 
 
-def rest_kernel(block, sign, ids, gram, coupling, *refs):
+def rest_kernel(block, ids, gram, coupling, *refs):
     packet, cov = refs[len(refs) - 2 :]
-    right, passenger = (coupling, None) if len(refs) == 3 else refs[:2]
     start = pl.multiple_of(ids[0], cov.shape[0])
+    left, at, passenger = coupling, start, None
+    if len(refs) > 3:
+        left, at, passenger = refs[0], 0, refs[1]
 
     @pl.when(ids[1] == block)
     def _():
-        product_rows(cov, gram, coupling, right, start, 1, 2, sign)
+        product_rows(cov, gram, left, at, coupling, 1, 2)
         pack(packet, cov, start, passenger, 1)
 
 
@@ -274,21 +276,21 @@
 def second_kernel(pieces, chunks, ids, *refs):
     packets = refs[:pieces]
     coupling, gram = refs[pieces : pieces + 2]
-    packet, off, cov, full, diag, rider = refs[len(refs) - 6 :]
+    packet, half, cov, full, diag, rider = refs[len(refs) - 6 :]
     rows = cov.shape[0]
     start = pl.multiple_of(ids[0], rows)
 
     @pl.when(ids[1] == TB - 2)
     def _():
         unpack(full, diag, rider, packets, start, chunks - 1)
-        off[...] = (-mm(full[...], coupling[...])).astype(BF16)
-        product_rows(cov, gram, coupling, off, start, 0, chunks, -1)
+        half[...] = mm(full[...], coupling[:, pl.ds(start, rows)]).astype(BF16)
+        product_rows(cov, gram, half, 0, coupling, 0, chunks)
         pack(packet, cov, start, diag, 0)
 
 
 def heard_kernel(parts, ids, *refs):
     parts, rest = refs[:parts], refs[parts:]
-    (factor, coupling, cov_3, off_2, cov_2, heard, gram_1, diag_0, coupling_1, coupling_0,
+    (factor, coupling, cov_3, full_2, cov_2, heard, gram_1, diag_0, coupling_1, coupling_0,
      off_out, cov_out, off, sems, out_sems) = rest
     rows, _ = cov_3.shape
     start = pl.multiple_of(ids[0], rows)
@@ -301,11 +303,12 @@
 
     @pl.when(block == TB - 2)
     def _():
-        write_out((off_2.at[pl.ds(start, rows)], cov_2), (off_out, cov_out), out_sems)
+        off[...] = (-mm(full_2[pl.ds(start, rows), :], coupling[...])).astype(BF16)
+        write_out((off, cov_2), (off_out, cov_out), out_sems)
 
     def finish(factor_1, factor_0, known):
         known[...] = coupling[...]
-        gram_1[...] = mm_t(factor_1[...], factor_1[...])
+        gram_1[...] = mm_t(factor_1[:, pl.ds(start, rows)], factor_1[...])
         diag_0[...] = jnp.sum(jnp.square(factor_0[...].astype(F32)), axis=0, keepdims=True)
 
     @pl.when(block < 2)
@@ -361,26 +364,40 @@
 
 def third_kernel(pieces, chunks, ids, *refs):
     packets = refs[:pieces]
-    coupling_1, gram_1, coupling_0, diag_0 = refs[pieces : pieces + 4]
-    off_0, off_1, cov_1, variances, full, diag, rider = refs[len(refs) - 7 :]
-    n = full.shape[0]
+    coupling_1, gram_1, coupling_0 = refs[pieces : pieces + 3]
+    off_0, cov_1, sums, full, diag, rider, half = refs[len(refs) - 7 :]
+    rows, _ = cov_1.shape
+    start = pl.multiple_of(ids[0], rows)
+    own = pl.ds(start, rows)
 
     @pl.when(ids[1] < 2)
     def _():
-        unpack(full, diag, rider, packets, ids[0], chunks - 1)
-        var_2 = diag[...]
-        var_3 = rider[...]
-        off_1[...] = (-mm(full[...], coupling_1[...])).astype(BF16)
-        cov_1[...] = (gram_1[...] - mm_t(coupling_1[...], off_1[...])).astype(BF16)
-        for i in range(0, n, TILE):
-            diag[:, i : i + TILE] = tile_diag(cov_1[i : i + TILE, i : i + TILE])
+        unpack(full, diag, rider, packets, start, chunks - 1)
+        half[...] = mm(full[...], coupling_1[:, own]).astype(BF16)
+        product_rows(cov_1, gram_1, half, 0, coupling_1, 0, 1)
         off_0[...] = (-mm(cov_1[...], coupling_0[...])).astype(BF16)
-        product = coupling_0[...].astype(F32) * off_0[...].astype(F32)
-        var_0 = diag_0[...] - jnp.sum(product, axis=0, keepdims=True)
+        product = coupling_0[own, :].astype(F32) * off_0[...].astype(F32)
+        sums[...] = jnp.zeros(sums.shape, F32)
+        sums[0:1, :] = jnp.sum(product, axis=0, keepdims=True)
+        for i in range(0, rows, TILE):
+            at = pl.ds(pl.multiple_of(start + i, TILE), TILE)
+            sums[1:2, at] = tile_diag(cov_1[i : i + TILE, at])
+
+
+def combine_kernel(ids, *refs):
+    diag_0, var_2, var_3, variances = refs[len(refs) - 4 :]
+    parts = refs[: len(refs) - 4]
+
+    @pl.when(ids[1] < 2)
+    def _():
+        if len(parts) > 1:
+            total = parts[0][...] + parts[1][...]
+        else:
+            total = jnp.sum(parts[0][...], axis=0)
         row = lax.broadcasted_iota(jnp.int32, variances.shape, 0)
-        merged = jnp.where(row == 0, var_0, jnp.where(row == 1, diag[...], 0.0))
-        merged = jnp.where(row == 2, var_2, jnp.where(row == 3, var_3, merged))
-        variances[...] = merged.astype(BF16)
+        values = jnp.where(row == 0, diag_0[...] - total[0:1], total[1:2])
+        values = jnp.where(row == 2, var_2[...], jnp.where(row == 3, var_3[...], values))
+        variances[...] = values.astype(BF16)
 
 
 def owned_lines(mask, variances):
@@ -406,9 +423,11 @@
             mask[at : at + 1, :] = jnp.full((1, mask.shape[1]), jnp.where(here, 1.0, 0.0), F32)
 
 
-def last_kernel(ids, coupling_0, gram, off_0, off_1, cov_1, variances, mask, _, __,
-                off_out, cov_out, own_out, cov, lines, sems):
-    rows = cov.shape[0]
+def last_kernel(pieces, ids, *refs):
+    offs, refs = refs[:pieces], refs[pieces:]
+    (coupling_0, gram, off_0, full, coupling_1, cov_1, variances, mask, _, _,
+     off_out, cov_out, own_out, cov, off_1, lines, sems) = refs
+    rows, n = cov.shape
     start = pl.multiple_of(ids[0], rows)
     block = ids[1]
     own = pl.ds(start, rows)
@@ -425,17 +444,26 @@
 
     @pl.when(block == 1)
     def _():
-        copies = [begin(off_1.at[own], off_out, 1), begin(cov_1.at[own], cov_out, 2), owned()]
+        copies = [begin(cov_1, cov_out, 1), owned()]
+        off_1[...] = (-mm(full[own, :], coupling_1[...])).astype(BF16)
+        copies.append(begin(off_1, off_out, 2))
         for copy in copies:
             copy.wait()
 
     @pl.when(block == 0)
     def _():
-        copies = [begin(off_0.at[own], off_out, 1), owned()]
+        copies = [begin(off_0, off_out, 1), owned()]
         parts = 2 if rows % (2 * TILE) == 0 else 1
+        size = rows // parts
+        bases = (start, n - rows - start) if pieces > 1 else (0,)
         for k in range(parts):
-            product_rows(cov, gram, coupling_0, off_0, start, k, parts, -1)
-            here = pl.ds(k * rows // parts, rows // parts)
+            cols = pl.ds(pl.multiple_of(start + k * size, size), size)
+            total = gram[k * size : (k + 1) * size, :]
+            for off, base in zip(offs, bases):
+                here = pl.ds(pl.multiple_of(base, rows), off.shape[0])
+                total -= mm_t(coupling_0[here, cols], off[...])
+            here = pl.ds(k * size, size)
+            cov[here, :] = total.astype(BF16)
             copies.append(begin(cov.at[here], cov_out.at[here], k + 2))
         for copy in copies:
             copy.wait()
@@ -511,6 +539,7 @@
     packet_shape = (size + SPARE, rows if paired else n)
     whole = (VMEM, (n, n), BF16)
     part = (VMEM, (rows, n), BF16)
+    tall = (VMEM, (n, rows), BF16)
     line = (VMEM, (1, n), F32)
     packed = (VMEM, packet_shape, BF16)
     out_rows = (HBM, (rows, n), BF16)
@@ -558,7 +587,7 @@
     packets_2 = [block_to_block(packet_a, [(3, 2)])]
     if chunks > 1:
         packet_b, cov_3 = call(
-            functools.partial(rest_kernel, TB - 1, 1),
+            functools.partial(rest_kernel, TB - 1),
             [packed, part],
             [gram, coupling, cov_3],
             [VMEM] * 3,
@@ -578,9 +607,9 @@
             [VMEM, VMEM],
             [],
         )
-    packet_a, off_2, cov_2, _, diag_2, _ = call(
+    packet_a, half_2, cov_2, full_2, diag_2, _ = call(
         functools.partial(second_kernel, pieces, chunks),
-        [packed, whole, part, whole, line, line],
+        [packed, tall, part, whole, line, line],
         [*packets_of(packets_2[-1]), coupling, gram, *opened],
         [VMEM] * (pieces + 2 + len(opened)),
         [],
@@ -591,9 +620,9 @@
     packets_1 = [block_to_block(packet_a, [(2, 1)])]
     if chunks > 1:
         packet, cov_2 = call(
-            functools.partial(rest_kernel, TB - 2, -1),
+            functools.partial(rest_kernel, TB - 2),
             [packed, part],
-            [gram, coupling, off_2, diag_2, cov_2],
+            [gram, coupling, half_2, diag_2, cov_2],
             [VMEM] * 5,
             [],
             {4: 1},
@@ -604,8 +633,8 @@
     parts = [x for piece in raw_factor for x in swapped(piece, packet)]
     heard_factor, gram_1, diag_0, coupling_1, coupling_0, off_rows, cov_rows = call(
         functools.partial(heard_kernel, len(parts)),
-        [whole, (VMEM, (n, n), F32), line, whole, whole, out_rows, out_rows],
-        [*parts, factor, coupling, cov_3, off_2, cov_2],
+        [whole, (VMEM, (rows, n), F32), line, whole, whole, out_rows, out_rows],
+        [*parts, factor, coupling, cov_3, full_2, cov_2],
         [VMEM] * (len(parts) + 5),
         [pltpu.VMEM((rows, n), BF16), sems(2 * (rows // TILE) + 1), sems(2)],
     )
@@ -633,26 +662,35 @@
             [VMEM, VMEM],
             [],
         )
-    off_0, off_1, cov_1, variances, *_ = call(
+    off_0, cov_1, sums, full_1, var_2, var_3, _ = call(
         functools.partial(third_kernel, pieces, chunks),
-        [whole, whole, whole, (VMEM, (SPARE, n), BF16), whole, line, line],
-        [*packets_of(carried[-1]), coupling_1, gram_1, coupling_0, diag_0,
-         *opened],
-        [VMEM] * (pieces + 4 + len(opened)),
+        [part, part, (VMEM, (8, n), F32), whole, line, line, tall],
+        [*packets_of(carried[-1]), coupling_1, gram_1, coupling_0, *opened],
+        [VMEM] * (pieces + 3 + len(opened)),
         [],
-        {pieces + 4 + i: 4 + i for i in range(len(opened))},
+        {pieces + 3 + i: 3 + i for i in range(len(opened))},
+    )
+    offs = swapped(off_0)
+    parts = packets_of(sums)
+    (variances,) = call(
+        combine_kernel,
+        [(VMEM, (SPARE, n), BF16)],
+        [*parts, diag_0, var_2, var_3],
+        [VMEM] * (len(parts) + 3),
+        [],
     )
     heard = block_to_block(variances, [(0, 2), (1, 3)])
 
     own_rows = (HBM, (SLOTS, n), F32)
     lines = pltpu.VMEM((SLOTS, n), F32)
     off_rows, cov_rows, owned_var = call(
-        last_kernel,
+        functools.partial(last_kernel, len(offs)),
         [out_rows, out_rows, own_rows],
-        [coupling_0, gram, off_0, off_1, cov_1, variances, mask, off_rows, cov_rows],
-        [VMEM] * 7 + [HBM, HBM],
-        [pltpu.VMEM((rows, n), BF16), lines, sems(4)],
-        {7: 0, 8: 1},
+        [*offs, coupling_0, gram, off_0, full_1, coupling_1, cov_1, variances, mask,
+         off_rows, cov_rows],
+        [VMEM] * (len(offs) + 8) + [HBM, HBM],
+        [pltpu.VMEM((rows, n), BF16), pltpu.VMEM((rows, n), BF16), lines, sems(4)],
+        {len(offs) + 8: 0, len(offs) + 9: 1},
     )
     (owned_var,) = call(
         deliver_kernel,

time: 74.4 us -> 74.1 us (level)
  the two profiles are of different devices: /device:TPU:31 before, /device:TPU:27 now
where the time goes in v7:
time: 74.1 us; the launch traced here: 73.8 us
  waiting for transfers between devices  35.1 us (47%)
  starting transfers between devices  20.2 us (27%)
  Pallas kernels  17.3 us (23%)
  between operations  1.15 us (2%)
    ppermute x11, waiting for transfers between devices, block_to_block(): return lax.ppermute(values, 'tm', pairs)  32.1 us
    pallas_call x18, Pallas kernels, call(): pl.pallas_call(located(kernel, rows, group), out_shape=shapes, in_specs=l...  17.3 us
    ppermute x11, starting transfers between devices, block_to_block(): return lax.ppermute(values, 'tm', pairs)  17.1 us
    ppermute x12, starting transfers between devices, peer(): return lax.ppermute(piece, 'tm', [(i, i ^ step) for i in range(TB * group)])  3.06 us
    ppermute x12, waiting for transfers between devices, peer(): return lax.ppermute(piece, 'tm', [(i, i ^ step) for i in range(TB * group)])  2.97 us
  transfers between devices with their start and end apart: 23, of which 7 were waited for; matrix products, arithmetic and copies ran while one was open for 0% of the time, Pallas kernels for 14%

profile of v7, /device:TPU:27, one launch (start us, length us, event | category | flops | bytes accessed | tf_op | source)
XLA Modules:
  0.0 73.8 jit_solution(5079751581722996021)
XLA Ops:
  0.6 0.7 %collective-permute-start = (bf16[512,1024]{1,0:T(8,128)(2,1)}, bf16[512,1024]{1,0:T(8,128)(2,1)S(1)}, u32[]{:S(2)}, u32[]{:S(2)}) collective-permute-start(bf16[512,1024]{1,0:T(8,128)(2,1)} %refs_0_.2), channel_id=1, source_target_pairs={{0,1},{1,0},{2,3},{3,2},{4,5},{5,4},{6,7},{7,6},{8,9},{9,8},{10,11... | collective-permute-start | bytes 3145736 | tf_op jit(solution)/shard_map/ppermute | solution.py:494
  1.4 0.1 collective-permute-start.1
  1.4 1.8 %shard_map.58 = (bf16[512,1024]{1,0:T(8,128)(2,1)S(1)}, bf16[256,1024]{1,0:T(8,128)(2,1)S(1)}, bf16[256,1024]{1,0:T(8,128)(2,1)S(1)}, bf16[128,1280]{1,0:T(8,128)(2,1)S(1)}, bf16[512,512]{1,0:T(8,128)(2,1)S(1)}) custom-call(bf16[512,1024]{1,0:T(8,128)(2,1)} %refs_0_.2, bf16[512,1024]{1,0:T(8,128)(2,1)} %refs_1_.1), custom_call_target="tpu_custom_call" | custom-call | tf_op jit(solution)/shard_map/pallas_call | solution.py:523
  3.3 0.6 collective-permute-done.refs_1_
  3.9 1.3 %shard_map.59 = (bf16[1024,1024]{1,0:T(8,128)(2,1)S(1)}, f32[512,1024]{1,0:T(8,128)S(1)}) custom-call(bf16[512,1024]{1,0:T(8,128)(2,1)S(1)} %get-tuple-element.52.refs_0_, bf16[512,1024]{1,0:T(8,128)(2,1)S(1)} %collective-permute-done.refs_1_), custom_call_target="tpu_custom_call" | custom-call | tf_op jit(solution)/shard_map/pallas_call | solution.py:523
  5.2 0.2 collective-permute-done.1.refs_2_
  5.4 1.8 %shard_map.60 = (bf16[1024,1024]{1,0:T(8,128)(2,1)S(1)}, bf16[272,512]{1,0:T(8,128)(2,1)S(1)}, bf16[512,1024]{1,0:T(8,128)(2,1)S(1)}) custom-call(bf16[256,1024]{1,0:T(8,128)(2,1)S(1)} %get-tuple-element.54.refs_0_, bf16[256,1024]{1,0:T(8,128)(2,1)S(1)} %get-tuple-element.55.refs_1_, bf16[512,1024]{1,0:T(8,128)(2,1)S(1)} %collective-permute-done.1.refs_2_, ...), custom_call_target="tpu_custom_call" | custom-call | tf_op jit(solution)/shard_map/pallas_call | solution.py:523
  7.2 0.7 collective-permute-start.4
  7.9 0.7 collective-permute-start.2
  8.6 0.0 collective-permute-done.4.refs_0_
  8.6 0.4 collective-permute-start.5
  9.0 2.2 %collective-permute-start.9 = (bf16[256,1024]{1,0:T(8,128)(2,1)S(1)}, bf16[256,1024]{1,0:T(8,128)(2,1)S(1)}, u32[]{:S(2)}, u32[]{:S(2)}) collective-permute-start(bf16[256,1024]{1,0:T(8,128)(2,1)S(1)} %get-tuple-element.55.refs_1_), channel_id=1, source_target_pairs={{2,0},{3,1},{0,2},{1,3},{10,8},{11,9},{8,10},{9,11},{18,16},{19,17... | collective-permute-start | bytes 1572872 | tf_op jit(solution)/shard_map/ppermute | solution.py:491
  11.2 3.1 %collective-permute-start.11 = (bf16[128,1280]{1,0:T(8,128)(2,1)S(1)}, bf16[128,1280]{1,0:T(8,128)(2,1)S(1)}, u32[]{:S(2)}, u32[]{:S(2)}) collective-permute-start(bf16[128,1280]{1,0:T(8,128)(2,1)S(1)} %get-tuple-element.69), channel_id=1, source_target_pairs={{2,0},{3,1},{0,2},{1,3},{10,8},{11,9},{8,10},{9,11},{18,16},{19,17... | collective-permute-start | bytes 983048 | tf_op jit(solution)/shard_map/ppermute | solution.py:491
  14.3 2.2 %collective-permute-start.13 = (bf16[512,512]{1,0:T(8,128)(2,1)S(1)}, bf16[512,512]{1,0:T(8,128)(2,1)S(1)}, u32[]{:S(2)}, u32[]{:S(2)}) collective-permute-start(bf16[512,512]{1,0:T(8,128)(2,1)S(1)} %get-tuple-element.71), channel_id=1, source_target_pairs={{3,1},{1,3},{11,9},{9,11},{19,17},{17,19},{27,25},{25,27}} | collective-permute-start | bytes 1572872 | tf_op jit(solution)/shard_map/ppermute | solution.py:491
  16.5 0.0 collective-permute-done.2.refs_0_
  16.5 0.1 collective-permute-start.3
  16.6 0.0 collective-permute-done.5.refs_1_
  16.6 3.1 %collective-permute-start.15 = (bf16[256,1024]{1,0:T(8,128)(2,1)S(1)}, bf16[256,1024]{1,0:T(8,128)(2,1)S(1)}, u32[]{:S(2)}, u32[]{:S(2)}) collective-permute-start(bf16[256,1024]{1,0:T(8,128)(2,1)S(1)} %get-tuple-element.54.refs_0_), channel_id=1, source_target_pairs={{2,0},{3,1},{0,2},{1,3},{10,8},{11,9},{8,10},{9,11},{18,16},{19,17... | collective-permute-start | bytes 1572872 | tf_op jit(solution)/shard_map/ppermute | solution.py:491
  19.8 0.0 collective-permute-done.3.refs_1_
  19.8 0.7 collective-permute-start.6
  20.5 10.8 %collective-permute-done.11.refs_0_ = bf16[128,1280]{1,0:T(8,128)(2,1)S(1)} collective-permute-done((bf16[128,1280]{1,0:T(8,128)(2,1)S(1)}, bf16[128,1280]{1,0:T(8,128)(2,1)S(1)}, u32[]{:S(2)}, u32[]{:S(2)}) %collective-permute-start.11) | collective-permute-done | bytes 327712 | tf_op jit(solution)/shard_map/ppermute | solution.py:491
  31.3 0.7 collective-permute-start.17
  32.0 0.0 collective-permute-done.9.refs_0_
  32.0 1.3 %collective-permute-start.18 = (bf16[272,512]{1,0:T(8,128)(2,1)S(1)}, bf16[272,512]{1,0:T(8,128)(2,1)S(1)}, u32[]{:S(2)}, u32[]{:S(2)}) collective-permute-start(bf16[272,512]{1,0:T(8,128)(2,1)S(1)} %get-tuple-element.85), channel_id=1, source_target_pairs={{4,2},{5,3},{12,10},{13,11},{20,18},{21,19},{28,26},{29,27}} | collective-permute-start | bytes 835592 | tf_op jit(solution)/shard_map/ppermute | solution.py:491
  33.3 9.2 %collective-permute-done.13.refs_2_ = bf16[512,512]{1,0:T(8,128)(2,1)S(1)} collective-permute-done((bf16[512,512]{1,0:T(8,128)(2,1)S(1)}, bf16[512,512]{1,0:T(8,128)(2,1)S(1)}, u32[]{:S(2)}, u32[]{:S(2)}) %collective-permute-start.13) | collective-permute-done | bytes 524320 | tf_op jit(solution)/shard_map/ppermute | solution.py:491
  42.5 0.0 collective-permute-start.12
  42.5 5.9 %collective-permute-done.15.refs_0_ = bf16[256,1024]{1,0:T(8,128)(2,1)S(1)} collective-permute-done((bf16[256,1024]{1,0:T(8,128)(2,1)S(1)}, bf16[256,1024]{1,0:T(8,128)(2,1)S(1)}, u32[]{:S(2)}, u32[]{:S(2)}) %collective-permute-start.15) | collective-permute-done | bytes 524320 | tf_op jit(solution)/shard_map/ppermute | solution.py:491
  48.5 1.3 %collective-permute-start.7 = (bf16[272,512]{1,0:T(8,128)(2,1)S(1)}, bf16[272,512]{1,0:T(8,128)(2,1)S(1)}, u32[]{:S(2)}, u32[]{:S(2)}) collective-permute-start(bf16[272,512]{1,0:T(8,128)(2,1)S(1)} %get-tuple-element.67), channel_id=1, source_target_pairs={{4,2},{5,3},{12,10},{13,11},{20,18},{21,19},{28,26},{29,27}} | collective-permute-start | bytes 835592 | tf_op jit(solution)/shard_map/ppermute | solution.py:491
  49.7 0.0 collective-permute-done.6.refs_0_
  49.8 0.1 collective-permute-start.14
  49.8 0.0 collective-permute-done.17.refs_0_
  49.8 0.5 collective-permute-start.16
  50.3 0.0 collective-permute-done.18.refs_1_
  50.3 0.1 collective-permute-start.10
  50.5 6.2 %collective-permute-done.7.refs_1_ = bf16[272,512]{1,0:T(8,128)(2,1)S(1)} collective-permute-done((bf16[272,512]{1,0:T(8,128)(2,1)S(1)}, bf16[272,512]{1,0:T(8,128)(2,1)S(1)}, u32[]{:S(2)}, u32[]{:S(2)}) %collective-permute-start.7) | collective-permute-done | bytes 278560 | tf_op jit(solution)/shard_map/ppermute | solution.py:491
  56.6 0.0 collective-permute-start.19
  56.7 0.0 collective-permute-done.12.refs_1_
  56.7 0.6 collective-permute-start.8
  57.3 0.0 collective-permute-done.14.refs_3_
  57.3 1.8 %shard_map.66 = (bf16[1024,1024]{1,0:T(8,128)(2,1)S(1)}, f32[512,1024]{1,0:T(8,128)S(1)}, f32[1,1024]{1,0:T(1,128)S(1)}, bf16[1024,1024]{1,0:T(8,128)(2,1)S(1)},...) custom-call(bf16[128,1280]{1,0:T(8,128)(2,1)S(1)} %collective-permute-done.11.refs_0_, ...), custom_call_target="tpu_custom_call" | custom-call | tf_op jit(solution)/shard_map/pallas_call | solution.py:523
  59.1 0.0 collective-permute-done.16.refs_1_
  59.1 1.2 %shard_map.67 = (bf16[1024,1024]{1,0:T(8,128)(2,1)S(1)}, bf16[1024,1024]{1,0:T(8,128)(2,1)S(1)}) custom-call(bf16[256,1024]{1,0:T(8,128)(2,1)S(1)} %collective-permute-done.15.refs_0_, bf16[256,1024]{1,0:T(8,128)(2,1)S(1)} %collective-permute-done.16.refs_1_, ...), custom_call_target="tpu_custom_call", output_to_operand_aliasing={{0}: (3, {}), {1}: (4, {})} | custom-call | tf_op jit(solution)/shard_map/pallas_call | solution.py:523
  60.3 0.0 collective-permute-done.10.refs_1_
  60.3 1.0 %shard_map.68 = (bf16[1024,1024]{1,0:T(8,128)(2,1)S(1)}, bf16[1024,1024]{1,0:T(8,128)(2,1)S(1)}) custom-call(bf16[256,1024]{1,0:T(8,128)(2,1)S(1)} %collective-permute-done.9.refs_0_, bf16[256,1024]{1,0:T(8,128)(2,1)S(1)} %collective-permute-done.10.refs_1_, ...), custom_call_target="tpu_custom_call", output_to_operand_aliasing={{0}: (3, {}), {1}: (4, {})} | custom-call | tf_op jit(solution)/shard_map/pallas_call | solution.py:523
  61.3 0.0 collective-permute-done.19.refs_1_
  61.3 0.4 shard_map.70
  61.7 0.0 collective-permute-done.8.refs_1_
  61.7 0.0 copy-start
  61.7 4.9 %shard_map.71 = (bf16[512,1024]{1,0:T(8,128)(2,1)S(1)}, bf16[512,1024]{1,0:T(8,128)(2,1)S(1)}, f32[8,1024]{1,0:T(8,128)S(1)}, bf16[1024,1024]{1,0:T(8,128)(2,1)S...) custom-call(bf16[272,512]{1,0:T(8,128)(2,1)S(1)} %shard_map.65.refs_, ...), custom_call_target="tpu_custom_call", output_to_operand_aliasing={{3}: (5, {}), {4}: (6, {}), {5}: (7, {})} | custom-call | tf_op jit(solution)/shard_map/pallas_call | solution.py:523
  66.7 0.0 collective-permute-start.20
  66.7 0.5 collective-permute-start.21
  67.2 2.2 %collective-permute-done.21.refs_1_ = f32[8,1024]{1,0:T(8,128)S(1)} collective-permute-done((f32[8,1024]{1,0:T(8,128)S(1)}, f32[8,1024]{1,0:T(8,128)S(1)}, u32[]{:S(2)}, u32[]{:S(2)}) %collective-permute-start.21) | collective-permute-done | bytes 32800 | tf_op jit(solution)/shard_map/ppermute | solution.py:494
  69.4 1.3 %collective-permute-start.22 = (bf16[16,1024]{1,0:T(8,128)(2,1)S(1)}, bf16[16,1024]{1,0:T(8,128)(2,1)S(1)}, u32[]{:S(2)}, u32[]{:S(2)}) collective-permute-start(bf16[16,1024]{1,0:T(8,128)(2,1)S(1)} %shard_map.72.refs_8_), channel_id=1, source_target_pairs={{0,4},{1,5},{2,6},{3,7},{8,12},{9,13},{10,14},{11,15},{16,20},{17,... | collective-permute-start | bytes 98312 | tf_op jit(solution)/shard_map/ppermute | solution.py:491
  70.7 0.0 copy-done
  70.7 0.6 shard_map.73.refs_9_.refs_0_
  71.3 0.0 collective-permute-done.20.refs_1_
  71.3 2.3 %shard_map.74 = (bf16[512,1024]{1,0:T(8,128)(2,1)}, bf16[512,1024]{1,0:T(8,128)(2,1)}, f32[2,1024]{1,0:T(2,128)}) custom-call(bf16[512,1024]{1,0:T(8,128)(2,1)S(1)} %get-tuple-element.89.refs_0_.refs_4_, bf16[512,1024]{1,0:T(8,128)(2,1)S(1)} %collective-permute-done.20.refs_1_, ...), custom_call_target="tpu_custom_call", output_to_operand_aliasing={{0}: (10, {}), {1}: (11, {})} | custom-call | tf_op jit(solution)/shard_map/pallas_call | solution.py:523
  73.6 0.0 collective-permute-done.22.refs_1_
  (8 shorter events, 0.2 us)
Async XLA Ops:
  0.6 3.2 %collective-permute-start = (bf16[512,1024]{1,0:T(8,128)(2,1)}, bf16[512,1024]{1,0:T(8,128)(2,1)S(1)}, u32[]{:S(2)}, u32[]{:S(2)}) collective-permute-start(bf16[512,1024]{1,0:T(8,128)(2,1)} %refs_0_.2), channel_id=1, source_target_pairs={{0,1},{1,0},{2,3},{3,2},{4,5},{5,4},{6,7},{7,6},{8,9},{9,8},{10,11... | collective-permute-start | bytes 3145736 | tf_op jit(solution)/shard_map/ppermute | solution.py:494
  1.4 4.0 %collective-permute-start.1 = (bf16[512,1024]{1,0:T(8,128)(2,1)}, bf16[512,1024]{1,0:T(8,128)(2,1)S(1)}, u32[]{:S(2)}, u32[]{:S(2)}) collective-permute-start(bf16[512,1024]{1,0:T(8,128)(2,1)} %refs_1_.1), channel_id=1, source_target_pairs={{0,1},{1,0},{2,3},{3,2},{4,5},{5,4},{6,7},{7,6},{8,9},{9,8},{10,11... | collective-permute-start | bytes 3145736 | tf_op jit(solution)/shard_map/ppermute | solution.py:494
  7.2 1.4 %collective-permute-start.4 = (bf16[272,512]{1,0:T(8,128)(2,1)S(1)}, bf16[272,512]{1,0:T(8,128)(2,1)S(1)}, u32[]{:S(2)}, u32[]{:S(2)}) collective-permute-start(bf16[272,512]{1,0:T(8,128)(2,1)S(1)} %get-tuple-element.60), channel_id=1, source_target_pairs={{6,4},{7,5},{14,12},{15,13},{22,20},{23,21},{30,28},{31,29}} | collective-permute-start | bytes 835592 | tf_op jit(solution)/shard_map/ppermute | solution.py:491
  7.9 8.6 %collective-permute-start.2 = (bf16[272,512]{1,0:T(8,128)(2,1)S(1)}, bf16[272,512]{1,0:T(8,128)(2,1)S(1)}, u32[]{:S(2)}, u32[]{:S(2)}) collective-permute-start(bf16[272,512]{1,0:T(8,128)(2,1)S(1)} %get-tuple-element.59), channel_id=1, source_target_pairs={{6,4},{7,5},{14,12},{15,13},{22,20},{23,21},{30,28},{31,29}} | collective-permute-start | bytes 835592 | tf_op jit(solution)/shard_map/ppermute | solution.py:491
  8.6 8.0 %collective-permute-start.5 = (bf16[272,512]{1,0:T(8,128)(2,1)S(1)}, bf16[272,512]{1,0:T(8,128)(2,1)S(1)}, u32[]{:S(2)}, u32[]{:S(2)}) collective-permute-start(bf16[272,512]{1,0:T(8,128)(2,1)S(1)} %collective-permute-done.4.refs_0_), channel_id=1, source_target_pairs={{0,1},{1,0},{2,3},{3,2},{4,5},{5,4},{6,7},{7,6},{8,9},{9,8},{10,11... | collective-permute-start | bytes 835592 | tf_op jit(solution)/shard_map/ppermute | solution.py:494
  9.0 22.9 %collective-permute-start.9 = (bf16[256,1024]{1,0:T(8,128)(2,1)S(1)}, bf16[256,1024]{1,0:T(8,128)(2,1)S(1)}, u32[]{:S(2)}, u32[]{:S(2)}) collective-permute-start(bf16[256,1024]{1,0:T(8,128)(2,1)S(1)} %get-tuple-element.55.refs_1_), channel_id=1, source_target_pairs={{2,0},{3,1},{0,2},{1,3},{10,8},{11,9},{8,10},{9,11},{18,16},{19,17... | collective-permute-start | bytes 1572872 | tf_op jit(solution)/shard_map/ppermute | solution.py:491
  11.2 20.1 %collective-permute-start.11 = (bf16[128,1280]{1,0:T(8,128)(2,1)S(1)}, bf16[128,1280]{1,0:T(8,128)(2,1)S(1)}, u32[]{:S(2)}, u32[]{:S(2)}) collective-permute-start(bf16[128,1280]{1,0:T(8,128)(2,1)S(1)} %get-tuple-element.69), channel_id=1, source_target_pairs={{2,0},{3,1},{0,2},{1,3},{10,8},{11,9},{8,10},{9,11},{18,16},{19,17... | collective-permute-start | bytes 983048 | tf_op jit(solution)/shard_map/ppermute | solution.py:491
  14.3 28.2 %collective-permute-start.13 = (bf16[512,512]{1,0:T(8,128)(2,1)S(1)}, bf16[512,512]{1,0:T(8,128)(2,1)S(1)}, u32[]{:S(2)}, u32[]{:S(2)}) collective-permute-start(bf16[512,512]{1,0:T(8,128)(2,1)S(1)} %get-tuple-element.71), channel_id=1, source_target_pairs={{3,1},{1,3},{11,9},{9,11},{19,17},{17,19},{27,25},{25,27}} | collective-permute-start | bytes 1572872 | tf_op jit(solution)/shard_map/ppermute | solution.py:491
  16.5 3.2 %collective-permute-start.3 = (bf16[272,512]{1,0:T(8,128)(2,1)S(1)}, bf16[272,512]{1,0:T(8,128)(2,1)S(1)}, u32[]{:S(2)}, u32[]{:S(2)}) collective-permute-start(bf16[272,512]{1,0:T(8,128)(2,1)S(1)} %collective-permute-done.2.refs_0_), channel_id=1, source_target_pairs={{0,1},{1,0},{2,3},{3,2},{4,5},{5,4},{6,7},{7,6},{8,9},{9,8},{10,11... | collective-permute-start | bytes 835592 | tf_op jit(solution)/shard_map/ppermute | solution.py:494
  16.6 31.8 %collective-permute-start.15 = (bf16[256,1024]{1,0:T(8,128)(2,1)S(1)}, bf16[256,1024]{1,0:T(8,128)(2,1)S(1)}, u32[]{:S(2)}, u32[]{:S(2)}) collective-permute-start(bf16[256,1024]{1,0:T(8,128)(2,1)S(1)} %get-tuple-element.54.refs_0_), channel_id=1, source_target_pairs={{2,0},{3,1},{0,2},{1,3},{10,8},{11,9},{8,10},{9,11},{18,16},{19,17... | collective-permute-start | bytes 1572872 | tf_op jit(solution)/shard_map/ppermute | solution.py:491
  19.8 29.9 %collective-permute-start.6 = (bf16[272,512]{1,0:T(8,128)(2,1)S(1)}, bf16[272,512]{1,0:T(8,128)(2,1)S(1)}, u32[]{:S(2)}, u32[]{:S(2)}) collective-permute-start(bf16[272,512]{1,0:T(8,128)(2,1)S(1)} %get-tuple-element.67), channel_id=1, source_target_pairs={{4,0},{5,1},{12,8},{13,9},{20,16},{21,17},{28,24},{29,25}} | collective-permute-start | bytes 835592 | tf_op jit(solution)/shard_map/ppermute | solution.py:491
  31.3 18.5 %collective-permute-start.17 = (bf16[272,512]{1,0:T(8,128)(2,1)S(1)}, bf16[272,512]{1,0:T(8,128)(2,1)S(1)}, u32[]{:S(2)}, u32[]{:S(2)}) collective-permute-start(bf16[272,512]{1,0:T(8,128)(2,1)S(1)} %get-tuple-element.85), channel_id=1, source_target_pairs={{4,0},{5,1},{12,8},{13,9},{20,16},{21,17},{28,24},{29,25}} | collective-permute-start | bytes 835592 | tf_op jit(solution)/shard_map/ppermute | solution.py:491
  32.0 18.4 %collective-permute-start.18 = (bf16[272,512]{1,0:T(8,128)(2,1)S(1)}, bf16[272,512]{1,0:T(8,128)(2,1)S(1)}, u32[]{:S(2)}, u32[]{:S(2)}) collective-permute-start(bf16[272,512]{1,0:T(8,128)(2,1)S(1)} %get-tuple-element.85), channel_id=1, source_target_pairs={{4,2},{5,3},{12,10},{13,11},{20,18},{21,19},{28,26},{29,27}} | collective-permute-start | bytes 835592 | tf_op jit(solution)/shard_map/ppermute | solution.py:491
  42.5 14.2 %collective-permute-start.12 = (bf16[128,1280]{1,0:T(8,128)(2,1)S(1)}, bf16[128,1280]{1,0:T(8,128)(2,1)S(1)}, u32[]{:S(2)}, u32[]{:S(2)}) collective-permute-start(bf16[128,1280]{1,0:T(8,128)(2,1)S(1)} %collective-permute-done.11.refs_0_), channel_id=1, source_target_pairs={{0,1},{1,0},{2,3},{3,2},{4,5},{5,4},{6,7},{7,6},{8,9},{9,8},{10,11... | collective-permute-start | bytes 983048 | tf_op jit(solution)/shard_map/ppermute | solution.py:494
  48.5 8.2 %collective-permute-start.7 = (bf16[272,512]{1,0:T(8,128)(2,1)S(1)}, bf16[272,512]{1,0:T(8,128)(2,1)S(1)}, u32[]{:S(2)}, u32[]{:S(2)}) collective-permute-start(bf16[272,512]{1,0:T(8,128)(2,1)S(1)} %get-tuple-element.67), channel_id=1, source_target_pairs={{4,2},{5,3},{12,10},{13,11},{20,18},{21,19},{28,26},{29,27}} | collective-permute-start | bytes 835592 | tf_op jit(solution)/shard_map/ppermute | solution.py:491
  49.8 7.5 %collective-permute-start.14 = (bf16[512,512]{1,0:T(8,128)(2,1)S(1)}, bf16[512,512]{1,0:T(8,128)(2,1)S(1)}, u32[]{:S(2)}, u32[]{:S(2)}) collective-permute-start(bf16[512,512]{1,0:T(8,128)(2,1)S(1)} %collective-permute-done.13.refs_2_), channel_id=1, source_target_pairs={{0,1},{1,0},{2,3},{3,2},{4,5},{5,4},{6,7},{7,6},{8,9},{9,8},{10,11... | collective-permute-start | bytes 1572872 | tf_op jit(solution)/shard_map/ppermute | solution.py:494
  49.8 9.2 %collective-permute-start.16 = (bf16[256,1024]{1,0:T(8,128)(2,1)S(1)}, bf16[256,1024]{1,0:T(8,128)(2,1)S(1)}, u32[]{:S(2)}, u32[]{:S(2)}) collective-permute-start(bf16[256,1024]{1,0:T(8,128)(2,1)S(1)} %collective-permute-done.15.refs_0_), channel_id=1, source_target_pairs={{0,1},{1,0},{2,3},{3,2},{4,5},{5,4},{6,7},{7,6},{8,9},{9,8},{10,11... | collective-permute-start | bytes 1572872 | tf_op jit(solution)/shard_map/ppermute | solution.py:494
  50.3 9.9 %collective-permute-start.10 = (bf16[256,1024]{1,0:T(8,128)(2,1)S(1)}, bf16[256,1024]{1,0:T(8,128)(2,1)S(1)}, u32[]{:S(2)}, u32[]{:S(2)}) collective-permute-start(bf16[256,1024]{1,0:T(8,128)(2,1)S(1)} %collective-permute-done.9.refs_0_), channel_id=1, source_target_pairs={{0,1},{1,0},{2,3},{3,2},{4,5},{5,4},{6,7},{7,6},{8,9},{9,8},{10,11... | collective-permute-start | bytes 1572872 | tf_op jit(solution)/shard_map/ppermute | solution.py:494
  56.6 4.6 %collective-permute-start.19 = (bf16[272,512]{1,0:T(8,128)(2,1)S(1)}, bf16[272,512]{1,0:T(8,128)(2,1)S(1)}, u32[]{:S(2)}, u32[]{:S(2)}) collective-permute-start(bf16[272,512]{1,0:T(8,128)(2,1)S(1)} %shard_map.69.refs_0_), channel_id=1, source_target_pairs={{0,1},{1,0},{2,3},{3,2},{4,5},{5,4},{6,7},{7,6},{8,9},{9,8},{10,11... | collective-permute-start | bytes 835592 | tf_op jit(solution)/shard_map/ppermute | solution.py:494
  56.7 5.0 %collective-permute-start.8 = (bf16[272,512]{1,0:T(8,128)(2,1)S(1)}, bf16[272,512]{1,0:T(8,128)(2,1)S(1)}, u32[]{:S(2)}, u32[]{:S(2)}) collective-permute-start(bf16[272,512]{1,0:T(8,128)(2,1)S(1)} %shard_map.65.refs_0_), channel_id=1, source_target_pairs={{0,1},{1,0},{2,3},{3,2},{4,5},{5,4},{6,7},{7,6},{8,9},{9,8},{10,11... | collective-permute-start | bytes 835592 | tf_op jit(solution)/shard_map/ppermute | solution.py:494
  61.7 9.0 %copy-start = (s32[4]{0:T(128)S(1)}, s32[4]{0:T(128)}, u32[]{:S(2)}) copy-start(s32[4]{0:T(128)} %refs_0_.3) | copy-start | bytes 52
  66.7 4.6 %collective-permute-start.20 = (bf16[512,1024]{1,0:T(8,128)(2,1)S(1)}, bf16[512,1024]{1,0:T(8,128)(2,1)S(1)}, u32[]{:S(2)}, u32[]{:S(2)}) collective-permute-start(bf16[512,1024]{1,0:T(8,128)(2,1)S(1)} %get-tuple-element.89.refs_0_.refs_4_), channel_id=1, source_target_pairs={{0,1},{1,0},{2,3},{3,2},{4,5},{5,4},{6,7},{7,6},{8,9},{9,8},{10,11... | collective-permute-start | bytes 3145736 | tf_op jit(solution)/shard_map/ppermute | solution.py:494
  66.7 2.7 %collective-permute-start.21 = (f32[8,1024]{1,0:T(8,128)S(1)}, f32[8,1024]{1,0:T(8,128)S(1)}, u32[]{:S(2)}, u32[]{:S(2)}) collective-permute-start(f32[8,1024]{1,0:T(8,128)S(1)} %get-tuple-element.92.refs_0_), channel_id=1, source_target_pairs={{0,1},{1,0},{2,3},{3,2},{4,5},{5,4},{6,7},{7,6},{8,9},{9,8},{10,11... | collective-permute-start | bytes 98312 | tf_op jit(solution)/shard_map/ppermute | solution.py:494
  69.4 4.2 %collective-permute-start.22 = (bf16[16,1024]{1,0:T(8,128)(2,1)S(1)}, bf16[16,1024]{1,0:T(8,128)(2,1)S(1)}, u32[]{:S(2)}, u32[]{:S(2)}) collective-permute-start(bf16[16,1024]{1,0:T(8,128)(2,1)S(1)} %shard_map.72.refs_8_), channel_id=1, source_target_pairs={{0,4},{1,5},{2,6},{3,7},{8,12},{9,13},{10,14},{11,15},{16,20},{17,... | collective-permute-start | bytes 98312 | tf_op jit(solution)/shard_map/ppermute | solution.py:491

commit v8 on v7

--- a/solution.py
+++ b/solution.py
@@ -243,7 +243,7 @@
         first, second, other = lowers
         placed = [
             (first, start),
-            (second, pl.multiple_of(start + first.shape[0], TILE)),
+            (second, pl.multiple_of(start + first.shape[0], TILE // 2)),
             (other, pl.multiple_of(n - rows - start, rows)),
         ]
     couple(coupling, placed, factor)
@@ -335,7 +335,7 @@
     placed = [(lowers[0], 0)]
     if pieces > 1:
         bases = (ids[0], n - rows - ids[0])
-        placed = [(p, pl.multiple_of(b + first, TILE)) for p, b in zip(lowers, bases)]
+        placed = [(p, pl.multiple_of(b + first, TILE // 2)) for p, b in zip(lowers, bases)]
 
     @pl.when(ids[1] == 0)
     def _():
@@ -662,12 +662,12 @@
             [VMEM, VMEM],
             [],
         )
-    off_0, cov_1, sums, full_1, var_2, var_3, _ = call(
+    off_0, cov_1, sums, full_1, var_2, var_3 = call(
         functools.partial(third_kernel, pieces, chunks),
-        [part, part, (VMEM, (8, n), F32), whole, line, line, tall],
+        [part, part, (VMEM, (8, n), F32), whole, line, line],
         [*packets_of(carried[-1]), coupling_1, gram_1, coupling_0, *opened],
         [VMEM] * (pieces + 3 + len(opened)),
-        [],
+        [pltpu.VMEM((n, rows), BF16)],
         {pieces + 3 + i: 3 + i for i in range(len(opened))},
     )
     offs = swapped(off_0)

time: 74.1 us -> 73.2 us (0.988)
  the two profiles are of different devices: /device:TPU:27 before, /device:TPU:3 now
where the time goes in v8:
time: 73.2 us; the launch traced here: 72.9 us
  waiting for transfers between devices  35.1 us (48%)
  starting transfers between devices  20.3 us (28%)
  Pallas kernels  16.4 us (22%)
  between operations  1.15 us (2%)
    ppermute x11, waiting for transfers between devices, block_to_block(): return lax.ppermute(values, 'tm', pairs)  32.1 us
    ppermute x11, starting transfers between devices, block_to_block(): return lax.ppermute(values, 'tm', pairs)  17.1 us
    pallas_call x18, Pallas kernels, call(): pl.pallas_call(located(kernel, rows, group), out_shape=shapes, in_specs=l...  16.4 us
    ppermute x12, starting transfers between devices, peer(): return lax.ppermute(piece, 'tm', [(i, i ^ step) for i in range(TB * group)])  3.13 us
    ppermute x12, waiting for transfers between devices, peer(): return lax.ppermute(piece, 'tm', [(i, i ^ step) for i in range(TB * group)])  2.95 us
  transfers between devices with their start and end apart: 23, of which 7 were waited for; matrix products, arithmetic and copies ran while one was open for 0% of the time, Pallas kernels for 14%

profile of v8, /device:TPU:3, one launch (start us, length us, event | category | flops | bytes accessed | tf_op | source)
XLA Modules:
  0.0 72.9 jit_solution(10996544252443924179)
XLA Ops:
  0.6 0.7 %collective-permute-start = (bf16[512,1024]{1,0:T(8,128)(2,1)}, bf16[512,1024]{1,0:T(8,128)(2,1)S(1)}, u32[]{:S(2)}, u32[]{:S(2)}) collective-permute-start(bf16[512,1024]{1,0:T(8,128)(2,1)} %refs_0_.2), channel_id=1, source_target_pairs={{0,1},{1,0},{2,3},{3,2},{4,5},{5,4},{6,7},{7,6},{8,9},{9,8},{10,11... | collective-permute-start | bytes 3145736 | tf_op jit(solution)/shard_map/ppermute | solution.py:494
  1.4 0.1 collective-permute-start.1
  1.4 1.9 %shard_map.58 = (bf16[512,1024]{1,0:T(8,128)(2,1)S(1)}, bf16[256,1024]{1,0:T(8,128)(2,1)S(1)}, bf16[256,1024]{1,0:T(8,128)(2,1)S(1)}, bf16[128,1280]{1,0:T(8,128)(2,1)S(1)}, bf16[512,512]{1,0:T(8,128)(2,1)S(1)}) custom-call(bf16[512,1024]{1,0:T(8,128)(2,1)} %refs_0_.2, bf16[512,1024]{1,0:T(8,128)(2,1)} %refs_1_.1), custom_call_target="tpu_custom_call" | custom-call | tf_op jit(solution)/shard_map/pallas_call | solution.py:523
  3.3 0.5 collective-permute-done.refs_1_
  3.9 1.3 %shard_map.59 = (bf16[1024,1024]{1,0:T(8,128)(2,1)S(1)}, f32[512,1024]{1,0:T(8,128)S(1)}) custom-call(bf16[512,1024]{1,0:T(8,128)(2,1)S(1)} %get-tuple-element.52.refs_0_, bf16[512,1024]{1,0:T(8,128)(2,1)S(1)} %collective-permute-done.refs_1_), custom_call_target="tpu_custom_call" | custom-call | tf_op jit(solution)/shard_map/pallas_call | solution.py:523
  5.2 0.2 collective-permute-done.1.refs_2_
  5.4 1.8 %shard_map.60 = (bf16[1024,1024]{1,0:T(8,128)(2,1)S(1)}, bf16[272,512]{1,0:T(8,128)(2,1)S(1)}, bf16[512,1024]{1,0:T(8,128)(2,1)S(1)}) custom-call(bf16[256,1024]{1,0:T(8,128)(2,1)S(1)} %get-tuple-element.54.refs_0_, bf16[256,1024]{1,0:T(8,128)(2,1)S(1)} %get-tuple-element.55.refs_1_, bf16[512,1024]{1,0:T(8,128)(2,1)S(1)} %collective-permute-done.1.refs_2_, ...), custom_call_target="tpu_custom_call" | custom-call | tf_op jit(solution)/shard_map/pallas_call | solution.py:523
  7.2 0.7 collective-permute-start.4
  7.9 0.7 collective-permute-start.2
  8.6 0.0 collective-permute-done.4.refs_0_
  8.6 0.4 collective-permute-start.5
  9.1 1.9 %collective-permute-start.9 = (bf16[256,1024]{1,0:T(8,128)(2,1)S(1)}, bf16[256,1024]{1,0:T(8,128)(2,1)S(1)}, u32[]{:S(2)}, u32[]{:S(2)}) collective-permute-start(bf16[256,1024]{1,0:T(8,128)(2,1)S(1)} %get-tuple-element.55.refs_1_), channel_id=1, source_target_pairs={{2,0},{3,1},{0,2},{1,3},{10,8},{11,9},{8,10},{9,11},{18,16},{19,17... | collective-permute-start | bytes 1572872 | tf_op jit(solution)/shard_map/ppermute | solution.py:491
  11.0 3.4 %collective-permute-start.11 = (bf16[128,1280]{1,0:T(8,128)(2,1)S(1)}, bf16[128,1280]{1,0:T(8,128)(2,1)S(1)}, u32[]{:S(2)}, u32[]{:S(2)}) collective-permute-start(bf16[128,1280]{1,0:T(8,128)(2,1)S(1)} %get-tuple-element.69), channel_id=1, source_target_pairs={{2,0},{3,1},{0,2},{1,3},{10,8},{11,9},{8,10},{9,11},{18,16},{19,17... | collective-permute-start | bytes 983048 | tf_op jit(solution)/shard_map/ppermute | solution.py:491
  14.3 1.9 %collective-permute-start.13 = (bf16[512,512]{1,0:T(8,128)(2,1)S(1)}, bf16[512,512]{1,0:T(8,128)(2,1)S(1)}, u32[]{:S(2)}, u32[]{:S(2)}) collective-permute-start(bf16[512,512]{1,0:T(8,128)(2,1)S(1)} %get-tuple-element.71), channel_id=1, source_target_pairs={{3,1},{1,3},{11,9},{9,11},{19,17},{17,19},{27,25},{25,27}} | collective-permute-start | bytes 1572872 | tf_op jit(solution)/shard_map/ppermute | solution.py:491
  16.3 0.0 collective-permute-done.2.refs_0_
  16.3 0.1 collective-permute-start.3
  16.4 0.0 collective-permute-done.5.refs_1_
  16.4 3.4 %collective-permute-start.15 = (bf16[256,1024]{1,0:T(8,128)(2,1)S(1)}, bf16[256,1024]{1,0:T(8,128)(2,1)S(1)}, u32[]{:S(2)}, u32[]{:S(2)}) collective-permute-start(bf16[256,1024]{1,0:T(8,128)(2,1)S(1)} %get-tuple-element.54.refs_0_), channel_id=1, source_target_pairs={{2,0},{3,1},{0,2},{1,3},{10,8},{11,9},{8,10},{9,11},{18,16},{19,17... | collective-permute-start | bytes 1572872 | tf_op jit(solution)/shard_map/ppermute | solution.py:491
  19.8 0.0 collective-permute-done.3.refs_1_
  19.8 0.7 collective-permute-start.6
  20.5 10.8 %collective-permute-done.11.refs_0_ = bf16[128,1280]{1,0:T(8,128)(2,1)S(1)} collective-permute-done((bf16[128,1280]{1,0:T(8,128)(2,1)S(1)}, bf16[128,1280]{1,0:T(8,128)(2,1)S(1)}, u32[]{:S(2)}, u32[]{:S(2)}) %collective-permute-start.11) | collective-permute-done | bytes 327712 | tf_op jit(solution)/shard_map/ppermute | solution.py:491
  31.3 0.7 collective-permute-start.17
  32.0 0.0 collective-permute-done.9.refs_0_
  32.0 1.3 %collective-permute-start.18 = (bf16[272,512]{1,0:T(8,128)(2,1)S(1)}, bf16[272,512]{1,0:T(8,128)(2,1)S(1)}, u32[]{:S(2)}, u32[]{:S(2)}) collective-permute-start(bf16[272,512]{1,0:T(8,128)(2,1)S(1)} %get-tuple-element.85), channel_id=1, source_target_pairs={{4,2},{5,3},{12,10},{13,11},{20,18},{21,19},{28,26},{29,27}} | collective-permute-start | bytes 835592 | tf_op jit(solution)/shard_map/ppermute | solution.py:491
  33.3 9.2 %collective-permute-done.13.refs_2_ = bf16[512,512]{1,0:T(8,128)(2,1)S(1)} collective-permute-done((bf16[512,512]{1,0:T(8,128)(2,1)S(1)}, bf16[512,512]{1,0:T(8,128)(2,1)S(1)}, u32[]{:S(2)}, u32[]{:S(2)}) %collective-permute-start.13) | collective-permute-done | bytes 524320 | tf_op jit(solution)/shard_map/ppermute | solution.py:491
  42.5 0.0 collective-permute-start.12
  42.5 5.9 %collective-permute-done.15.refs_0_ = bf16[256,1024]{1,0:T(8,128)(2,1)S(1)} collective-permute-done((bf16[256,1024]{1,0:T(8,128)(2,1)S(1)}, bf16[256,1024]{1,0:T(8,128)(2,1)S(1)}, u32[]{:S(2)}, u32[]{:S(2)}) %collective-permute-start.15) | collective-permute-done | bytes 524320 | tf_op jit(solution)/shard_map/ppermute | solution.py:491
  48.5 1.3 %collective-permute-start.7 = (bf16[272,512]{1,0:T(8,128)(2,1)S(1)}, bf16[272,512]{1,0:T(8,128)(2,1)S(1)}, u32[]{:S(2)}, u32[]{:S(2)}) collective-permute-start(bf16[272,512]{1,0:T(8,128)(2,1)S(1)} %get-tuple-element.67), channel_id=1, source_target_pairs={{4,2},{5,3},{12,10},{13,11},{20,18},{21,19},{28,26},{29,27}} | collective-permute-start | bytes 835592 | tf_op jit(solution)/shard_map/ppermute | solution.py:491
  49.7 0.0 collective-permute-done.6.refs_0_
  49.8 0.1 collective-permute-start.14
  49.8 0.0 collective-permute-done.17.refs_0_
  49.8 0.5 collective-permute-start.16
  50.3 0.0 collective-permute-done.18.refs_1_
  50.3 0.1 collective-permute-start.10
  50.5 6.2 %collective-permute-done.7.refs_1_ = bf16[272,512]{1,0:T(8,128)(2,1)S(1)} collective-permute-done((bf16[272,512]{1,0:T(8,128)(2,1)S(1)}, bf16[272,512]{1,0:T(8,128)(2,1)S(1)}, u32[]{:S(2)}, u32[]{:S(2)}) %collective-permute-start.7) | collective-permute-done | bytes 278560 | tf_op jit(solution)/shard_map/ppermute | solution.py:491
  56.6 0.0 collective-permute-start.19
  56.7 0.0 collective-permute-done.12.refs_1_
  56.7 0.6 collective-permute-start.8
  57.3 0.0 collective-permute-done.14.refs_3_
  57.3 1.8 %shard_map.66 = (bf16[1024,1024]{1,0:T(8,128)(2,1)S(1)}, f32[512,1024]{1,0:T(8,128)S(1)}, f32[1,1024]{1,0:T(1,128)S(1)}, bf16[1024,1024]{1,0:T(8,128)(2,1)S(1)},...) custom-call(bf16[128,1280]{1,0:T(8,128)(2,1)S(1)} %collective-permute-done.11.refs_0_, ...), custom_call_target="tpu_custom_call" | custom-call | tf_op jit(solution)/shard_map/pallas_call | solution.py:523
  59.1 0.0 collective-permute-done.16.refs_1_
  59.1 1.2 %shard_map.67 = (bf16[1024,1024]{1,0:T(8,128)(2,1)S(1)}, bf16[1024,1024]{1,0:T(8,128)(2,1)S(1)}) custom-call(bf16[256,1024]{1,0:T(8,128)(2,1)S(1)} %collective-permute-done.15.refs_0_, bf16[256,1024]{1,0:T(8,128)(2,1)S(1)} %collective-permute-done.16.refs_1_, ...), custom_call_target="tpu_custom_call", output_to_operand_aliasing={{0}: (3, {}), {1}: (4, {})} | custom-call | tf_op jit(solution)/shard_map/pallas_call | solution.py:523
  60.3 0.0 collective-permute-done.10.refs_1_
  60.3 1.0 %shard_map.68 = (bf16[1024,1024]{1,0:T(8,128)(2,1)S(1)}, bf16[1024,1024]{1,0:T(8,128)(2,1)S(1)}) custom-call(bf16[256,1024]{1,0:T(8,128)(2,1)S(1)} %collective-permute-done.9.refs_0_, bf16[256,1024]{1,0:T(8,128)(2,1)S(1)} %collective-permute-done.10.refs_1_, ...), custom_call_target="tpu_custom_call", output_to_operand_aliasing={{0}: (3, {}), {1}: (4, {})} | custom-call | tf_op jit(solution)/shard_map/pallas_call | solution.py:523
  61.3 0.0 collective-permute-done.19.refs_1_
  61.3 0.4 shard_map.70
  61.7 0.0 collective-permute-done.8.refs_1_
  61.7 0.0 copy-start
  61.7 4.0 %shard_map.71 = (bf16[512,1024]{1,0:T(8,128)(2,1)S(1)}, bf16[512,1024]{1,0:T(8,128)(2,1)S(1)}, f32[8,1024]{1,0:T(8,128)S(1)}, bf16[1024,1024]{1,0:T(8,128)(2,1)S...) custom-call(bf16[272,512]{1,0:T(8,128)(2,1)S(1)} %shard_map.65.refs_, ...), custom_call_target="tpu_custom_call", output_to_operand_aliasing={{3}: (5, {}), {4}: (6, {}), {5}: (7, {})} | custom-call | tf_op jit(solution)/shard_map/pallas_call | solution.py:523
  65.7 0.1 collective-permute-start.20
  65.8 0.5 collective-permute-start.21
  66.3 2.2 %collective-permute-done.21.refs_1_ = f32[8,1024]{1,0:T(8,128)S(1)} collective-permute-done((f32[8,1024]{1,0:T(8,128)S(1)}, f32[8,1024]{1,0:T(8,128)S(1)}, u32[]{:S(2)}, u32[]{:S(2)}) %collective-permute-start.21) | collective-permute-done | bytes 32800 | tf_op jit(solution)/shard_map/ppermute | solution.py:494
  68.5 1.3 %collective-permute-start.22 = (bf16[16,1024]{1,0:T(8,128)(2,1)S(1)}, bf16[16,1024]{1,0:T(8,128)(2,1)S(1)}, u32[]{:S(2)}, u32[]{:S(2)}) collective-permute-start(bf16[16,1024]{1,0:T(8,128)(2,1)S(1)} %shard_map.72.refs_8_), channel_id=1, source_target_pairs={{0,4},{1,5},{2,6},{3,7},{8,12},{9,13},{10,14},{11,15},{16,20},{17,... | collective-permute-start | bytes 98312 | tf_op jit(solution)/shard_map/ppermute | solution.py:491
  69.8 0.0 copy-done
  69.8 0.6 shard_map.73.refs_9_.refs_0_
  70.4 0.0 collective-permute-done.20.refs_1_
  70.4 2.3 %shard_map.74 = (bf16[512,1024]{1,0:T(8,128)(2,1)}, bf16[512,1024]{1,0:T(8,128)(2,1)}, f32[2,1024]{1,0:T(2,128)}) custom-call(bf16[512,1024]{1,0:T(8,128)(2,1)S(1)} %get-tuple-element.89.refs_0_.refs_4_, bf16[512,1024]{1,0:T(8,128)(2,1)S(1)} %collective-permute-done.20.refs_1_, ...), custom_call_target="tpu_custom_call", output_to_operand_aliasing={{0}: (10, {}), {1}: (11, {})} | custom-call | tf_op jit(solution)/shard_map/pallas_call | solution.py:523
  72.7 0.0 collective-permute-done.22.refs_1_
  (8 shorter events, 0.2 us)
Async XLA Ops:
  0.6 3.2 %collective-permute-start = (bf16[512,1024]{1,0:T(8,128)(2,1)}, bf16[512,1024]{1,0:T(8,128)(2,1)S(1)}, u32[]{:S(2)}, u32[]{:S(2)}) collective-permute-start(bf16[512,1024]{1,0:T(8,128)(2,1)} %refs_0_.2), channel_id=1, source_target_pairs={{0,1},{1,0},{2,3},{3,2},{4,5},{5,4},{6,7},{7,6},{8,9},{9,8},{10,11... | collective-permute-start | bytes 3145736 | tf_op jit(solution)/shard_map/ppermute | solution.py:494
  1.4 4.0 %collective-permute-start.1 = (bf16[512,1024]{1,0:T(8,128)(2,1)}, bf16[512,1024]{1,0:T(8,128)(2,1)S(1)}, u32[]{:S(2)}, u32[]{:S(2)}) collective-permute-start(bf16[512,1024]{1,0:T(8,128)(2,1)} %refs_1_.1), channel_id=1, source_target_pairs={{0,1},{1,0},{2,3},{3,2},{4,5},{5,4},{6,7},{7,6},{8,9},{9,8},{10,11... | collective-permute-start | bytes 3145736 | tf_op jit(solution)/shard_map/ppermute | solution.py:494
  7.2 1.4 %collective-permute-start.4 = (bf16[272,512]{1,0:T(8,128)(2,1)S(1)}, bf16[272,512]{1,0:T(8,128)(2,1)S(1)}, u32[]{:S(2)}, u32[]{:S(2)}) collective-permute-start(bf16[272,512]{1,0:T(8,128)(2,1)S(1)} %get-tuple-element.60), channel_id=1, source_target_pairs={{6,4},{7,5},{14,12},{15,13},{22,20},{23,21},{30,28},{31,29}} | collective-permute-start | bytes 835592 | tf_op jit(solution)/shard_map/ppermute | solution.py:491
  7.9 8.4 %collective-permute-start.2 = (bf16[272,512]{1,0:T(8,128)(2,1)S(1)}, bf16[272,512]{1,0:T(8,128)(2,1)S(1)}, u32[]{:S(2)}, u32[]{:S(2)}) collective-permute-start(bf16[272,512]{1,0:T(8,128)(2,1)S(1)} %get-tuple-element.59), channel_id=1, source_target_pairs={{6,4},{7,5},{14,12},{15,13},{22,20},{23,21},{30,28},{31,29}} | collective-permute-start | bytes 835592 | tf_op jit(solution)/shard_map/ppermute | solution.py:491
  8.6 7.8 %collective-permute-start.5 = (bf16[272,512]{1,0:T(8,128)(2,1)S(1)}, bf16[272,512]{1,0:T(8,128)(2,1)S(1)}, u32[]{:S(2)}, u32[]{:S(2)}) collective-permute-start(bf16[272,512]{1,0:T(8,128)(2,1)S(1)} %collective-permute-done.4.refs_0_), channel_id=1, source_target_pairs={{0,1},{1,0},{2,3},{3,2},{4,5},{5,4},{6,7},{7,6},{8,9},{9,8},{10,11... | collective-permute-start | bytes 835592 | tf_op jit(solution)/shard_map/ppermute | solution.py:494
  9.1 22.9 %collective-permute-start.9 = (bf16[256,1024]{1,0:T(8,128)(2,1)S(1)}, bf16[256,1024]{1,0:T(8,128)(2,1)S(1)}, u32[]{:S(2)}, u32[]{:S(2)}) collective-permute-start(bf16[256,1024]{1,0:T(8,128)(2,1)S(1)} %get-tuple-element.55.refs_1_), channel_id=1, source_target_pairs={{2,0},{3,1},{0,2},{1,3},{10,8},{11,9},{8,10},{9,11},{18,16},{19,17... | collective-permute-start | bytes 1572872 | tf_op jit(solution)/shard_map/ppermute | solution.py:491
  11.0 20.3 %collective-permute-start.11 = (bf16[128,1280]{1,0:T(8,128)(2,1)S(1)}, bf16[128,1280]{1,0:T(8,128)(2,1)S(1)}, u32[]{:S(2)}, u32[]{:S(2)}) collective-permute-start(bf16[128,1280]{1,0:T(8,128)(2,1)S(1)} %get-tuple-element.69), channel_id=1, source_target_pairs={{2,0},{3,1},{0,2},{1,3},{10,8},{11,9},{8,10},{9,11},{18,16},{19,17... | collective-permute-start | bytes 983048 | tf_op jit(solution)/shard_map/ppermute | solution.py:491
  14.3 28.2 %collective-permute-start.13 = (bf16[512,512]{1,0:T(8,128)(2,1)S(1)}, bf16[512,512]{1,0:T(8,128)(2,1)S(1)}, u32[]{:S(2)}, u32[]{:S(2)}) collective-permute-start(bf16[512,512]{1,0:T(8,128)(2,1)S(1)} %get-tuple-element.71), channel_id=1, source_target_pairs={{3,1},{1,3},{11,9},{9,11},{19,17},{17,19},{27,25},{25,27}} | collective-permute-start | bytes 1572872 | tf_op jit(solution)/shard_map/ppermute | solution.py:491
  16.3 3.5 %collective-permute-start.3 = (bf16[272,512]{1,0:T(8,128)(2,1)S(1)}, bf16[272,512]{1,0:T(8,128)(2,1)S(1)}, u32[]{:S(2)}, u32[]{:S(2)}) collective-permute-start(bf16[272,512]{1,0:T(8,128)(2,1)S(1)} %collective-permute-done.2.refs_0_), channel_id=1, source_target_pairs={{0,1},{1,0},{2,3},{3,2},{4,5},{5,4},{6,7},{7,6},{8,9},{9,8},{10,11... | collective-permute-start | bytes 835592 | tf_op jit(solution)/shard_map/ppermute | solution.py:494
  16.4 32.1 %collective-permute-start.15 = (bf16[256,1024]{1,0:T(8,128)(2,1)S(1)}, bf16[256,1024]{1,0:T(8,128)(2,1)S(1)}, u32[]{:S(2)}, u32[]{:S(2)}) collective-permute-start(bf16[256,1024]{1,0:T(8,128)(2,1)S(1)} %get-tuple-element.54.refs_0_), channel_id=1, source_target_pairs={{2,0},{3,1},{0,2},{1,3},{10,8},{11,9},{8,10},{9,11},{18,16},{19,17... | collective-permute-start | bytes 1572872 | tf_op jit(solution)/shard_map/ppermute | solution.py:491
  19.8 29.9 %collective-permute-start.6 = (bf16[272,512]{1,0:T(8,128)(2,1)S(1)}, bf16[272,512]{1,0:T(8,128)(2,1)S(1)}, u32[]{:S(2)}, u32[]{:S(2)}) collective-permute-start(bf16[272,512]{1,0:T(8,128)(2,1)S(1)} %get-tuple-element.67), channel_id=1, source_target_pairs={{4,0},{5,1},{12,8},{13,9},{20,16},{21,17},{28,24},{29,25}} | collective-permute-start | bytes 835592 | tf_op jit(solution)/shard_map/ppermute | solution.py:491
  31.3 18.5 %collective-permute-start.17 = (bf16[272,512]{1,0:T(8,128)(2,1)S(1)}, bf16[272,512]{1,0:T(8,128)(2,1)S(1)}, u32[]{:S(2)}, u32[]{:S(2)}) collective-permute-start(bf16[272,512]{1,0:T(8,128)(2,1)S(1)} %get-tuple-element.85), channel_id=1, source_target_pairs={{4,0},{5,1},{12,8},{13,9},{20,16},{21,17},{28,24},{29,25}} | collective-permute-start | bytes 835592 | tf_op jit(solution)/shard_map/ppermute | solution.py:491
  32.0 18.3 %collective-permute-start.18 = (bf16[272,512]{1,0:T(8,128)(2,1)S(1)}, bf16[272,512]{1,0:T(8,128)(2,1)S(1)}, u32[]{:S(2)}, u32[]{:S(2)}) collective-permute-start(bf16[272,512]{1,0:T(8,128)(2,1)S(1)} %get-tuple-element.85), channel_id=1, source_target_pairs={{4,2},{5,3},{12,10},{13,11},{20,18},{21,19},{28,26},{29,27}} | collective-permute-start | bytes 835592 | tf_op jit(solution)/shard_map/ppermute | solution.py:491
  42.5 14.2 %collective-permute-start.12 = (bf16[128,1280]{1,0:T(8,128)(2,1)S(1)}, bf16[128,1280]{1,0:T(8,128)(2,1)S(1)}, u32[]{:S(2)}, u32[]{:S(2)}) collective-permute-start(bf16[128,1280]{1,0:T(8,128)(2,1)S(1)} %collective-permute-done.11.refs_0_), channel_id=1, source_target_pairs={{0,1},{1,0},{2,3},{3,2},{4,5},{5,4},{6,7},{7,6},{8,9},{9,8},{10,11... | collective-permute-start | bytes 983048 | tf_op jit(solution)/shard_map/ppermute | solution.py:494
  48.5 8.2 %collective-permute-start.7 = (bf16[272,512]{1,0:T(8,128)(2,1)S(1)}, bf16[272,512]{1,0:T(8,128)(2,1)S(1)}, u32[]{:S(2)}, u32[]{:S(2)}) collective-permute-start(bf16[272,512]{1,0:T(8,128)(2,1)S(1)} %get-tuple-element.67), channel_id=1, source_target_pairs={{4,2},{5,3},{12,10},{13,11},{20,18},{21,19},{28,26},{29,27}} | collective-permute-start | bytes 835592 | tf_op jit(solution)/shard_map/ppermute | solution.py:491
  49.8 7.5 %collective-permute-start.14 = (bf16[512,512]{1,0:T(8,128)(2,1)S(1)}, bf16[512,512]{1,0:T(8,128)(2,1)S(1)}, u32[]{:S(2)}, u32[]{:S(2)}) collective-permute-start(bf16[512,512]{1,0:T(8,128)(2,1)S(1)} %collective-permute-done.13.refs_2_), channel_id=1, source_target_pairs={{0,1},{1,0},{2,3},{3,2},{4,5},{5,4},{6,7},{7,6},{8,9},{9,8},{10,11... | collective-permute-start | bytes 1572872 | tf_op jit(solution)/shard_map/ppermute | solution.py:494
  49.8 9.2 %collective-permute-start.16 = (bf16[256,1024]{1,0:T(8,128)(2,1)S(1)}, bf16[256,1024]{1,0:T(8,128)(2,1)S(1)}, u32[]{:S(2)}, u32[]{:S(2)}) collective-permute-start(bf16[256,1024]{1,0:T(8,128)(2,1)S(1)} %collective-permute-done.15.refs_0_), channel_id=1, source_target_pairs={{0,1},{1,0},{2,3},{3,2},{4,5},{5,4},{6,7},{7,6},{8,9},{9,8},{10,11... | collective-permute-start | bytes 1572872 | tf_op jit(solution)/shard_map/ppermute | solution.py:494
  50.3 9.9 %collective-permute-start.10 = (bf16[256,1024]{1,0:T(8,128)(2,1)S(1)}, bf16[256,1024]{1,0:T(8,128)(2,1)S(1)}, u32[]{:S(2)}, u32[]{:S(2)}) collective-permute-start(bf16[256,1024]{1,0:T(8,128)(2,1)S(1)} %collective-permute-done.9.refs_0_), channel_id=1, source_target_pairs={{0,1},{1,0},{2,3},{3,2},{4,5},{5,4},{6,7},{7,6},{8,9},{9,8},{10,11... | collective-permute-start | bytes 1572872 | tf_op jit(solution)/shard_map/ppermute | solution.py:494
  56.6 4.6 %collective-permute-start.19 = (bf16[272,512]{1,0:T(8,128)(2,1)S(1)}, bf16[272,512]{1,0:T(8,128)(2,1)S(1)}, u32[]{:S(2)}, u32[]{:S(2)}) collective-permute-start(bf16[272,512]{1,0:T(8,128)(2,1)S(1)} %shard_map.69.refs_0_), channel_id=1, source_target_pairs={{0,1},{1,0},{2,3},{3,2},{4,5},{5,4},{6,7},{7,6},{8,9},{9,8},{10,11... | collective-permute-start | bytes 835592 | tf_op jit(solution)/shard_map/ppermute | solution.py:494
  56.7 5.0 %collective-permute-start.8 = (bf16[272,512]{1,0:T(8,128)(2,1)S(1)}, bf16[272,512]{1,0:T(8,128)(2,1)S(1)}, u32[]{:S(2)}, u32[]{:S(2)}) collective-permute-start(bf16[272,512]{1,0:T(8,128)(2,1)S(1)} %shard_map.65.refs_0_), channel_id=1, source_target_pairs={{0,1},{1,0},{2,3},{3,2},{4,5},{5,4},{6,7},{7,6},{8,9},{9,8},{10,11... | collective-permute-start | bytes 835592 | tf_op jit(solution)/shard_map/ppermute | solution.py:494
  61.7 8.1 %copy-start = (s32[4]{0:T(128)S(1)}, s32[4]{0:T(128)}, u32[]{:S(2)}) copy-start(s32[4]{0:T(128)} %refs_0_.3) | copy-start | bytes 52
  65.7 4.7 %collective-permute-start.20 = (bf16[512,1024]{1,0:T(8,128)(2,1)S(1)}, bf16[512,1024]{1,0:T(8,128)(2,1)S(1)}, u32[]{:S(2)}, u32[]{:S(2)}) collective-permute-start(bf16[512,1024]{1,0:T(8,128)(2,1)S(1)} %get-tuple-element.89.refs_0_.refs_4_), channel_id=1, source_target_pairs={{0,1},{1,0},{2,3},{3,2},{4,5},{5,4},{6,7},{7,6},{8,9},{9,8},{10,11... | collective-permute-start | bytes 3145736 | tf_op jit(solution)/shard_map/ppermute | solution.py:494
  65.8 2.7 %collective-permute-start.21 = (f32[8,1024]{1,0:T(8,128)S(1)}, f32[8,1024]{1,0:T(8,128)S(1)}, u32[]{:S(2)}, u32[]{:S(2)}) collective-permute-start(f32[8,1024]{1,0:T(8,128)S(1)} %get-tuple-element.92.refs_0_), channel_id=1, source_target_pairs={{0,1},{1,0},{2,3},{3,2},{4,5},{5,4},{6,7},{7,6},{8,9},{9,8},{10,11... | collective-permute-start | bytes 98312 | tf_op jit(solution)/shard_map/ppermute | solution.py:494
  68.5 4.2 %collective-permute-start.22 = (bf16[16,1024]{1,0:T(8,128)(2,1)S(1)}, bf16[16,1024]{1,0:T(8,128)(2,1)S(1)}, u32[]{:S(2)}, u32[]{:S(2)}) collective-permute-start(bf16[16,1024]{1,0:T(8,128)(2,1)S(1)} %shard_map.72.refs_8_), channel_id=1, source_target_pairs={{0,4},{1,5},{2,6},{3,7},{8,12},{9,13},{10,14},{11,15},{16,20},{17,... | collective-permute-start | bytes 98312 | tf_op jit(solution)/shard_map/ppermute | solution.py:491
